TPU v7x, 256 devices: a whole 4x4x8 slice. The times are simulated.
256 devices in a mesh: batch: 8 (over x, core), seq: 32 (over y, z).
Axes of the slice: x: 4, y: 4, z: 8, core: 2. Of those that a mesh axis runs over, the one named last changes fastest.
Arguments:
- cotangent: bfloat16 [8, 4096, 4096], P('batch', 'seq'), may hold values from -23 to 23
- fixed_point: bfloat16 [8, 4096, 4096], P('batch', 'seq'), may hold values from -6 to 6
- input_map: bfloat16 [8, 4096, 128], P('batch', 'seq'), may hold values from -0.00390625 to 0.00390625
- output_map: bfloat16 [8, 4096, 128], P('batch', 'seq'), may hold values from -6 to 6
- step_size: float32 [8, 64, 4096], P('batch', None, 'seq'), may hold values from 0.3 to 3.4
- forget: float32 [8, 4096], P('batch', 'seq'), may hold values from 0 to 1, as said below
- decay_rate: float32 [64], replicated, may hold values from 4.8828125e-06 to 0.04
- skip_gain: float32 [64], replicated, may hold values from 0.3 to 0.65
Outputs:
- adjoint_sum: bfloat16 [8, 4096, 4096], P('batch', 'seq')
- rate_grad: float32 [64], replicated
- skip_grad: float32 [64], replicated
Inputs may be any that keep to these rules, and one draw needn't show every extreme that they name: `forget`: nonzero at few positions.
All inputs are finite; a program needn't handle non-finite values.
Results may differ from a plain program's by a relative error of at most 0.034.
Values may be sent and summed in bfloat16 or wider, within the bound.
No kernel may reach another device: no remote copies, remote signals or barrier semaphores. Data moves between devices by JAX's collectives and lax.ppermute only.
A program may use at most 128 MiB of HBM per device.

v0:
```python
import jax
import jax.numpy as jnp
from jax import lax
from jax.sharding import Mesh
from jax.sharding import PartitionSpec as P

H = 64
P_SIZE = 64
N = 128
TERMS = 4
SEQ = ("seq_0", "seq_1")
BATCH_SEQ = ("batch_0", "batch_1", "seq_0", "seq_1")
BATCH = ("batch_0", "batch_1")


def side_by_side(arrays, axis, split_dim, concat_dim, along):
    widths = [a.shape[along] for a in arrays]
    both = jnp.concatenate(arrays, axis=along)
    filled = lax.all_to_all(both, axis, split_axis=split_dim, concat_axis=concat_dim, tiled=True)
    return tuple(jnp.split(filled, [sum(widths[:k]) for k in range(1, len(widths))], axis=along))


def from_everyone(shard, axis):
    copies = jnp.broadcast_to(shard, (lax.axis_size(axis), *shard.shape))
    return lax.all_to_all(copies, axis, split_axis=0, concat_axis=0, tiled=True)


def in_order(tiles, dim):
    shape = list(tiles.shape[1:])
    shape[dim] *= tiles.shape[0]
    return jnp.moveaxis(tiles, 0, dim).reshape(shape)


def gathered_copies(shard, axis, dim):
    tiles = from_everyone(shard, axis)
    return in_order(tiles, dim)


def over_axes(shard, axes):
    for axis in axes:
        shard = lax.psum(shard, axis)
    return shard


def tables(input_rows, output_rows, step_rows, forget, decay_rate):
    log_step = -decay_rate[:, None, None] * step_rows - forget[None, :, :]
    log_decay = jnp.cumsum(log_step, axis=2)
    step_sum = jnp.cumsum(step_rows, axis=2)
    decay_end = log_decay[:, :, -1]
    block_len = log_decay.shape[2]
    causal = lax.broadcasted_iota(jnp.int32, (block_len, block_len), 0) >= lax.broadcasted_iota(
        jnp.int32, (block_len, block_len), 1
    )
    scores = jnp.einsum("ktn,ksn->kts", output_rows, input_rows, preferred_element_type=jnp.float32)
    log_gap = jnp.where(
        causal[None, None], log_decay[:, :, :, None] - log_decay[:, :, None, :], -jnp.inf
    )
    mixing = (scores[None] * jnp.exp(log_gap) * step_rows[:, :, None, :]).astype(jnp.bfloat16)
    input_weight = (
        (step_rows * jnp.exp(decay_end[:, :, None] - log_decay))[..., None]
        * input_rows[None].astype(jnp.float32)
    ).astype(jnp.bfloat16)
    output_weight = (jnp.exp(log_decay)[..., None] * output_rows[None].astype(jnp.float32)).astype(
        jnp.bfloat16
    )
    decay_run = jnp.cumsum(decay_end, axis=1)
    blocks = decay_end.shape[1]
    rows_at = lax.broadcasted_iota(jnp.int32, (blocks, blocks), 0)
    cols_at = lax.broadcasted_iota(jnp.int32, (blocks, blocks), 1)
    back_reach = jnp.exp(
        jnp.where(
            (cols_at > rows_at)[None],
            decay_run[:, None, :] - decay_end[:, None, :] - decay_run[:, :, None],
            -jnp.inf,
        )
    )
    fore_reach = jnp.exp(
        jnp.where(
            (cols_at < rows_at)[None],
            decay_run[:, :, None] - decay_end[:, :, None] - decay_run[:, None, :],
            -jnp.inf,
        )
    )
    return (
        mixing,
        input_weight,
        output_weight,
        decay_end,
        decay_run,
        step_sum,
        back_reach,
        fore_reach,
    )


def local_fore(group_table, fixed_groups):
    state_local = jnp.einsum(
        "hksn,kshp->hknp", group_table[1], fixed_groups, preferred_element_type=jnp.float32
    )
    state_own = jnp.einsum("hkj,hjnp->hknp", group_table[7], state_local)
    inner_part = jnp.einsum(
        "hkts,kshp->kthp", group_table[0], fixed_groups, preferred_element_type=jnp.float32
    )
    return (state_local, state_own, inner_part)


def local_back(group_table, vector):
    state_local = jnp.einsum(
        "hktn,kthp->hknp", group_table[2], vector, preferred_element_type=jnp.float32
    )
    state_own = jnp.einsum("hkj,hjnp->hknp", group_table[6], state_local)
    inner_part = jnp.einsum(
        "hkts,kthp->kshp", group_table[0], vector, preferred_element_type=jnp.float32
    )
    return (state_local, state_own, inner_part)


def finish(weight_rows, state_in, inner_part):
    return inner_part + jnp.einsum(
        "hksn,hknp->kshp",
        weight_rows,
        state_in.astype(jnp.bfloat16),
        preferred_element_type=jnp.float32,
    )


def pieces(step_sum, vector, fixed_groups, outputs, adjoint, state_out, state_in):
    vector_wide = vector.astype(jnp.float32)
    fixed_wide = fixed_groups.astype(jnp.float32)
    skip_part = jnp.sum(vector_wide * fixed_wide, axis=(0, 1, 3))
    step_rows = jnp.transpose(step_sum, (1, 2, 0))[..., None]
    inner_sum = jnp.sum(step_rows * (vector_wide * outputs - fixed_wide * adjoint), axis=(0, 1, 3))
    third_sum = jnp.sum(step_sum[:, :, -1][:, :, None, None] * state_out * state_in, axis=(1, 2, 3))
    return (-(inner_sum + third_sum), skip_part)


def body(cotangent, fixed_point, input_map, output_map, step_size, forget, decay_rate, skip_gain):
    sequences = cotangent.shape[0]
    length_dev = cotangent.shape[1]
    seq_count = lax.axis_size(SEQ)
    cot_rows, fixed_rows = side_by_side((cotangent, fixed_point), SEQ, 2, 1, 0)
    step_rows = lax.all_to_all(
        step_size.astype(jnp.bfloat16), SEQ, split_axis=1, concat_axis=2, tiled=True
    ).astype(step_size.dtype)
    input_rows, output_rows, forget_rows = (
        gathered_copies(input_map, SEQ, 1),
        gathered_copies(output_map, SEQ, 1),
        gathered_copies(forget.astype(jnp.bfloat16), SEQ, 1).astype(forget.dtype),
    )
    head_share = H // seq_count
    first_head = lax.axis_index(SEQ) * head_share
    own_rate = lax.dynamic_slice_in_dim(decay_rate, first_head, head_share)
    own_skip = lax.dynamic_slice_in_dim(skip_gain, first_head, head_share)
    group_shape = (sequences, seq_count, length_dev, head_share, P_SIZE)
    vector = cot_rows.reshape(group_shape)
    fixed_groups = fixed_rows.reshape(group_shape)
    group_table = jax.vmap(tables, in_axes=(0, 0, 0, 0, None))(
        input_rows.reshape(sequences, seq_count, length_dev, N),
        output_rows.reshape(sequences, seq_count, length_dev, N),
        step_rows.reshape(sequences, head_share, seq_count, length_dev),
        forget_rows.reshape(sequences, seq_count, length_dev),
        own_rate,
    )
    decay_end = group_table[3]
    state_local, state_own, inner_part = jax.vmap(local_fore)(group_table, fixed_groups)
    state_in = state_own
    outputs = jax.vmap(finish)(group_table[2], state_in, inner_part)
    state_out = state_local + jnp.exp(decay_end)[..., None, None] * state_in
    summed = jnp.zeros(group_shape, jnp.float32)
    rate_sum = jnp.zeros((H,), jnp.float32)
    skip_sum = jnp.zeros((H,), jnp.float32)
    for number in range(TERMS):
        state_local, state_own, inner_part = jax.vmap(local_back)(group_table, vector)
        state_in = state_own
        adjoint = jax.vmap(finish)(group_table[1], state_in, inner_part)
        rate_part, skip_part = jax.vmap(pieces)(
            group_table[5], vector, fixed_groups, outputs, adjoint, state_out, state_in
        )
        rate_part = lax.dynamic_update_slice_in_dim(
            jnp.zeros((H,), jnp.float32), jnp.sum(rate_part, axis=0), first_head, 0
        )
        skip_part = lax.dynamic_update_slice_in_dim(
            jnp.zeros((H,), jnp.float32), jnp.sum(skip_part, axis=0), first_head, 0
        )
        rate_part, skip_part = (over_axes(rate_part, BATCH_SEQ), over_axes(skip_part, BATCH_SEQ))
        rate_sum = rate_sum + rate_part
        skip_sum = skip_sum + skip_part
        vector_wide = vector.astype(jnp.float32)
        summed = summed + vector_wide
        if number + 1 < TERMS:
            vector = (adjoint + own_skip[None, None, None, :, None] * vector_wide).astype(
                jnp.bfloat16
            )
    result_rows = summed.astype(jnp.bfloat16).reshape(
        sequences, seq_count * length_dev, head_share * P_SIZE
    )
    result_rows = lax.all_to_all(result_rows, SEQ, split_axis=1, concat_axis=2, tiled=True)
    divisor = jnp.float32(sequences * lax.axis_size(BATCH) * length_dev * seq_count)
    return (result_rows, rate_sum / divisor, skip_sum / divisor)


def solution(mesh):
    torus = Mesh(mesh.devices.reshape(4, 2, 4, 8), ("batch_0", "batch_1", "seq_0", "seq_1"))
    return jax.shard_map(
        body,
        mesh=torus,
        in_specs=(
            P(BATCH, SEQ, None),
            P(BATCH, SEQ, None),
            P(BATCH, SEQ, None),
            P(BATCH, SEQ, None),
            P(BATCH, None, SEQ),
            P(BATCH, SEQ),
            P(),
            P(),
        ),
        out_specs=(P(BATCH, SEQ, None), P(), P()),
        check_vma=False,
    )
```

profile of v0, /device:TPU:32, one launch (start us, length us, event | category | flops | bytes accessed | tf_op | source)
XLA Modules:
  0.0 298.1 jit_solution(10278016321710463408)
XLA Ops:
  1.9 11.4 %all-to-all-start.4 = ((bf16[32,1,128]{2,1,0:T(2,128)(2,1)}), bf16[32,1,128]{2,1,0:T(2,128)(2,1)S(1)}, u32[]{:S(2)}, u32[]{:S(2)}) async-start(bf16[32,1,128]{2,1,0:T(2,128)(2,1)} %broadcast_in_dim.68), calls=%async_computation.4 | async-start | bytes 32768 | tf_op jit(solution)/shard_map/all_to_all | solution.py:25
  14.1 7.8 %all-to-all-done.4 = bf16[32,1,128]{2,1,0:T(2,128)(2,1)S(1)} async-done(((bf16[32,1,128]{2,1,0:T(2,128)(2,1)}), bf16[32,1,128]{2,1,0:T(2,128)(2,1)S(1)}, u32[]{:S(2)}, u32[]{:S(2)}) %all-to-all-start.4) | async-done | bytes 8224 | tf_op jit(solution)/shard_map/all_to_all | solution.py:25
  21.9 12.8 %all_to_all.57 = bf16[32,2,128]{2,1,0:T(2,128)(2,1)S(1)} all-to-all(bf16[32,2,128]{2,1,0:T(2,128)(2,1)S(1)} %bitcast.176), channel_id=1, replica_groups=mesh['batch_0'=4,'batch_1'=2,'seq_0'=4,'seq_1'=8] {'seq_0','seq_1'}, dimensions={0} | all-to-all | bytes 32768 | tf_op jit(solution)/shard_map/all_to_all | solution.py:142
  35.6 30.5 %all_to_all.58 = bf16[32,1,128,128]{3,2,1,0:T(8,128)(2,1)S(1)} all-to-all(bf16[32,1,128,128]{3,2,1,0:T(8,128)(2,1)S(1)} %broadcast_in_dim.40), channel_id=1, replica_groups=mesh['batch_0'=4,'batch_1'=2,'seq_0'=4,'seq_1'=8] {'seq_0','seq_1'}, dimensions={0} | all-to-all | bytes 2097152 | tf_op jit(solution)/shard_map/all_to_all | solution.py:25
  67.4 5.1 %all-to-all-start.2 = ((bf16[32,1,128,128]{3,2,1,0:T(8,128)(2,1)}), bf16[32,1,128,128]{3,2,1,0:T(8,128)(2,1)S(1)}, u32[]{:S(2)}, u32[]{:S(2)}) async-start(bf16[32,1,128,128]{3,2,1,0:T(8,128)(2,1)} %broadcast_in_dim.66), calls=%async_computation.2 | async-start | bytes 2097152 | tf_op jit(solution)/shard_map/all_to_all | solution.py:25
  72.5 2.8 pad_maximum_fusion
  75.2 6.2 %copy.112 = bf16[2,128,4096]{1,0,2:T(2,128)(2,1)} copy(bf16[2,128,4096]{2,1,0:T(8,128)(2,1)} %pad_maximum_fusion) | data formatting | bytes 4194304 | tf_op jit(solution)/shard_map/concatenate | solution.py:18
  81.4 16.6 %all-to-all-done.2 = bf16[32,1,128,128]{3,2,1,0:T(8,128)(2,1)S(1)} async-done(((bf16[32,1,128,128]{3,2,1,0:T(8,128)(2,1)}), bf16[32,1,128,128]{3,2,1,0:T(8,128)(2,1)S(1)}, u32[]{:S(2)}, u32[]{:S(2)}) %all-to-all-start.2) | async-done | bytes 1048608 | tf_op jit(solution)/shard_map/all_to_all | solution.py:25
  98.0 5.2 %all-to-all-start = ((bf16[2,128,4096]{1,0,2:T(2,128)(2,1)}), bf16[2,128,4096]{1,0,2:T(2,128)(2,1)}, u32[]{:S(2)}, u32[]{:S(2)}) async-start(bf16[2,128,4096]{1,0,2:T(2,128)(2,1)} %copy.112), calls=%async_computation | async-start | bytes 4194304 | tf_op jit(solution)/shard_map/all_to_all | solution.py:19
  111.2 38.6 %all-to-all-done = bf16[2,128,4096]{1,0,2:T(2,128)(2,1)} async-done(((bf16[2,128,4096]{1,0,2:T(2,128)(2,1)}), bf16[2,128,4096]{1,0,2:T(2,128)(2,1)}, u32[]{:S(2)}, u32[]{:S(2)}) %all-to-all-start) | async-done | bytes 2097184 | tf_op jit(solution)/shard_map/all_to_all | solution.py:19
  177.5 4.0 %add_multiply_fusion = (f32[2,32,128,64]{2,1,3,0:T(8,128)}, bf16[2,32,128,64]{2,1,3,0:T(8,128)(2,1)S(1)}) fusion(f32[2,32,128,64]{2,3,1,0:T(8,128)S(1)} %fusion.33, f32[2,32]{1,0:T(2,128)S(1)} %get-tuple-element.40, f32[2,32]{1,0:T(2,128)S(1)} %slice_reduce_fusion, f32[2,32]{1,0:T(2,128)S(1)} %bitcast.173, f32[2,32]{1,0:T(2,128)S(1)} %subtract_reduce_fusion, ...), kind=kOutput, calls=%fused_computation.68 | convolution fusion | flops 35655680 | bytes 5244928 | tf_op jit(solution)/shard_map/vmap(hkj,hjnp->hknp)/dot_general | solution.py:100
  181.4 3.0 %fusion.59 = f32[32,2,64,128]{3,2,1,0:T(8,128)S(1)} fusion(f32[32,2,64,128]{3,2,1,0:T(8,128)S(1)} %fusion.116, bf16[2,32,128,64]{2,1,3,0:T(8,128)(2,1)S(1)} %get-tuple-element.33, f32[32,128,128]{2,1,0:T(8,128)S(1)} %copy-done, f32[2,32,128]{2,1,0:T(8,128)S(1)} %bitcast_exponential_fusion), kind=kOutput, calls=%fused_computation.87 | convolution fusion | flops 136839168 | bytes 7372800 | tf_op jit(solution)/shard_map/vmap(hksn,hknp->kshp)/dot_general | solution.py:119
  184.5 4.1 %fusion.23 = (f32[2]{0:T(128)S(1)}, f32[2]{0:T(128)S(1)}, f32[2]{0:T(128)S(1)}, f32[2]{0:T(128)S(1)}, f32[2]{0:T(128)S(1)}, /*index=5*/f32[2]{0:T(128)S(1)}, bf16[1,32,128,2,64]{2,4,3,1,0:T(8,128)(2,1)S(1)}) fusion(bf16[1,32,128,2,64]{2,4,3,1,0:T(8,128)(2,1)S(1)} %get-tuple-element.48, f32[1,32,128,2,64]{2,4,3,1,0:T(8,128)S(1)} %bitcast.151, ...), kind=kOutput, calls=%fused_computation.37 | convolution fusion | flops 150994944 | bytes 18939960 | tf_op jit(solution)/shard_map/vmap(hksn,hknp->kshp)/dot_general | solution.py:119
  188.6 2.5 fusion.3
  193.0 5.5 %copy.147 = bf16[1,32,128,2,64]{4,3,2,1,0:T(2,128)(2,1)} copy(bf16[1,32,128,2,64]{2,4,3,1,0:T(8,128)(2,1)} %fusion.8) | data formatting | bytes 2097152 | tf_op jit(solution)/shard_map/reshape | solution.py:194
  198.5 8.7 %reshape.401 = bf16[1,4096,128]{2,0,1:T(2,128)(2,1)} reshape(bf16[1,32,128,2,64]{4,3,2,1,0:T(2,128)(2,1)} %copy.147) | data formatting | bytes 2097152 | tf_op jit(solution)/shard_map/reshape | solution.py:194
  207.8 24.4 %reduce.26 = bf16[4096,128]{1,0:T(8,128)(2,1)} reduce(bf16[4096,1,128]{2,1,0:T(2,128)(2,1)} %bitcast.154, bf16[]{:T(256)} %broadcast.176), dimensions={1}, to_apply=%bitcast.117.reduce_sub_computation | reduce | bytes 2097154
  234.3 6.1 %all-to-all-start.5 = ((bf16[32,2,8192]{2,1,0:T(2,128)(2,1)}), bf16[32,2,8192]{2,1,0:T(2,128)(2,1)}, u32[]{:S(2)}, u32[]{:S(2)}) async-start(bf16[32,2,8192]{2,1,0:T(2,128)(2,1)} %reshape.408), calls=%async_computation.5 | async-start | bytes 2097152 | tf_op jit(solution)/shard_map/all_to_all | solution.py:197
  241.0 5.4 %multiply_reduce_fusion.1 = (f32[2]{0:T(128)S(1)}, f32[2]{0:T(128)S(1)}, f32[2]{0:T(128)S(1)}, f32[2]{0:T(128)S(1)}, bf16[2,32,128,64]{2,1,3,0:T(8,128)(2,1)S(1)}) fusion(f32[2,32,128,64]{2,1,3,0:T(8,128)} %get-tuple-element.32, f32[2,32,128,64]{2,1,3,0:T(8,128)} %get-tuple-element.51, f32[2,32,128,64]{2,1,3,0:T(8,128)} %get-tuple-element.47, ...), kind=kOutput, calls=%fused_computation.64 | convolution fusion | flops 38277120 | bytes 10487328 | tf_op jit(solution)/shard_map/vmap(hkj,hjnp->hknp)/dot_general | solution.py:111
  251.7 10.5 %all-reduce.2 = (f32[64]{0:T(128)S(1)}, f32[64]{0:T(128)S(1)}) all-reduce(f32[64]{0:T(128)S(1)} %get-tuple-element.55, f32[64]{0:T(128)S(1)} %get-tuple-element.54), channel_id=1, replica_groups=mesh['batch_0'=4,'batch_1'=2,'seq_0'=4,'seq_1'=8] {'batch_0'}, use_global_device_ids=true, to_apply=%region_5.6 | all-reduce | flops 128 | bytes 1024 | tf_op jit(solution)/shard_map/psum | solution.py:41
  262.2 2.5 all-reduce.3
  264.6 10.4 %all-reduce.1 = (f32[64]{0:T(128)S(1)}, f32[64]{0:T(128)S(1)}) all-reduce(f32[64]{0:T(128)S(1)} %get-tuple-element.28, f32[64]{0:T(128)S(1)} %get-tuple-element.29), channel_id=1, replica_groups=mesh['batch_0'=4,'batch_1'=2,'seq_0'=4,'seq_1'=8] {'seq_0'}, use_global_device_ids=true, to_apply=%region_7.8 | all-reduce | flops 128 | bytes 1024 | tf_op jit(solution)/shard_map/psum | solution.py:41
  275.0 15.6 %all-reduce = (f32[64]{0:T(128)S(1)}, f32[64]{0:T(128)S(1)}) all-reduce(f32[64]{0:T(128)S(1)} %get-tuple-element.24, f32[64]{0:T(128)S(1)} %get-tuple-element.25), channel_id=1, replica_groups=mesh['batch_0'=4,'batch_1'=2,'seq_0'=4,'seq_1'=8] {'seq_1'}, use_global_device_ids=true, to_apply=%region_8.9 | all-reduce | flops 128 | bytes 1024 | tf_op jit(solution)/shard_map/psum | solution.py:41
  291.7 4.3 %reshape.409 = bf16[4096,1,128]{2,1,0:T(2,128)(2,1)S(1)} reshape(bf16[32,2,8192]{2,1,0:T(2,128)(2,1)} %all-to-all-done.5) | data formatting | bytes 2097152
  (99 shorter events, 53.2 us)
Async XLA Ops:
  0.6 65.5 %copy-start.10 = (bf16[1,128,128]{2,1,0:T(8,128)(2,1)S(1)}, bf16[1,128,128]{2,1,0:T(8,128)(2,1)}, u32[]{:S(2)}) copy-start(bf16[1,128,128]{2,1,0:T(8,128)(2,1)} %param.10) | copy-start | bytes 98308
  1.9 19.9 %all-to-all-start.4 = ((bf16[32,1,128]{2,1,0:T(2,128)(2,1)}), bf16[32,1,128]{2,1,0:T(2,128)(2,1)S(1)}, u32[]{:S(2)}, u32[]{:S(2)}) async-start(bf16[32,1,128]{2,1,0:T(2,128)(2,1)} %broadcast_in_dim.68), calls=%async_computation.4 | async-start | bytes 32768 | tf_op jit(solution)/shard_map/all_to_all | solution.py:25
  66.2 6.3 %copy-start.9 = (bf16[1,128,4096]{2,1,0:T(8,128)(2,1)S(1)}, bf16[1,128,4096]{2,1,0:T(8,128)(2,1)}, u32[]{:S(2)}) copy-start(bf16[1,128,4096]{2,1,0:T(8,128)(2,1)} %param.9) | copy-start | bytes 3145732
  67.4 30.7 %all-to-all-start.2 = ((bf16[32,1,128,128]{3,2,1,0:T(8,128)(2,1)}), bf16[32,1,128,128]{3,2,1,0:T(8,128)(2,1)S(1)}, u32[]{:S(2)}, u32[]{:S(2)}) async-start(bf16[32,1,128,128]{3,2,1,0:T(8,128)(2,1)} %broadcast_in_dim.66), calls=%async_computation.2 | async-start | bytes 2097152 | tf_op jit(solution)/shard_map/all_to_all | solution.py:25
  81.4 21.9 %copy-start.11 = (f32[64]{0:T(128)S(1)}, f32[64]{0:T(128)}, u32[]{:S(2)}) copy-start(f32[64]{0:T(128)} %param.15) | copy-start | bytes 772
  81.4 22.0 %copy-start.12 = (f32[64]{0:T(128)S(1)}, f32[64]{0:T(128)}, u32[]{:S(2)}) copy-start(f32[64]{0:T(128)} %param.14) | copy-start | bytes 772
  98.0 5.3 %copy-start.1 = (bf16[32,1,128,128]{3,2,1,0:T(8,128)(2,1)}, bf16[32,1,128,128]{3,2,1,0:T(8,128)(2,1)S(1)}, u32[]{:S(2)}) copy-start(bf16[32,1,128,128]{3,2,1,0:T(8,128)(2,1)S(1)} %all-to-all-done.2) | copy-start | bytes 3145732
  98.0 51.8 %all-to-all-start = ((bf16[2,128,4096]{1,0,2:T(2,128)(2,1)}), bf16[2,128,4096]{1,0,2:T(2,128)(2,1)}, u32[]{:S(2)}, u32[]{:S(2)}) async-start(bf16[2,128,4096]{1,0,2:T(2,128)(2,1)} %copy.112), calls=%async_computation | async-start | bytes 4194304 | tf_op jit(solution)/shard_map/all_to_all | solution.py:19
  107.5 1.6 copy-start.2
  152.0 1.6 copy-start
  152.9 31.6 %copy-start.5 = (f32[1,32,128,128]{2,3,1,0:T(8,128)}, f32[1,32,128,128]{2,3,1,0:T(8,128)S(1)}, u32[]{:S(2)}) copy-start(f32[1,32,128,128]{2,3,1,0:T(8,128)S(1)} %get-tuple-element.35) | copy-start | bytes 6291460
  155.2 2.2 copy-start.7
  184.5 4.1 %copy-start.3 = (f32[32,2,64,128]{3,2,1,0:T(8,128)}, f32[32,2,64,128]{3,2,1,0:T(8,128)S(1)}, u32[]{:S(2)}) copy-start(f32[32,2,64,128]{3,2,1,0:T(8,128)S(1)} %fusion.59) | copy-start | bytes 6291460
  234.3 57.3 %all-to-all-start.5 = ((bf16[32,2,8192]{2,1,0:T(2,128)(2,1)}), bf16[32,2,8192]{2,1,0:T(2,128)(2,1)}, u32[]{:S(2)}, u32[]{:S(2)}) async-start(bf16[32,2,8192]{2,1,0:T(2,128)(2,1)} %reshape.408), calls=%async_computation.5 | async-start | bytes 2097152 | tf_op jit(solution)/shard_map/all_to_all | solution.py:197
  241.0 8.2 %copy-start.8 = (f32[32,128,128]{2,1,0:T(8,128)S(1)}, f32[32,128,128]{2,1,0:T(8,128)}, u32[]{:S(2)}) copy-start(f32[32,128,128]{2,1,0:T(8,128)} %fusion.65) | copy-start | bytes 6291460
  246.9 2.3 copy-start.4
  246.9 2.3 copy-start.6
where the time goes:
time: 300 us; the launch traced here: 298 us
  blocking collectives  82.3 us (27%)
  waiting for transfers between devices  63 us (21%)
  matrix products  49.2 us (16%)
  other arithmetic  38.7 us (13%)
  local copies, waits for them, and re-layouts  36.1 us (12%)
  starting transfers between devices  27.8 us (9%)
    psum x4, blocking collectives, over_axes(): shard = lax.psum(shard, axis)  39 us
    all_to_all x1, waiting for transfers between devices, side_by_side(): lax.all_to_all(both, axis, split_axis=split_dim, concat_axis=concat_dim,...  38.6 us
    all_to_all x1, blocking collectives, from_everyone(): return lax.all_to_all(copies, axis, split_axis=0, concat_axis=0, tiled=True)  30.5 us
    unnamed x1, other arithmetic  24.4 us
    all_to_all x2, waiting for transfers between devices, from_everyone(): return lax.all_to_all(copies, axis, split_axis=0, concat_axis=0, tiled=True)  24.4 us
    all_to_all x2, starting transfers between devices, from_everyone(): return lax.all_to_all(copies, axis, split_axis=0, concat_axis=0, tiled=True)  16.4 us
    reshape x2, local copies, waits for them, and re-layouts, body(): summed.astype(jnp.bfloat16)  14.3 us
    dot_general x5, matrix products, finish(): jnp.einsum('hksn,hknp->kshp', weight_rows, state_in.astype(jnp.bfloat16),...  13.3 us
  transfers between devices with their start and end apart: 4, of which 3 were waited for; matrix products, arithmetic and copies ran while one was open for 10% of the time, Pallas kernels for 0%

commit v1 on v0

v1 whole, which is shorter than its diff:
```python
import jax
import jax.numpy as jnp
from jax import lax
from jax.experimental import pallas as pl
from jax.experimental.pallas import tpu as pltpu
from jax.sharding import Mesh
from jax.sharding import PartitionSpec as P

H = 64
HEAD = 64
N = 128
Q = 128
EXTRA = 8
GROUPS = 32
NY = 4
NZ = 8
UNROLL = 4
SEQ = ("seq_0", "seq_1")
BATCH = ("batch_0", "batch_1")
F32 = jnp.float32
BF16 = jnp.bfloat16


def shifted(x, axis, by):
    size = lax.axis_size(axis)
    return lax.ppermute(x, axis, [(i, (i + by) % size) for i in range(size)])


def swapped(x, axis, bit):
    size = lax.axis_size(axis)
    return lax.ppermute(x, axis, [(i, i ^ bit) for i in range(size)])


def halves(x):
    high = x.astype(BF16)
    return high, (x - high.astype(F32)).astype(BF16)


def pack_kernel(cot_ref, step_ref, forget_ref, out_ref):
    step_high, step_low = halves(step_ref[...])
    forget_high, forget_low = halves(forget_ref[...])
    for j in range(4):
        out_ref[j, :Q, :] = cot_ref[:, j * 128 : (j + 1) * 128]
        rows = jnp.concatenate(
            [
                step_high[2 * j : 2 * j + 2].astype(F32),
                step_low[2 * j : 2 * j + 2].astype(F32),
                forget_high.astype(F32),
                forget_low.astype(F32),
                jnp.zeros((2, Q), F32),
            ],
            axis=0,
        )
        out_ref[j, Q : Q + EXTRA, :] = rows.astype(BF16)


def pack(cot, step, forget):
    return pl.pallas_call(
        pack_kernel,
        grid=(8,),
        in_specs=[
            pl.BlockSpec((Q, 512), lambda i: (0, i)),
            pl.BlockSpec((8, Q), lambda i: (i, 0)),
            pl.BlockSpec((1, Q), lambda i: (0, 0)),
        ],
        out_specs=pl.BlockSpec((4, Q + EXTRA, 128), lambda i: (i, 0, 0)),
        out_shape=jax.ShapeDtypeStruct((GROUPS, Q + EXTRA, 128), BF16),
        name="pack",
    )(cot, step, forget)


def split_kernel(in_ref, out_ref):
    for j in range(4):
        out_ref[j] = in_ref[:, j * 128 : (j + 1) * 128]


def split(x):
    return pl.pallas_call(
        split_kernel,
        grid=(8,),
        in_specs=[pl.BlockSpec((Q, 512), lambda i: (0, i))],
        out_specs=pl.BlockSpec((4, Q, 128), lambda i: (i, 0, 0)),
        out_shape=jax.ShapeDtypeStruct((GROUPS, Q, 128), BF16),
        name="split",
    )(x)


def join_kernel(in_ref, out_ref):
    for j in range(4):
        out_ref[:, j * 128 : (j + 1) * 128] = in_ref[j]


def join(x):
    return pl.pallas_call(
        join_kernel,
        grid=(8,),
        in_specs=[pl.BlockSpec((4, Q, 128), lambda i: (i, 0, 0))],
        out_specs=pl.BlockSpec((Q, 512), lambda i: (0, i)),
        out_shape=jax.ShapeDtypeStruct((Q, GROUPS * 128), BF16),
        name="join",
    )(x)


def dot(a, b):
    return lax.dot_general(a, b, (((1,), (0,)), ((), ())), preferred_element_type=F32)


def dot_t(a, b):
    return lax.dot_general(a, b, (((1,), (1,)), ((), ())), preferred_element_type=F32)


def fetch_maps(pos_ref, pieces, maps_ref, sem):
    my_y, my_z = pos_ref[0], pos_ref[1]
    copies = []
    for dy in range(NY):
        for dz in range(NZ):
            if dy == 0:
                source = pieces[0].at[dz]
            elif dy == 1:
                source = pieces[1].at[dz]
            elif dy == 3:
                source = pieces[2].at[dz]
            else:
                source = pieces[3].at[dz] if dz < 4 else pieces[4].at[dz - 4]
            place = ((my_y + dy) % NY) * NZ + (my_z + dz) % NZ
            copies.append(pltpu.make_async_copy(source, maps_ref.at[place], sem))
    for c in copies:
        c.start()
    for c in copies:
        c.wait()


def constants():
    rows = lax.broadcasted_iota(jnp.int32, (Q, Q), 0)
    cols = lax.broadcasted_iota(jnp.int32, (Q, Q), 1)
    lower = (rows >= cols).astype(F32).astype(BF16)
    same = (rows == cols).astype(F32).astype(BF16)
    return rows <= cols, lower, same


def prepare(c, in_ref, maps_ref, rate_ref, consts, mat_ref, turn_ref, e_ref, g_ref, s_ref, m_ref):
    upper, lower, same = consts
    both = maps_ref[c]
    b_rows, c_rows = both[:N], both[N:]
    prod = dot_t(jnp.concatenate([b_rows, same], axis=0), c_rows)
    mat_ref[c, :, :N] = jnp.where(upper, prod[:Q], 0.0).astype(BF16)
    mat_ref[c, :, N:] = b_rows
    turn_ref[c] = prod[Q:].astype(BF16)
    rows = in_ref[c, Q : Q + EXTRA, :].astype(F32)

    def wide(first, second):
        return jnp.concatenate(
            [jnp.broadcast_to(rows[first : first + 1], (HEAD, Q)), jnp.broadcast_to(rows[second : second + 1], (HEAD, Q))],
            axis=0,
        ).astype(BF16)

    steps = jnp.concatenate([wide(0, 1), wide(2, 3)], axis=1)
    forgets = jnp.concatenate([wide(4, 4), wide(5, 5)], axis=1)
    lower_twice = jnp.concatenate([lower, lower], axis=1)
    same_twice = jnp.concatenate([same, same], axis=1)
    sums = dot_t(jnp.concatenate([lower_twice, same_twice], axis=0), steps)
    step_sum, step_col = sums[:Q], sums[Q:]
    forget_sum = dot_t(lower_twice, forgets)
    log_decay = -(rate_ref[0:1, :] * step_sum + forget_sum)
    middle = 0.5 * log_decay[Q - 1 : Q, :]
    gap = log_decay - middle
    e_ref[c] = jnp.exp(gap)
    g_ref[c] = step_col * jnp.exp(-gap)
    if s_ref is not None:
        s_ref[c] = step_sum
    m_ref[c] = jnp.broadcast_to(jnp.exp(middle), (8, 128))


def series_kernel(pos_ref, in_ref, p0, p1, p2, p3, p4, rate_ref, out_ref, maps_ref, mat_ref, turn_ref, e_ref, g_ref, m_ref, v_ref, sum_ref, back_ref, sem):
    fetch_maps(pos_ref, (p0, p1, p2, p3, p4), maps_ref, sem)
    consts = constants()

    def prep(i, _):
        for j in range(2):
            prepare(i * 2 + j, in_ref, maps_ref, rate_ref, consts, mat_ref, turn_ref, e_ref, g_ref, None, m_ref)
        return 0

    lax.fori_loop(0, GROUPS // 2, prep, 0)
    skip = rate_ref[1:2, :]
    for k in range(3):
        back_ref[...] = jnp.zeros((N, 128), F32)

        def step(i, _):
            back = back_ref[...]
            for j in range(UNROLL):
                c = GROUPS - 1 - (i * UNROLL + j)
                v = (in_ref[c, :Q, :] if k == 0 else v_ref[c]).astype(F32)
                x = (e_ref[c] * v).astype(BF16)
                local = dot(turn_ref[c], x)
                adj = g_ref[c] * dot(mat_ref[c], jnp.concatenate([x, back.astype(BF16)], axis=0))
                scale = m_ref[c, 0:1, :] * m_ref[jnp.maximum(c - 1, 0), 0:1, :]
                back = scale * (back + local)
                new = (adj + skip * v).astype(BF16)
                total = (v if k == 0 else sum_ref[c]) + new.astype(F32)
                if k < 2:
                    v_ref[c] = new
                    sum_ref[c] = total
                else:
                    out_ref[c] = total.astype(BF16)
            back_ref[...] = back
            return 0

        lax.fori_loop(0, GROUPS // UNROLL, step, 0)


def rate_kernel(pos_ref, in_ref, sum_ref, fixed_ref, p0, p1, p2, p3, p4, rate_ref, out_ref, maps_ref, mat_ref, turn_ref, e_ref, g_ref, s_ref, m_ref, back_ref, acc_ref, sem):
    fetch_maps(pos_ref, (p0, p1, p2, p3, p4), maps_ref, sem)
    consts = constants()

    def prep(i, _):
        for j in range(2):
            prepare(i * 2 + j, in_ref, maps_ref, rate_ref, consts, mat_ref, turn_ref, e_ref, g_ref, s_ref, m_ref)
        return 0

    lax.fori_loop(0, GROUPS // 2, prep, 0)
    back_ref[...] = jnp.zeros((N, 256), F32)
    acc_ref[...] = jnp.zeros((2, 8, 128), F32)

    def step(i, _):
        back, tangent = back_ref[:, :128], back_ref[:, 128:]
        rate_sum, skip_sum = acc_ref[0], acc_ref[1]
        for j in range(2):
            c = GROUPS - 1 - (i * 2 + j)
            v = sum_ref[c].astype(F32)
            z = fixed_ref[c].astype(F32)
            s = s_ref[c]
            ev = e_ref[c] * v
            x = jnp.concatenate([ev.astype(BF16), (ev * s).astype(BF16)], axis=1)
            local = dot(turn_ref[c], x)
            tangent = tangent + s[Q - 1 : Q, :] * back
            state = jnp.concatenate([back.astype(BF16), tangent.astype(BF16)], axis=1)
            both = dot(mat_ref[c], jnp.concatenate([x, state], axis=0))
            change = g_ref[c] * (both[:, 128:] - s * both[:, :128])
            rate_sum = rate_sum + jnp.sum((z * change).reshape(16, 8, 128), axis=0)
            skip_sum = skip_sum + jnp.sum((z * v).reshape(16, 8, 128), axis=0)
            scale = m_ref[c, 0:1, :] * m_ref[jnp.maximum(c - 1, 0), 0:1, :]
            back = scale * (back + local[:, :128])
            tangent = scale * (tangent + local[:, 128:])
        back_ref[:, :128] = back
        back_ref[:, 128:] = tangent
        acc_ref[0] = rate_sum
        acc_ref[1] = skip_sum
        return 0

    lax.fori_loop(0, GROUPS // 2, step, 0)
    lane = lax.broadcasted_iota(jnp.int32, (8, 128), 1)
    row = lax.broadcasted_iota(jnp.int32, (8, 128), 0)
    first = (pos_ref[0] * NZ + pos_ref[1]) * 2
    result = jnp.zeros((8, 128), F32)
    for kind in range(2):
        for head in range(2):
            picked = jnp.where((lane >= HEAD) if head else (lane < HEAD), acc_ref[kind], 0.0)
            value = jnp.sum(picked, keepdims=True)
            value = -value if kind == 0 else value
            result = jnp.where((row == kind) & (lane == first + head), value, result)
    out_ref[...] = result


def full(shape):
    return pl.BlockSpec(shape, lambda *_: (0,) * len(shape))


HBM = pl.BlockSpec(memory_space=pltpu.HBM)
SMEM = pl.BlockSpec(memory_space=pltpu.SMEM)


def table_scratch(with_sums):
    square = pltpu.VMEM((GROUPS, Q, 128), F32)
    return [
        pltpu.VMEM((GROUPS, 2 * N, 128), BF16),
        pltpu.VMEM((GROUPS, Q, 256), BF16),
        pltpu.VMEM((GROUPS, N, Q), BF16),
        square,
        square,
        *([square] if with_sums else []),
        pltpu.VMEM((GROUPS, 8, 128), F32),
    ]


def series(pos, rows, pieces, rate):
    return pl.pallas_call(
        series_kernel,
        in_specs=[SMEM, full(rows.shape), HBM, HBM, HBM, HBM, HBM, full(rate.shape)],
        out_specs=full((GROUPS, Q, 128)),
        out_shape=jax.ShapeDtypeStruct((GROUPS, Q, 128), BF16),
        scratch_shapes=[
            *table_scratch(False),
            pltpu.VMEM((GROUPS, Q, 128), BF16),
            pltpu.VMEM((GROUPS, Q, 128), F32),
            pltpu.VMEM((N, 128), F32),
            pltpu.SemaphoreType.DMA,
        ],
        name="series",
        cost_estimate=pl.CostEstimate(flops=3_000_000_000, transcendentals=1_000_000, bytes_accessed=5_000_000),
    )(pos, rows, *pieces, rate)


def rates(pos, rows, summed, fixed, pieces, rate):
    return pl.pallas_call(
        rate_kernel,
        in_specs=[SMEM, full(rows.shape), full(summed.shape), full(fixed.shape), HBM, HBM, HBM, HBM, HBM, full(rate.shape)],
        out_specs=full((8, 128)),
        out_shape=jax.ShapeDtypeStruct((8, 128), F32),
        scratch_shapes=[
            *table_scratch(True),
            pltpu.VMEM((N, 256), F32),
            pltpu.VMEM((2, 8, 128), F32),
            pltpu.SemaphoreType.DMA,
        ],
        name="rates",
        cost_estimate=pl.CostEstimate(flops=2_000_000_000, transcendentals=1_000_000, bytes_accessed=5_000_000),
    )(pos, rows, summed, fixed, *pieces, rate)


def gather_maps(input_map, output_map):
    own = jnp.concatenate([input_map, output_map], axis=0)
    up, down = [own], [own]
    for _ in range(3):
        up.append(shifted(up[-1], "seq_1", 1))
        down.append(shifted(down[-1], "seq_1", -1))
    far_first = shifted(up[3][:N], "seq_1", 1)
    far_second = shifted(down[3][N:], "seq_1", -1)
    far = jnp.concatenate([far_first, far_second], axis=0)
    line = jnp.stack([own, down[1], down[2], down[3], far, up[3], up[2], up[1]])
    from_next = shifted(line, "seq_0", -1)
    from_last = shifted(line, "seq_0", 1)
    low = shifted(from_last[:4], "seq_0", 1)
    high = shifted(from_next[4:], "seq_0", -1)
    return line, from_next, from_last, low, high


def body(cotangent, fixed_point, input_map, output_map, step_size, forget, decay_rate, skip_gain):
    my_y, my_z = lax.axis_index("seq_0"), lax.axis_index("seq_1")
    pos = jnp.stack([my_y, my_z]).astype(jnp.int32)
    first = (my_y * NZ + my_z) * 2
    own = jnp.stack([lax.dynamic_slice_in_dim(a, first, 2) for a in (decay_rate, skip_gain)])
    rate = jnp.repeat(own, HEAD, axis=1)

    packed = pack(cotangent[0], step_size[0], forget)
    rows = lax.all_to_all(packed, SEQ, split_axis=0, concat_axis=0, tiled=True)
    pieces = gather_maps(input_map[0], output_map[0])
    fixed = lax.all_to_all(split(fixed_point[0]), SEQ, split_axis=0, concat_axis=0, tiled=True)
    summed = series(pos, rows, pieces, rate)
    result = lax.all_to_all(summed, SEQ, split_axis=0, concat_axis=0, tiled=True)
    totals = rates(pos, rows, summed, fixed, pieces, rate)
    for axis in ("batch_1", "batch_0", "seq_0", "seq_1"):
        bit = 1
        while bit < lax.axis_size(axis):
            totals = totals + swapped(totals, axis, bit)
            bit *= 2
    scale = 1.0 / (lax.axis_size(BATCH) * Q * GROUPS)
    return join(result)[None], totals[0, :H] * scale, totals[1, :H] * scale


def solution(mesh):
    torus = Mesh(mesh.devices.reshape(4, 2, 4, 8), ("batch_0", "batch_1", "seq_0", "seq_1"))
    return jax.shard_map(
        body,
        mesh=torus,
        in_specs=(
            P(BATCH, SEQ, None),
            P(BATCH, SEQ, None),
            P(BATCH, SEQ, None),
            P(BATCH, SEQ, None),
            P(BATCH, None, SEQ),
            P(BATCH, SEQ),
            P(),
            P(),
        ),
        out_specs=(P(BATCH, SEQ, None), P(), P()),
        check_vma=False,
    )
```

time: 300 us -> 190 us (0.63)
  blocking collectives: 82.3 us -> 0 us
  Pallas kernels: 0 us -> 52.1 us
  matrix products: 49.2 us -> 0 us
  starting transfers between devices: 27.8 us -> 65.6 us
  other arithmetic: 38.7 us -> 3.16 us
  local copies, waits for them, and re-layouts: 36.1 us -> 7.03 us
  waiting for transfers between devices: 63 us -> 59.5 us
    all_to_all x4 -> x3, waiting for transfers between devices: 63 us -> 0.01 us  [the longest x1 0.01 us: body(): lax.all_to_all(summed, SEQ, split_axis=0, concat_axis=0, tiled=True)]
    ppermute x0 -> x20, waiting for transfers between devices: none -> 59.5 us  [the longest x12 41.1 us: shifted(): return lax.ppermute(x, axis, [(i, (i + by) % size) for i in range(size)])]
    pallas_call x0 -> x5, Pallas kernels: none -> 52.1 us  [the longest x1 21.5 us: series(): pl.pallas_call(series_kernel, in_specs=[SMEM, full(rows.shape), HBM, HBM,...]
    dot_general x21 -> x0, matrix products: 49.2 us -> none  [the longest x5 13.3 us: finish(): jnp.einsum('hksn,hknp->kshp', weight_rows, state_in.astype(jnp.bfloat16),...]
    all_to_all x2 -> x0, blocking collectives: 43.3 us -> none  [the longest x1 30.5 us: from_everyone(): return lax.all_to_all(copies, axis, split_axis=0, concat_axis=0, tiled=True)]
    psum x4 -> x0, blocking collectives: 39 us -> none  [over_axes(): shard = lax.psum(shard, axis)]
    ppermute x0 -> x20, starting transfers between devices: none -> 32.7 us  [the longest x12 16.6 us: shifted(): return lax.ppermute(x, axis, [(i, (i + by) % size) for i in range(size)])]
    unnamed x1 -> x2, other arithmetic: 24.4 us -> 1.26 us
  transfers between devices with their start and end apart: 4 -> 23, of which waited for: 3 -> 14; matrix products, arithmetic and copies ran while one was open for 10% -> 4% of each run, Pallas kernels for 0% -> 22%
where the time goes in v1:
time: 190 us; the launch traced here: 188 us
  starting transfers between devices  65.6 us (35%)
  waiting for transfers between devices  59.5 us (31%)
  Pallas kernels  52.1 us (27%)
  local copies, waits for them, and re-layouts  7.03 us (4%)
  other arithmetic  3.16 us (2%)
    ppermute x12, waiting for transfers between devices, shifted(): return lax.ppermute(x, axis, [(i, (i + by) % size) for i in range(size)])  41.1 us
    pallas_call x1, Pallas kernels, series(): pl.pallas_call(series_kernel, in_specs=[SMEM, full(rows.shape), HBM, HBM,...  21.5 us
    ppermute x8, waiting for transfers between devices, swapped(): return lax.ppermute(x, axis, [(i, i ^ bit) for i in range(size)])  18.4 us
    ppermute x12, starting transfers between devices, shifted(): return lax.ppermute(x, axis, [(i, (i + by) % size) for i in range(size)])  16.6 us
    ppermute x8, starting transfers between devices, swapped(): return lax.ppermute(x, axis, [(i, i ^ bit) for i in range(size)])  16.1 us
    pallas_call x1, Pallas kernels, rates(): pl.pallas_call(rate_kernel, in_specs=[SMEM, full(rows.shape), full(summed...  14.9 us
    all_to_all x1, starting transfers between devices, body(): rows = lax.all_to_all(packed, SEQ, split_axis=0, concat_axis=0, tiled=True)  11.5 us
    all_to_all x1, starting transfers between devices, body(): lax.all_to_all(split(fixed_point[0]), SEQ, split_axis=0, concat_axis=0, t...  11.1 us
  transfers between devices with their start and end apart: 23, of which 14 were waited for; matrix products, arithmetic and copies ran while one was open for 4% of the time, Pallas kernels for 22%

profile of v1, /device:TPU:32, one launch (start us, length us, event | category | flops | bytes accessed | tf_op | source)
XLA Modules:
  0.0 188.1 jit_solution(15851521722281677993)
XLA Ops:
  0.6 5.3 %pack.1 = bf16[32,136,128]{2,1,0:T(8,128)(2,1)} custom-call(bf16[128,4096]{1,0:T(8,128)(2,1)} %bitcast.34, f32[64,128]{1,0:T(8,128)} %bitcast.41, f32[1,128]{1,0:T(1,128)} %forget_ref.1), custom_call_target="tpu_custom_call" | custom-call | tf_op jit(solution)/shard_map/pack/pallas_call | solution.py:58
  5.9 11.5 %all-to-all-start = ((bf16[32,136,128]{2,1,0:T(8,128)(2,1)}), bf16[32,136,128]{2,1,0:T(8,128)(2,1)S(1)}, u32[]{:S(2)}, u32[]{:S(2)}) async-start(bf16[32,136,128]{2,1,0:T(8,128)(2,1)} %pack.1), calls=%async_computation | async-start | bytes 2228224 | tf_op jit(solution)/shard_map/all_to_all | solution.py:345
  19.6 5.2 %split.1 = bf16[32,128,128]{2,1,0:T(8,128)(2,1)} custom-call(bf16[128,4096]{1,0:T(8,128)(2,1)} %bitcast.35), custom_call_target="tpu_custom_call" | custom-call | tf_op jit(solution)/shard_map/split/pallas_call | solution.py:78
  25.4 18.4 %collective-permute-done = bf16[256,128]{1,0:T(8,128)(2,1)S(1)} collective-permute-done((bf16[256,128]{1,0:T(8,128)(2,1)S(1)}, bf16[256,128]{1,0:T(8,128)(2,1)S(1)}, u32[]{:S(2)}, u32[]{:S(2)}) %collective-permute-start) | collective-permute-done | bytes 65568 | tf_op jit(solution)/shard_map/ppermute | solution.py:26
  53.8 2.5 %collective-permute-start.6 = (bf16[128,128]{1,0:T(8,128)(2,1)S(1)}, bf16[128,128]{1,0:T(8,128)(2,1)S(1)}, u32[]{:S(2)}, u32[]{:S(2)}) collective-permute-start(bf16[128,128]{1,0:T(8,128)(2,1)S(1)} %slice.24), channel_id=1, source_target_pairs={{0,1},{1,2},{2,3},{3,4},{4,5},{5,6},{6,7},{7,0},{8,9},{9,10},{10,1... | collective-permute-start | bytes 98312 | tf_op jit(solution)/shard_map/ppermute | solution.py:26
  56.4 11.1 %all-to-all-start.2 = ((bf16[32,128,128]{2,1,0:T(8,128)(2,1)}), bf16[32,128,128]{2,1,0:T(8,128)(2,1)S(1)}, u32[]{:S(2)}, u32[]{:S(2)}) async-start(bf16[32,128,128]{2,1,0:T(8,128)(2,1)} %split.1), calls=%async_computation.2 | async-start | bytes 2097152 | tf_op jit(solution)/shard_map/all_to_all | solution.py:347
  73.9 16.2 %collective-permute-done.9.p2 = bf16[8,256,128]{2,1,0:T(8,128)(2,1)S(1)} collective-permute-done((bf16[8,256,128]{2,1,0:T(8,128)(2,1)}, bf16[8,256,128]{2,1,0:T(8,128)(2,1)S(1)}, u32[]{:S(2)}, u32[]{:S(2)}) %collective-permute-start.9) | collective-permute-done | bytes 524320 | tf_op jit(solution)/shard_map/ppermute | solution.py:26
  90.5 3.0 %collective-permute-start.11 = (bf16[4,256,128]{2,1,0:T(8,128)(2,1)S(1)}, bf16[4,256,128]{2,1,0:T(8,128)(2,1)S(1)}, u32[]{:S(2)}, u32[]{:S(2)}) collective-permute-start(bf16[4,256,128]{2,1,0:T(8,128)(2,1)S(1)} %slice.27), channel_id=1, source_target_pairs={{0,24},{8,0},{16,8},{24,16},{1,25},{9,1},{17,9},{25,17},{2,26},{10... | collective-permute-start | bytes 786440 | tf_op jit(solution)/shard_map/ppermute | solution.py:26
  95.0 3.1 %collective-permute-done.10.p3 = bf16[4,256,128]{2,1,0:T(8,128)(2,1)S(1)} collective-permute-done((bf16[4,256,128]{2,1,0:T(8,128)(2,1)S(1)}, bf16[4,256,128]{2,1,0:T(8,128)(2,1)S(1)}, u32[]{:S(2)}, u32[]{:S(2)}) %collective-permute-start.10) | collective-permute-done | bytes 262176 | tf_op jit(solution)/shard_map/ppermute | solution.py:26
  99.5 21.5 %series.1.sum_ref = bf16[32,128,128]{2,1,0:T(8,128)(2,1)} custom-call(s32[2]{0:T(128)} %pad_add_fusion.pos_ref, bf16[32,136,128]{2,1,0:T(8,128)(2,1)} %copy-done.1, bf16[8,256,128]{2,1,0:T(8,128)(2,1)} %bitcast_dynamic-update-slice_fusion.p0, bf16[8,256,128]{2,1,0:T(8,128)(2,1)} %copy-done.4, bf16[8,256,128]{2,1,0:T(8,128)(2,1)} %copy-done.3, ...), custom_call_target="tpu_custom_call" | custom-call | flops 3000000000 | bytes 5000000 | tf_op jit(solution)/shard_map/series/pallas_call | solution.py:286
  121.0 10.3 %all-to-all-start.1 = ((bf16[32,128,128]{2,1,0:T(8,128)(2,1)}), bf16[32,128,128]{2,1,0:T(8,128)(2,1)S(1)}, u32[]{:S(2)}, u32[]{:S(2)}) async-start(bf16[32,128,128]{2,1,0:T(8,128)(2,1)} %series.1.sum_ref), calls=%async_computation.1 | async-start | bytes 2097152 | tf_op jit(solution)/shard_map/all_to_all | solution.py:349
  131.3 14.9 %rates.1 = f32[8,128]{1,0:T(8,128)} custom-call(s32[2]{0:T(128)} %pad_add_fusion.pos_ref, bf16[32,136,128]{2,1,0:T(8,128)(2,1)} %copy-done.1, bf16[32,128,128]{2,1,0:T(8,128)(2,1)} %series.1.sum_ref, bf16[32,128,128]{2,1,0:T(8,128)(2,1)} %copy-done.2, bf16[8,256,128]{2,1,0:T(8,128)(2,1)} %bitcast_dynamic-update-slice_fusion.p0, ...), custom_call_target="tpu_custom_call" | custom-call | flops 2000000000 | bytes 5000000 | tf_op jit(solution)/shard_map/rates/pallas_call | solution.py:304
  149.8 2.1 %collective-permute-done.13 = f32[8,128]{1,0:T(8,128)S(1)} collective-permute-done((f32[8,128]{1,0:T(8,128)S(1)}, f32[8,128]{1,0:T(8,128)S(1)}, u32[]{:S(2)}, u32[]{:S(2)}) %collective-permute-start.13) | collective-permute-done | bytes 4128 | tf_op jit(solution)/shard_map/ppermute | solution.py:31
  151.9 3.0 %collective-permute-start.14 = (f32[8,128]{1,0:T(8,128)S(1)}, f32[8,128]{1,0:T(8,128)S(1)}, u32[]{:S(2)}, u32[]{:S(2)}) collective-permute-start(f32[8,128]{1,0:T(8,128)S(1)} %add.34), channel_id=1, source_target_pairs={{0,128},{64,192},{128,0},{192,64},{1,129},{65,193},{129,1},{193,65... | collective-permute-start | bytes 12296 | tf_op jit(solution)/shard_map/ppermute | solution.py:31
  154.9 2.1 %collective-permute-done.14 = f32[8,128]{1,0:T(8,128)S(1)} collective-permute-done((f32[8,128]{1,0:T(8,128)S(1)}, f32[8,128]{1,0:T(8,128)S(1)}, u32[]{:S(2)}, u32[]{:S(2)}) %collective-permute-start.14) | collective-permute-done | bytes 4128 | tf_op jit(solution)/shard_map/ppermute | solution.py:31
  158.5 2.1 %collective-permute-done.15 = f32[8,128]{1,0:T(8,128)S(1)} collective-permute-done((f32[8,128]{1,0:T(8,128)S(1)}, f32[8,128]{1,0:T(8,128)S(1)}, u32[]{:S(2)}, u32[]{:S(2)}) %collective-permute-start.15) | collective-permute-done | bytes 4128 | tf_op jit(solution)/shard_map/ppermute | solution.py:31
  160.6 3.0 %collective-permute-start.16 = (f32[8,128]{1,0:T(8,128)S(1)}, f32[8,128]{1,0:T(8,128)S(1)}, u32[]{:S(2)}, u32[]{:S(2)}) collective-permute-start(f32[8,128]{1,0:T(8,128)S(1)} %add.36), channel_id=1, source_target_pairs={{0,16},{8,24},{16,0},{24,8},{1,17},{9,25},{17,1},{25,9},{2,18},{10... | collective-permute-start | bytes 12296 | tf_op jit(solution)/shard_map/ppermute | solution.py:31
  163.6 2.1 %collective-permute-done.16 = f32[8,128]{1,0:T(8,128)S(1)} collective-permute-done((f32[8,128]{1,0:T(8,128)S(1)}, f32[8,128]{1,0:T(8,128)S(1)}, u32[]{:S(2)}, u32[]{:S(2)}) %collective-permute-start.16) | collective-permute-done | bytes 4128 | tf_op jit(solution)/shard_map/ppermute | solution.py:31
  166.0 3.4 %collective-permute-done.17 = f32[8,128]{1,0:T(8,128)S(1)} collective-permute-done((f32[8,128]{1,0:T(8,128)S(1)}, f32[8,128]{1,0:T(8,128)S(1)}, u32[]{:S(2)}, u32[]{:S(2)}) %collective-permute-start.17) | collective-permute-done | bytes 4128 | tf_op jit(solution)/shard_map/ppermute | solution.py:31
  169.4 2.4 %collective-permute-start.18 = (f32[8,128]{1,0:T(8,128)S(1)}, f32[8,128]{1,0:T(8,128)S(1)}, u32[]{:S(2)}, u32[]{:S(2)}) collective-permute-start(f32[8,128]{1,0:T(8,128)S(1)} %add.38), channel_id=1, source_target_pairs={{0,2},{1,3},{2,0},{3,1},{4,6},{5,7},{6,4},{7,5},{8,10},{9,11},{10,... | collective-permute-start | bytes 12296 | tf_op jit(solution)/shard_map/ppermute | solution.py:31
  171.7 2.1 %collective-permute-done.18 = f32[8,128]{1,0:T(8,128)S(1)} collective-permute-done((f32[8,128]{1,0:T(8,128)S(1)}, f32[8,128]{1,0:T(8,128)S(1)}, u32[]{:S(2)}, u32[]{:S(2)}) %collective-permute-start.18) | collective-permute-done | bytes 4128 | tf_op jit(solution)/shard_map/ppermute | solution.py:31
  173.9 4.5 %collective-permute-start.19 = (f32[8,128]{1,0:T(8,128)S(1)}, f32[8,128]{1,0:T(8,128)S(1)}, u32[]{:S(2)}, u32[]{:S(2)}) collective-permute-start(f32[8,128]{1,0:T(8,128)S(1)} %add.39), channel_id=1, source_target_pairs={{0,4},{1,5},{2,6},{3,7},{4,0},{5,1},{6,2},{7,3},{8,12},{9,13},{10,... | collective-permute-start | bytes 12296 | tf_op jit(solution)/shard_map/ppermute | solution.py:31
  178.3 3.0 %collective-permute-done.19 = f32[8,128]{1,0:T(8,128)S(1)} collective-permute-done((f32[8,128]{1,0:T(8,128)S(1)}, f32[8,128]{1,0:T(8,128)S(1)}, u32[]{:S(2)}, u32[]{:S(2)}) %collective-permute-start.19) | collective-permute-done | bytes 4128 | tf_op jit(solution)/shard_map/ppermute | solution.py:31
  182.9 5.2 %join.1 = bf16[128,4096]{1,0:T(8,128)(2,1)} custom-call(bf16[32,128,128]{2,1,0:T(8,128)(2,1)} %copy-done), custom_call_target="tpu_custom_call" | custom-call | tf_op jit(solution)/shard_map/join/pallas_call | solution.py:94
  (76 shorter events, 29.4 us)
Async XLA Ops:
  5.9 50.4 %all-to-all-start = ((bf16[32,136,128]{2,1,0:T(8,128)(2,1)}), bf16[32,136,128]{2,1,0:T(8,128)(2,1)S(1)}, u32[]{:S(2)}, u32[]{:S(2)}) async-start(bf16[32,136,128]{2,1,0:T(8,128)(2,1)} %pack.1), calls=%async_computation | async-start | bytes 2228224 | tf_op jit(solution)/shard_map/all_to_all | solution.py:345
  17.5 26.3 %collective-permute-start = (bf16[256,128]{1,0:T(8,128)(2,1)S(1)}, bf16[256,128]{1,0:T(8,128)(2,1)S(1)}, u32[]{:S(2)}, u32[]{:S(2)}) collective-permute-start(bf16[256,128]{1,0:T(8,128)(2,1)S(1)} %pad_maximum_fusion), channel_id=1, source_target_pairs={{0,7},{1,0},{2,1},{3,2},{4,3},{5,4},{6,5},{7,6},{8,15},{9,8},{10,9... | collective-permute-start | bytes 196616 | tf_op jit(solution)/shard_map/ppermute | solution.py:26
  17.8 27.2 %collective-permute-start.3 = (bf16[256,128]{1,0:T(8,128)(2,1)S(1)}, bf16[256,128]{1,0:T(8,128)(2,1)S(1)}, u32[]{:S(2)}, u32[]{:S(2)}) collective-permute-start(bf16[256,128]{1,0:T(8,128)(2,1)S(1)} %pad_maximum_fusion), channel_id=1, source_target_pairs={{0,1},{1,2},{2,3},{3,4},{4,5},{5,6},{6,7},{7,0},{8,9},{9,10},{10,1... | collective-permute-start | bytes 196616 | tf_op jit(solution)/shard_map/ppermute | solution.py:26
  43.8 4.3 %collective-permute-start.1 = (bf16[256,128]{1,0:T(8,128)(2,1)S(1)}, bf16[256,128]{1,0:T(8,128)(2,1)S(1)}, u32[]{:S(2)}, u32[]{:S(2)}) collective-permute-start(bf16[256,128]{1,0:T(8,128)(2,1)S(1)} %collective-permute-done), channel_id=1, source_target_pairs={{0,7},{1,0},{2,1},{3,2},{4,3},{5,4},{6,5},{7,6},{8,15},{9,8},{10,9... | collective-permute-start | bytes 196616 | tf_op jit(solution)/shard_map/ppermute | solution.py:26
  45.0 4.3 %collective-permute-start.4 = (bf16[256,128]{1,0:T(8,128)(2,1)S(1)}, bf16[256,128]{1,0:T(8,128)(2,1)S(1)}, u32[]{:S(2)}, u32[]{:S(2)}) collective-permute-start(bf16[256,128]{1,0:T(8,128)(2,1)S(1)} %collective-permute-done.3), channel_id=1, source_target_pairs={{0,1},{1,2},{2,3},{3,4},{4,5},{5,6},{6,7},{7,0},{8,9},{9,10},{10,1... | collective-permute-start | bytes 196616 | tf_op jit(solution)/shard_map/ppermute | solution.py:26
  48.1 4.9 %collective-permute-start.2 = (bf16[256,128]{1,0:T(8,128)(2,1)S(1)}, bf16[256,128]{1,0:T(8,128)(2,1)S(1)}, u32[]{:S(2)}, u32[]{:S(2)}) collective-permute-start(bf16[256,128]{1,0:T(8,128)(2,1)S(1)} %collective-permute-done.1), channel_id=1, source_target_pairs={{0,7},{1,0},{2,1},{3,2},{4,3},{5,4},{6,5},{7,6},{8,15},{9,8},{10,9... | collective-permute-start | bytes 196616 | tf_op jit(solution)/shard_map/ppermute | solution.py:26
  49.3 4.6 %collective-permute-start.5 = (bf16[256,128]{1,0:T(8,128)(2,1)S(1)}, bf16[256,128]{1,0:T(8,128)(2,1)S(1)}, u32[]{:S(2)}, u32[]{:S(2)}) collective-permute-start(bf16[256,128]{1,0:T(8,128)(2,1)S(1)} %collective-permute-done.4), channel_id=1, source_target_pairs={{0,1},{1,2},{2,3},{3,4},{4,5},{5,6},{6,7},{7,0},{8,9},{9,10},{10,1... | collective-permute-start | bytes 196616 | tf_op jit(solution)/shard_map/ppermute | solution.py:26
  53.0 15.1 %collective-permute-start.7 = (bf16[128,128]{1,0:T(8,128)(2,1)S(1)}, bf16[128,128]{1,0:T(8,128)(2,1)S(1)}, u32[]{:S(2)}, u32[]{:S(2)}) collective-permute-start(bf16[128,128]{1,0:T(8,128)(2,1)S(1)} %slice.25), channel_id=1, source_target_pairs={{0,7},{1,0},{2,1},{3,2},{4,3},{5,4},{6,5},{7,6},{8,15},{9,8},{10,9... | collective-permute-start | bytes 98312 | tf_op jit(solution)/shard_map/ppermute | solution.py:26
  53.8 14.3 %collective-permute-start.6 = (bf16[128,128]{1,0:T(8,128)(2,1)S(1)}, bf16[128,128]{1,0:T(8,128)(2,1)S(1)}, u32[]{:S(2)}, u32[]{:S(2)}) collective-permute-start(bf16[128,128]{1,0:T(8,128)(2,1)S(1)} %slice.24), channel_id=1, source_target_pairs={{0,1},{1,2},{2,3},{3,4},{4,5},{5,6},{6,7},{7,0},{8,9},{9,10},{10,1... | collective-permute-start | bytes 98312 | tf_op jit(solution)/shard_map/ppermute | solution.py:26
  56.4 64.6 %all-to-all-start.2 = ((bf16[32,128,128]{2,1,0:T(8,128)(2,1)}), bf16[32,128,128]{2,1,0:T(8,128)(2,1)S(1)}, u32[]{:S(2)}, u32[]{:S(2)}) async-start(bf16[32,128,128]{2,1,0:T(8,128)(2,1)} %split.1), calls=%async_computation.2 | async-start | bytes 2097152 | tf_op jit(solution)/shard_map/all_to_all | solution.py:347
  67.5 26.0 %copy-start.7 = (f32[64]{0:T(128)S(1)}, f32[64]{0:T(128)}, u32[]{:S(2)}) copy-start(f32[64]{0:T(128)} %param.15) | copy-start | bytes 772
  70.7 19.4 %collective-permute-start.9 = (bf16[8,256,128]{2,1,0:T(8,128)(2,1)}, bf16[8,256,128]{2,1,0:T(8,128)(2,1)S(1)}, u32[]{:S(2)}, u32[]{:S(2)}) collective-permute-start(bf16[8,256,128]{2,1,0:T(8,128)(2,1)} %bitcast_dynamic-update-slice_fusion.p0), channel_id=1, source_target_pairs={{0,8},{8,16},{16,24},{24,0},{1,9},{9,17},{17,25},{25,1},{2,10},{10... | collective-permute-start | bytes 1572872 | tf_op jit(solution)/shard_map/ppermute | solution.py:26
  72.2 18.3 %collective-permute-start.8 = (bf16[8,256,128]{2,1,0:T(8,128)(2,1)}, bf16[8,256,128]{2,1,0:T(8,128)(2,1)S(1)}, u32[]{:S(2)}, u32[]{:S(2)}) collective-permute-start(bf16[8,256,128]{2,1,0:T(8,128)(2,1)} %bitcast_dynamic-update-slice_fusion.p0), channel_id=1, source_target_pairs={{0,24},{8,0},{16,8},{24,16},{1,25},{9,1},{17,9},{25,17},{2,26},{10... | collective-permute-start | bytes 1572872 | tf_op jit(solution)/shard_map/ppermute | solution.py:26
  90.1 8.0 %collective-permute-start.10 = (bf16[4,256,128]{2,1,0:T(8,128)(2,1)S(1)}, bf16[4,256,128]{2,1,0:T(8,128)(2,1)S(1)}, u32[]{:S(2)}, u32[]{:S(2)}) collective-permute-start(bf16[4,256,128]{2,1,0:T(8,128)(2,1)S(1)} %slice.26), channel_id=1, source_target_pairs={{0,8},{8,16},{16,24},{24,0},{1,9},{9,17},{17,25},{25,1},{2,10},{10... | collective-permute-start | bytes 786440 | tf_op jit(solution)/shard_map/ppermute | solution.py:26
  90.5 7.6 %collective-permute-start.11 = (bf16[4,256,128]{2,1,0:T(8,128)(2,1)S(1)}, bf16[4,256,128]{2,1,0:T(8,128)(2,1)S(1)}, u32[]{:S(2)}, u32[]{:S(2)}) collective-permute-start(bf16[4,256,128]{2,1,0:T(8,128)(2,1)S(1)} %slice.27), channel_id=1, source_target_pairs={{0,24},{8,0},{16,8},{24,16},{1,25},{9,1},{17,9},{25,17},{2,26},{10... | collective-permute-start | bytes 786440 | tf_op jit(solution)/shard_map/ppermute | solution.py:26
  121.0 60.9 %all-to-all-start.1 = ((bf16[32,128,128]{2,1,0:T(8,128)(2,1)}), bf16[32,128,128]{2,1,0:T(8,128)(2,1)S(1)}, u32[]{:S(2)}, u32[]{:S(2)}) async-start(bf16[32,128,128]{2,1,0:T(8,128)(2,1)} %series.1.sum_ref), calls=%async_computation.1 | async-start | bytes 2097152 | tf_op jit(solution)/shard_map/all_to_all | solution.py:349
  146.2 1.5 collective-permute-start.12
  148.3 3.6 %collective-permute-start.13 = (f32[8,128]{1,0:T(8,128)S(1)}, f32[8,128]{1,0:T(8,128)S(1)}, u32[]{:S(2)}, u32[]{:S(2)}) collective-permute-start(f32[8,128]{1,0:T(8,128)S(1)} %add.33), channel_id=1, source_target_pairs={{0,64},{64,0},{128,192},{192,128},{1,65},{65,1},{129,193},{193,129... | collective-permute-start | bytes 12296 | tf_op jit(solution)/shard_map/ppermute | solution.py:31
  151.9 5.1 %collective-permute-start.14 = (f32[8,128]{1,0:T(8,128)S(1)}, f32[8,128]{1,0:T(8,128)S(1)}, u32[]{:S(2)}, u32[]{:S(2)}) collective-permute-start(f32[8,128]{1,0:T(8,128)S(1)} %add.34), channel_id=1, source_target_pairs={{0,128},{64,192},{128,0},{192,64},{1,129},{65,193},{129,1},{193,65... | collective-permute-start | bytes 12296 | tf_op jit(solution)/shard_map/ppermute | solution.py:31
  157.0 3.6 %collective-permute-start.15 = (f32[8,128]{1,0:T(8,128)S(1)}, f32[8,128]{1,0:T(8,128)S(1)}, u32[]{:S(2)}, u32[]{:S(2)}) collective-permute-start(f32[8,128]{1,0:T(8,128)S(1)} %add.35), channel_id=1, source_target_pairs={{0,8},{8,0},{16,24},{24,16},{1,9},{9,1},{17,25},{25,17},{2,10},{10... | collective-permute-start | bytes 12296 | tf_op jit(solution)/shard_map/ppermute | solution.py:31
  160.6 5.1 %collective-permute-start.16 = (f32[8,128]{1,0:T(8,128)S(1)}, f32[8,128]{1,0:T(8,128)S(1)}, u32[]{:S(2)}, u32[]{:S(2)}) collective-permute-start(f32[8,128]{1,0:T(8,128)S(1)} %add.36), channel_id=1, source_target_pairs={{0,16},{8,24},{16,0},{24,8},{1,17},{9,25},{17,1},{25,9},{2,18},{10... | collective-permute-start | bytes 12296 | tf_op jit(solution)/shard_map/ppermute | solution.py:31
  165.8 3.6 %collective-permute-start.17 = (f32[8,128]{1,0:T(8,128)S(1)}, f32[8,128]{1,0:T(8,128)S(1)}, u32[]{:S(2)}, u32[]{:S(2)}) collective-permute-start(f32[8,128]{1,0:T(8,128)S(1)} %add.37), channel_id=1, source_target_pairs={{0,1},{1,0},{2,3},{3,2},{4,5},{5,4},{6,7},{7,6},{8,9},{9,8},{10,11... | collective-permute-start | bytes 12296 | tf_op jit(solution)/shard_map/ppermute | solution.py:31
  169.4 4.5 %collective-permute-start.18 = (f32[8,128]{1,0:T(8,128)S(1)}, f32[8,128]{1,0:T(8,128)S(1)}, u32[]{:S(2)}, u32[]{:S(2)}) collective-permute-start(f32[8,128]{1,0:T(8,128)S(1)} %add.38), channel_id=1, source_target_pairs={{0,2},{1,3},{2,0},{3,1},{4,6},{5,7},{6,4},{7,5},{8,10},{9,11},{10,... | collective-permute-start | bytes 12296 | tf_op jit(solution)/shard_map/ppermute | solution.py:31
  173.9 7.5 %collective-permute-start.19 = (f32[8,128]{1,0:T(8,128)S(1)}, f32[8,128]{1,0:T(8,128)S(1)}, u32[]{:S(2)}, u32[]{:S(2)}) collective-permute-start(f32[8,128]{1,0:T(8,128)S(1)} %add.39), channel_id=1, source_target_pairs={{0,4},{1,5},{2,6},{3,7},{4,0},{5,1},{6,2},{7,3},{8,12},{9,13},{10,... | collective-permute-start | bytes 12296 | tf_op jit(solution)/shard_map/ppermute | solution.py:31
  (10 other events, 89.8 us)

commit v2 on v1

--- a/solution.py
+++ b/solution.py
@@ -14,7 +14,9 @@
 GROUPS = 32
 NY = 4
 NZ = 8
-UNROLL = 4
+UNROLL = 16
+PREP = 16
+PAIRED = 8
 SEQ = ("seq_0", "seq_1")
 BATCH = ("batch_0", "batch_1")
 F32 = jnp.float32
@@ -31,72 +33,86 @@
     return lax.ppermute(x, axis, [(i, i ^ bit) for i in range(size)])
 
 
+def full(shape):
+    return pl.BlockSpec(shape, lambda *_: (0,) * len(shape))
+
+
+HBM = pl.BlockSpec(memory_space=pltpu.HBM)
+SMEM = pl.BlockSpec(memory_space=pltpu.SMEM)
+
+
 def halves(x):
     high = x.astype(BF16)
     return high, (x - high.astype(F32)).astype(BF16)
 
 
-def pack_kernel(cot_ref, step_ref, forget_ref, out_ref):
+def pack_kernel(step_ref, forget_ref, cot_ref, out_ref, sem):
+    copies = [
+        pltpu.make_async_copy(cot_ref.at[:, pl.ds(j * 128, 128)], out_ref.at[j, pl.ds(0, Q), :], sem)
+        for j in range(GROUPS)
+    ]
+    for c in copies:
+        c.start()
     step_high, step_low = halves(step_ref[...])
-    forget_high, forget_low = halves(forget_ref[...])
-    for j in range(4):
-        out_ref[j, :Q, :] = cot_ref[:, j * 128 : (j + 1) * 128]
-        rows = jnp.concatenate(
-            [
-                step_high[2 * j : 2 * j + 2].astype(F32),
-                step_low[2 * j : 2 * j + 2].astype(F32),
-                forget_high.astype(F32),
-                forget_low.astype(F32),
-                jnp.zeros((2, Q), F32),
-            ],
-            axis=0,
-        )
+    step_high, step_low = step_high.astype(F32), step_low.astype(F32)
+    tail = [f.astype(F32) for f in halves(forget_ref[...])] + [jnp.zeros((2, Q), F32)]
+    for j in range(GROUPS):
+        two = slice(2 * j, 2 * j + 2)
+        rows = jnp.concatenate([step_high[two], step_low[two], *tail], axis=0)
         out_ref[j, Q : Q + EXTRA, :] = rows.astype(BF16)
+    for c in copies:
+        c.wait()
 
 
 def pack(cot, step, forget):
     return pl.pallas_call(
         pack_kernel,
-        grid=(8,),
-        in_specs=[
-            pl.BlockSpec((Q, 512), lambda i: (0, i)),
-            pl.BlockSpec((8, Q), lambda i: (i, 0)),
-            pl.BlockSpec((1, Q), lambda i: (0, 0)),
-        ],
-        out_specs=pl.BlockSpec((4, Q + EXTRA, 128), lambda i: (i, 0, 0)),
+        in_specs=[full(step.shape), full(forget.shape), HBM],
+        out_specs=full((GROUPS, Q + EXTRA, 128)),
         out_shape=jax.ShapeDtypeStruct((GROUPS, Q + EXTRA, 128), BF16),
+        scratch_shapes=[pltpu.SemaphoreType.DMA],
         name="pack",
-    )(cot, step, forget)
-
-
-def split_kernel(in_ref, out_ref):
-    for j in range(4):
-        out_ref[j] = in_ref[:, j * 128 : (j + 1) * 128]
+    )(step, forget, cot)
+
+
+def split_kernel(in_ref, out_ref, sem):
+    copies = [
+        pltpu.make_async_copy(in_ref.at[:, pl.ds(j * 128, 128)], out_ref.at[j], sem) for j in range(GROUPS)
+    ]
+    for c in copies:
+        c.start()
+    for c in copies:
+        c.wait()
 
 
 def split(x):
     return pl.pallas_call(
         split_kernel,
-        grid=(8,),
-        in_specs=[pl.BlockSpec((Q, 512), lambda i: (0, i))],
-        out_specs=pl.BlockSpec((4, Q, 128), lambda i: (i, 0, 0)),
+        in_specs=[HBM],
+        out_specs=full((GROUPS, Q, 128)),
         out_shape=jax.ShapeDtypeStruct((GROUPS, Q, 128), BF16),
+        scratch_shapes=[pltpu.SemaphoreType.DMA],
         name="split",
     )(x)
 
 
-def join_kernel(in_ref, out_ref):
-    for j in range(4):
-        out_ref[:, j * 128 : (j + 1) * 128] = in_ref[j]
+def join_kernel(in_ref, out_ref, sem):
+    copies = [
+        pltpu.make_async_copy(in_ref.at[j], out_ref.at[:, pl.ds(j * 128, 128)], sem) for j in range(GROUPS)
+    ]
+    for c in copies:
+        c.start()
+    for c in copies:
+        c.wait()
 
 
 def join(x):
     return pl.pallas_call(
         join_kernel,
-        grid=(8,),
-        in_specs=[pl.BlockSpec((4, Q, 128), lambda i: (i, 0, 0))],
-        out_specs=pl.BlockSpec((Q, 512), lambda i: (0, i)),
+        in_specs=[full(x.shape)],
+        out_specs=HBM,
         out_shape=jax.ShapeDtypeStruct((Q, GROUPS * 128), BF16),
+        scratch_shapes=[pltpu.SemaphoreType.DMA],
         name="join",
     )(x)
 
@@ -176,33 +192,42 @@
     consts = constants()
 
     def prep(i, _):
-        for j in range(2):
-            prepare(i * 2 + j, in_ref, maps_ref, rate_ref, consts, mat_ref, turn_ref, e_ref, g_ref, None, m_ref)
+        for j in range(PREP):
+            prepare(i * PREP + j, in_ref, maps_ref, rate_ref, consts, mat_ref, turn_ref, e_ref, g_ref, None, m_ref)
         return 0
 
-    lax.fori_loop(0, GROUPS // 2, prep, 0)
+    lax.fori_loop(0, GROUPS // PREP, prep, 0)
     skip = rate_ref[1:2, :]
     for k in range(3):
         back_ref[...] = jnp.zeros((N, 128), F32)
 
         def step(i, _):
+            groups = [GROUPS - 1 - (i * UNROLL + j) for j in range(UNROLL)]
+            values = [(in_ref[c, :Q, :] if k == 0 else v_ref[c]).astype(F32) for c in groups]
+            turned = [(e_ref[c] * v).astype(BF16) for c, v in zip(groups, values)]
+            local = [dot(turn_ref[c], x) for c, x in zip(groups, turned)]
             back = back_ref[...]
-            for j in range(UNROLL):
-                c = GROUPS - 1 - (i * UNROLL + j)
-                v = (in_ref[c, :Q, :] if k == 0 else v_ref[c]).astype(F32)
-                x = (e_ref[c] * v).astype(BF16)
-                local = dot(turn_ref[c], x)
-                adj = g_ref[c] * dot(mat_ref[c], jnp.concatenate([x, back.astype(BF16)], axis=0))
+            states = []
+            for j, c in enumerate(groups):
+                states.append(back.astype(BF16))
                 scale = m_ref[c, 0:1, :] * m_ref[jnp.maximum(c - 1, 0), 0:1, :]
-                back = scale * (back + local)
-                new = (adj + skip * v).astype(BF16)
-                total = (v if k == 0 else sum_ref[c]) + new.astype(F32)
+                back = scale * (back + local[j])
+            back_ref[...] = back
+            mixed = [
+                dot(mat_ref[c], jnp.concatenate([x, b], axis=0)) for c, x, b in zip(groups, turned, states)
+            ]
+            fresh = [
+                (g_ref[c] * r + skip * v).astype(BF16) for c, r, v in zip(groups, mixed, values)
+            ]
+            totals = [
+                (v if k == 0 else sum_ref[c]) + n.astype(F32) for c, v, n in zip(groups, values, fresh)
+            ]
+            for c, n, t in zip(groups, fresh, totals):
                 if k < 2:
-                    v_ref[c] = new
-                    sum_ref[c] = total
+                    v_ref[c] = n
+                    sum_ref[c] = t
                 else:
-                    out_ref[c] = total.astype(BF16)
-            back_ref[...] = back
+                    out_ref[c] = t.astype(BF16)
             return 0
 
         lax.fori_loop(0, GROUPS // UNROLL, step, 0)
@@ -213,43 +238,45 @@
     consts = constants()
 
     def prep(i, _):
-        for j in range(2):
-            prepare(i * 2 + j, in_ref, maps_ref, rate_ref, consts, mat_ref, turn_ref, e_ref, g_ref, s_ref, m_ref)
+        for j in range(PREP):
+            prepare(i * PREP + j, in_ref, maps_ref, rate_ref, consts, mat_ref, turn_ref, e_ref, g_ref, s_ref, m_ref)
         return 0
 
-    lax.fori_loop(0, GROUPS // 2, prep, 0)
+    lax.fori_loop(0, GROUPS // PREP, prep, 0)
     back_ref[...] = jnp.zeros((N, 256), F32)
     acc_ref[...] = jnp.zeros((2, 8, 128), F32)
 
     def step(i, _):
+        groups = [GROUPS - 1 - (i * PAIRED + j) for j in range(PAIRED)]
+        values = [sum_ref[c].astype(F32) for c in groups]
+        turned = []
+        for c, v in zip(groups, values):
+            ev = e_ref[c] * v
+            turned.append(jnp.concatenate([ev.astype(BF16), (ev * s_ref[c]).astype(BF16)], axis=1))
+        local = [dot(turn_ref[c], x) for c, x in zip(groups, turned)]
         back, tangent = back_ref[:, :128], back_ref[:, 128:]
+        states = []
+        for j, c in enumerate(groups):
+            tangent = tangent + s_ref[c, Q - 1 : Q, :] * back
+            states.append(jnp.concatenate([back.astype(BF16), tangent.astype(BF16)], axis=1))
+            scale = m_ref[c, 0:1, :] * m_ref[jnp.maximum(c - 1, 0), 0:1, :]
+            back = scale * (back + local[j][:, :128])
+            tangent = scale * (tangent + local[j][:, 128:])
+        back_ref[:, :128] = back
+        back_ref[:, 128:] = tangent
+        mixed = [dot(mat_ref[c], jnp.concatenate([x, b], axis=0)) for c, x, b in zip(groups, turned, states)]
         rate_sum, skip_sum = acc_ref[0], acc_ref[1]
-        for j in range(2):
-            c = GROUPS - 1 - (i * 2 + j)
-            v = sum_ref[c].astype(F32)
+        for c, v, r in zip(groups, values, mixed):
             z = fixed_ref[c].astype(F32)
-            s = s_ref[c]
-            ev = e_ref[c] * v
-            x = jnp.concatenate([ev.astype(BF16), (ev * s).astype(BF16)], axis=1)
-            local = dot(turn_ref[c], x)
-            tangent = tangent + s[Q - 1 : Q, :] * back
-            state = jnp.concatenate([back.astype(BF16), tangent.astype(BF16)], axis=1)
-            both = dot(mat_ref[c], jnp.concatenate([x, state], axis=0))
-            change = g_ref[c] * (both[:, 128:] - s * both[:, :128])
+            change = g_ref[c] * (r[:, 128:] - s_ref[c] * r[:, :128])
             rate_sum = rate_sum + jnp.sum((z * change).reshape(16, 8, 128), axis=0)
             skip_sum = skip_sum + jnp.sum((z * v).reshape(16, 8, 128), axis=0)
-            scale = m_ref[c, 0:1, :] * m_ref[jnp.maximum(c - 1, 0), 0:1, :]
-            back = scale * (back + local[:, :128])
-            tangent = scale * (tangent + local[:, 128:])
-        back_ref[:, :128] = back
-        back_ref[:, 128:] = tangent
         acc_ref[0] = rate_sum
         acc_ref[1] = skip_sum
         return 0
 
-    lax.fori_loop(0, GROUPS // 2, step, 0)
+    lax.fori_loop(0, GROUPS // PAIRED, step, 0)
     lane = lax.broadcasted_iota(jnp.int32, (8, 128), 1)
-    row = lax.broadcasted_iota(jnp.int32, (8, 128), 0)
     first = (pos_ref[0] * NZ + pos_ref[1]) * 2
     result = jnp.zeros((8, 128), F32)
     for kind in range(2):
@@ -257,16 +284,8 @@
             picked = jnp.where((lane >= HEAD) if head else (lane < HEAD), acc_ref[kind], 0.0)
             value = jnp.sum(picked, keepdims=True)
             value = -value if kind == 0 else value
-            result = jnp.where((row == kind) & (lane == first + head), value, result)
+            result = jnp.where(lane == kind * H + first + head, value, result)
     out_ref[...] = result
-
-
-def full(shape):
-    return pl.BlockSpec(shape, lambda *_: (0,) * len(shape))
-
-
-HBM = pl.BlockSpec(memory_space=pltpu.HBM)
-SMEM = pl.BlockSpec(memory_space=pltpu.SMEM)
 
 
 def table_scratch(with_sums):
@@ -317,7 +336,7 @@
     )(pos, rows, summed, fixed, *pieces, rate)
 
 
-def gather_maps(input_map, output_map):
+def gather_line(input_map, output_map):
     own = jnp.concatenate([input_map, output_map], axis=0)
     up, down = [own], [own]
     for _ in range(3):
@@ -326,7 +345,10 @@
     far_first = shifted(up[3][:N], "seq_1", 1)
     far_second = shifted(down[3][N:], "seq_1", -1)
     far = jnp.concatenate([far_first, far_second], axis=0)
-    line = jnp.stack([own, down[1], down[2], down[3], far, up[3], up[2], up[1]])
+    return jnp.stack([own, down[1], down[2], down[3], far, up[3], up[2], up[1]])
+
+
+def gather_plane(line):
     from_next = shifted(line, "seq_0", -1)
     from_last = shifted(line, "seq_0", 1)
     low = shifted(from_last[:4], "seq_0", 1)
@@ -334,33 +356,36 @@
     return line, from_next, from_last, low, high
 
 
-def body(cotangent, fixed_point, input_map, output_map, step_size, forget, decay_rate, skip_gain):
+def inner(cotangent, fixed_point, input_map, output_map, step_size, forget, decay_rate, skip_gain):
     my_y, my_z = lax.axis_index("seq_0"), lax.axis_index("seq_1")
     pos = jnp.stack([my_y, my_z]).astype(jnp.int32)
     first = (my_y * NZ + my_z) * 2
     own = jnp.stack([lax.dynamic_slice_in_dim(a, first, 2) for a in (decay_rate, skip_gain)])
     rate = jnp.repeat(own, HEAD, axis=1)
 
-    packed = pack(cotangent[0], step_size[0], forget)
+    line = gather_line(input_map[0], output_map[0])
+    packed, line = lax.optimization_barrier((pack(cotangent[0], step_size[0], forget), line))
+    pieces = gather_plane(line)
     rows = lax.all_to_all(packed, SEQ, split_axis=0, concat_axis=0, tiled=True)
-    pieces = gather_maps(input_map[0], output_map[0])
     fixed = lax.all_to_all(split(fixed_point[0]), SEQ, split_axis=0, concat_axis=0, tiled=True)
     summed = series(pos, rows, pieces, rate)
     result = lax.all_to_all(summed, SEQ, split_axis=0, concat_axis=0, tiled=True)
     totals = rates(pos, rows, summed, fixed, pieces, rate)
-    for axis in ("batch_1", "batch_0", "seq_0", "seq_1"):
+    for axis in BATCH:
         bit = 1
         while bit < lax.axis_size(axis):
             totals = totals + swapped(totals, axis, bit)
             bit *= 2
-    scale = 1.0 / (lax.axis_size(BATCH) * Q * GROUPS)
-    return join(result)[None], totals[0, :H] * scale, totals[1, :H] * scale
+    copies = jnp.broadcast_to(totals[:1], (GROUPS, 1, 128))
+    totals = lax.all_to_all(copies, SEQ, split_axis=0, concat_axis=0, tiled=True)
+    totals = jnp.sum(totals, axis=(0, 1)) * (1.0 / (lax.axis_size(BATCH) * Q * GROUPS))
+    return join(result)[None], totals[:H], totals[H:]
 
 
 def solution(mesh):
     torus = Mesh(mesh.devices.reshape(4, 2, 4, 8), ("batch_0", "batch_1", "seq_0", "seq_1"))
     return jax.shard_map(
-        body,
+        inner,
         mesh=torus,
         in_specs=(
             P(BATCH, SEQ, None),

time: 190 us -> 186 us (0.979)
  waiting for transfers between devices: 59.5 us -> 85.6 us
  Pallas kernels: 52.1 us -> 26.3 us
  starting transfers between devices: 65.6 us -> 43.3 us
  blocking collectives: 0 us -> 17.4 us
    all_to_all x3, waiting for transfers between devices: 0.01 us -> 50.9 us  [the longest x1 27.3 us: inner(): lax.all_to_all(summed, SEQ, split_axis=0, concat_axis=0, tiled=True)]
    all_to_all x0 -> x1, blocking collectives: none -> 17.4 us  [inner(): lax.all_to_all(copies, SEQ, split_axis=0, concat_axis=0, tiled=True)]
    all_to_all x3, starting transfers between devices: 32.9 us -> 19 us  [the longest x1 8.73 us: inner(): rows = lax.all_to_all(packed, SEQ, split_axis=0, concat_axis=0, tiled=True)]
    ppermute x8 -> x3, waiting for transfers between devices: 18.4 us -> 5.58 us  [swapped(): return lax.ppermute(x, axis, [(i, i ^ bit) for i in range(size)])]
    ppermute x12, waiting for transfers between devices: 41.1 us -> 29.1 us  [shifted(): return lax.ppermute(x, axis, [(i, (i + by) % size) for i in range(size)])]
    ppermute x8 -> x3, starting transfers between devices: 16.1 us -> 4.6 us  [swapped(): return lax.ppermute(x, axis, [(i, i ^ bit) for i in range(size)])]
    pallas_call x1, Pallas kernels: 21.5 us -> 10.2 us  [series(): pl.pallas_call(series_kernel, in_specs=[SMEM, full(rows.shape), HBM, HBM,...]
    pallas_call x3, Pallas kernels: 15.7 us -> 7.31 us  [the longest x1 2.98 us: pack(): pl.pallas_call(pack_kernel, in_specs=[full(step.shape), full(forget.shape...]
  transfers between devices with their start and end apart: 23 -> 18, of which waited for: 14 -> 13; matrix products, arithmetic and copies ran while one was open for 4% -> 2% of each run, Pallas kernels for 22% -> 8%
where the time goes in v2:
time: 186 us; the launch traced here: 185 us
  waiting for transfers between devices  85.6 us (46%)
  starting transfers between devices  43.3 us (23%)
  Pallas kernels  26.3 us (14%)
  blocking collectives  17.4 us (9%)
  local copies, waits for them, and re-layouts  7.92 us (4%)
  other arithmetic  3.35 us (2%)
    ppermute x12, waiting for transfers between devices, shifted(): return lax.ppermute(x, axis, [(i, (i + by) % size) for i in range(size)])  29.1 us
    all_to_all x1, waiting for transfers between devices, inner(): lax.all_to_all(summed, SEQ, split_axis=0, concat_axis=0, tiled=True)  27.3 us
    all_to_all x1, waiting for transfers between devices, inner(): rows = lax.all_to_all(packed, SEQ, split_axis=0, concat_axis=0, tiled=True)  23.7 us
    ppermute x12, starting transfers between devices, shifted(): return lax.ppermute(x, axis, [(i, (i + by) % size) for i in range(size)])  19.7 us
    all_to_all x1, blocking collectives, inner(): lax.all_to_all(copies, SEQ, split_axis=0, concat_axis=0, tiled=True)  17.4 us
    pallas_call x1, Pallas kernels, series(): pl.pallas_call(series_kernel, in_specs=[SMEM, full(rows.shape), HBM, HBM,...  10.2 us
    pallas_call x1, Pallas kernels, rates(): pl.pallas_call(rate_kernel, in_specs=[SMEM, full(rows.shape), full(summed...  8.77 us
    all_to_all x1, starting transfers between devices, inner(): rows = lax.all_to_all(packed, SEQ, split_axis=0, concat_axis=0, tiled=True)  8.73 us
  transfers between devices with their start and end apart: 18, of which 13 were waited for; matrix products, arithmetic and copies ran while one was open for 2% of the time, Pallas kernels for 8%

profile of v2, /device:TPU:32, one launch (start us, length us, event | category | flops | bytes accessed | tf_op | source)
XLA Modules:
  0.0 184.9 jit_solution(691463629827290067)
XLA Ops:
  1.4 1.9 %collective-permute-start = (bf16[256,128]{1,0:T(8,128)(2,1)S(1)}, bf16[256,128]{1,0:T(8,128)(2,1)S(1)}, u32[]{:S(2)}, u32[]{:S(2)}) collective-permute-start(bf16[256,128]{1,0:T(8,128)(2,1)S(1)} %pad_maximum_fusion), channel_id=1, source_target_pairs={{0,7},{1,0},{2,1},{3,2},{4,3},{5,4},{6,5},{7,6},{8,15},{9,8},{10,9... | collective-permute-start | bytes 196616 | tf_op jit(solution)/shard_map/ppermute | solution.py:28
  3.5 3.0 %pack.1 = bf16[32,136,128]{2,1,0:T(8,128)(2,1)} custom-call(f32[64,128]{1,0:T(8,128)} %bitcast.41, f32[1,128]{1,0:T(1,128)} %forget_ref.1, bf16[128,4096]{1,0:T(8,128)(2,1)} %bitcast.33), custom_call_target="tpu_custom_call" | custom-call | tf_op jit(solution)/shard_map/pack/pallas_call | solution.py:68
  7.2 3.9 %collective-permute-start.1 = (bf16[256,128]{1,0:T(8,128)(2,1)S(1)}, bf16[256,128]{1,0:T(8,128)(2,1)S(1)}, u32[]{:S(2)}, u32[]{:S(2)}) collective-permute-start(bf16[256,128]{1,0:T(8,128)(2,1)S(1)} %collective-permute-done), channel_id=1, source_target_pairs={{0,7},{1,0},{2,1},{3,2},{4,3},{5,4},{6,5},{7,6},{8,15},{9,8},{10,9... | collective-permute-start | bytes 196616 | tf_op jit(solution)/shard_map/ppermute | solution.py:28
  13.0 3.2 %collective-permute-start.2 = (bf16[256,128]{1,0:T(8,128)(2,1)S(1)}, bf16[256,128]{1,0:T(8,128)(2,1)S(1)}, u32[]{:S(2)}, u32[]{:S(2)}) collective-permute-start(bf16[256,128]{1,0:T(8,128)(2,1)S(1)} %collective-permute-done.1), channel_id=1, source_target_pairs={{0,7},{1,0},{2,1},{3,2},{4,3},{5,4},{6,5},{7,6},{8,15},{9,8},{10,9... | collective-permute-start | bytes 196616 | tf_op jit(solution)/shard_map/ppermute | solution.py:28
  18.1 3.6 %collective-permute-start.7 = (bf16[128,128]{1,0:T(8,128)(2,1)S(1)}, bf16[128,128]{1,0:T(8,128)(2,1)S(1)}, u32[]{:S(2)}, u32[]{:S(2)}) collective-permute-start(bf16[128,128]{1,0:T(8,128)(2,1)S(1)} %slice.32), channel_id=1, source_target_pairs={{0,7},{1,0},{2,1},{3,2},{4,3},{5,4},{6,5},{7,6},{8,15},{9,8},{10,9... | collective-permute-start | bytes 98312 | tf_op jit(solution)/shard_map/ppermute | solution.py:28
  23.3 3.9 %collective-permute-done.6 = bf16[128,128]{1,0:T(8,128)(2,1)S(1)} collective-permute-done((bf16[128,128]{1,0:T(8,128)(2,1)S(1)}, bf16[128,128]{1,0:T(8,128)(2,1)S(1)}, u32[]{:S(2)}, u32[]{:S(2)}) %collective-permute-start.6) | collective-permute-done | bytes 32800 | tf_op jit(solution)/shard_map/ppermute | solution.py:28
  29.7 8.7 %all-to-all-start = ((bf16[32,136,128]{2,1,0:T(8,128)(2,1)}), bf16[32,136,128]{2,1,0:T(8,128)(2,1)S(1)}, u32[]{:S(2)}, u32[]{:S(2)}) async-start(bf16[32,136,128]{2,1,0:T(8,128)(2,1)} %pack.1), calls=%async_computation | async-start | bytes 2228224 | tf_op jit(solution)/shard_map/all_to_all | solution.py:369
  38.5 2.2 %split.1 = bf16[32,128,128]{2,1,0:T(8,128)(2,1)} custom-call(bf16[128,4096]{1,0:T(8,128)(2,1)} %bitcast.34), custom_call_target="tpu_custom_call" | custom-call | tf_op jit(solution)/shard_map/split/pallas_call | solution.py:89
  40.7 23.7 %all-to-all-done.in_ref = bf16[32,136,128]{2,1,0:T(8,128)(2,1)S(1)} async-done(((bf16[32,136,128]{2,1,0:T(8,128)(2,1)}), bf16[32,136,128]{2,1,0:T(8,128)(2,1)S(1)}, u32[]{:S(2)}, u32[]{:S(2)}) %all-to-all-start) | async-done | bytes 1114144 | tf_op jit(solution)/shard_map/all_to_all | solution.py:369
  64.3 5.2 %all-to-all-start.2 = ((bf16[32,128,128]{2,1,0:T(8,128)(2,1)}), bf16[32,128,128]{2,1,0:T(8,128)(2,1)S(1)}, u32[]{:S(2)}, u32[]{:S(2)}) async-start(bf16[32,128,128]{2,1,0:T(8,128)(2,1)} %split.1), calls=%async_computation.2 | async-start | bytes 2097152 | tf_op jit(solution)/shard_map/all_to_all | solution.py:370
  71.1 1.8 collective-permute-start.8
  72.9 19.0 %collective-permute-done.9.p2 = bf16[8,256,128]{2,1,0:T(8,128)(2,1)S(1)} collective-permute-done((bf16[8,256,128]{2,1,0:T(8,128)(2,1)}, bf16[8,256,128]{2,1,0:T(8,128)(2,1)S(1)}, u32[]{:S(2)}, u32[]{:S(2)}) %collective-permute-start.9) | collective-permute-done | bytes 524320 | tf_op jit(solution)/shard_map/ppermute | solution.py:28
  92.9 2.5 %collective-permute-start.11 = (bf16[4,256,128]{2,1,0:T(8,128)(2,1)S(1)}, bf16[4,256,128]{2,1,0:T(8,128)(2,1)S(1)}, u32[]{:S(2)}, u32[]{:S(2)}) collective-permute-start(bf16[4,256,128]{2,1,0:T(8,128)(2,1)S(1)} %slice.34), channel_id=1, source_target_pairs={{0,24},{8,0},{16,8},{24,16},{1,25},{9,1},{17,9},{25,17},{2,26},{10... | collective-permute-start | bytes 786440 | tf_op jit(solution)/shard_map/ppermute | solution.py:28
  96.9 2.8 %collective-permute-done.10.p3 = bf16[4,256,128]{2,1,0:T(8,128)(2,1)} collective-permute-done((bf16[4,256,128]{2,1,0:T(8,128)(2,1)S(1)}, bf16[4,256,128]{2,1,0:T(8,128)(2,1)}, u32[]{:S(2)}, u32[]{:S(2)}) %collective-permute-start.10) | collective-permute-done | bytes 262176 | tf_op jit(solution)/shard_map/ppermute | solution.py:28
  100.4 10.2 %series.1.sum_ref = bf16[32,128,128]{2,1,0:T(8,128)(2,1)} custom-call(s32[2]{0:T(128)} %pad_add_fusion.pos_ref, bf16[32,136,128]{2,1,0:T(8,128)(2,1)} %copy-done.1, bf16[8,256,128]{2,1,0:T(8,128)(2,1)} %bitcast_dynamic-update-slice_fusion.p0, bf16[8,256,128]{2,1,0:T(8,128)(2,1)} %copy-done.4, bf16[8,256,128]{2,1,0:T(8,128)(2,1)} %copy-done.3, ...), custom_call_target="tpu_custom_call" | custom-call | flops 3000000000 | bytes 5000000 | tf_op jit(solution)/shard_map/series/pallas_call | solution.py:305
  111.6 8.8 %rates.1 = f32[8,128]{1,0:T(8,128)} custom-call(s32[2]{0:T(128)} %pad_add_fusion.pos_ref, bf16[32,136,128]{2,1,0:T(8,128)(2,1)} %copy-done.1, bf16[32,128,128]{2,1,0:T(8,128)(2,1)} %series.1.sum_ref, bf16[32,128,128]{2,1,0:T(8,128)(2,1)} %copy-done.2, bf16[8,256,128]{2,1,0:T(8,128)(2,1)} %bitcast_dynamic-update-slice_fusion.p0, ...), custom_call_target="tpu_custom_call" | custom-call | flops 2000000000 | bytes 5000000 | tf_op jit(solution)/shard_map/rates/pallas_call | solution.py:323
  120.4 1.6 collective-permute-start.12
  121.9 2.3 %collective-permute-done.12 = f32[8,128]{1,0:T(8,128)S(1)} collective-permute-done((f32[8,128]{1,0:T(8,128)}, f32[8,128]{1,0:T(8,128)S(1)}, u32[]{:S(2)}, u32[]{:S(2)}) %collective-permute-start.12) | collective-permute-done | bytes 4128 | tf_op jit(solution)/shard_map/ppermute | solution.py:33
  125.0 3.0 %collective-permute-start.13 = (f32[8,128]{1,0:T(8,128)S(1)}, f32[8,128]{1,0:T(8,128)S(1)}, u32[]{:S(2)}, u32[]{:S(2)}) collective-permute-start(f32[8,128]{1,0:T(8,128)S(1)} %add.18), channel_id=1, source_target_pairs={{0,128},{64,192},{128,0},{192,64},{1,129},{65,193},{129,1},{193,65... | collective-permute-start | bytes 12296 | tf_op jit(solution)/shard_map/ppermute | solution.py:33
  128.0 2.1 %collective-permute-done.13 = f32[8,128]{1,0:T(8,128)S(1)} collective-permute-done((f32[8,128]{1,0:T(8,128)S(1)}, f32[8,128]{1,0:T(8,128)S(1)}, u32[]{:S(2)}, u32[]{:S(2)}) %collective-permute-start.13) | collective-permute-done | bytes 4128 | tf_op jit(solution)/shard_map/ppermute | solution.py:33
  131.3 17.4 %all_to_all.20 = f32[32,1,128]{2,1,0:T(1,128)S(1)} all-to-all(f32[32,1,128]{2,1,0:T(1,128)S(1)} %broadcast_in_dim.11), channel_id=1, replica_groups=mesh['batch_0'=4,'batch_1'=2,'seq_0'=4,'seq_1'=8] {'seq_0','seq_1'}, dimensions={0} | all-to-all | bytes 32768 | tf_op jit(solution)/shard_map/all_to_all | solution.py:380
  148.7 5.0 %all-to-all-start.1 = ((bf16[32,128,128]{2,1,0:T(8,128)(2,1)}), bf16[32,128,128]{2,1,0:T(8,128)(2,1)S(1)}, u32[]{:S(2)}, u32[]{:S(2)}) async-start(bf16[32,128,128]{2,1,0:T(8,128)(2,1)} %series.1.sum_ref), calls=%async_computation.1 | async-start | bytes 2097152 | tf_op jit(solution)/shard_map/all_to_all | solution.py:372
  154.3 27.3 %all-to-all-done.1.in_ref = bf16[32,128,128]{2,1,0:T(8,128)(2,1)S(1)} async-done(((bf16[32,128,128]{2,1,0:T(8,128)(2,1)}), bf16[32,128,128]{2,1,0:T(8,128)(2,1)S(1)}, u32[]{:S(2)}, u32[]{:S(2)}) %all-to-all-start.1) | async-done | bytes 1048608 | tf_op jit(solution)/shard_map/all_to_all | solution.py:372
  182.5 2.2 %join.1 = bf16[128,4096]{1,0:T(8,128)(2,1)} custom-call(bf16[32,128,128]{2,1,0:T(8,128)(2,1)} %copy-done), custom_call_target="tpu_custom_call" | custom-call | tf_op jit(solution)/shard_map/join/pallas_call | solution.py:110
  (64 shorter events, 18.8 us)
Async XLA Ops:
  1.4 5.1 %copy-start.6 = (bf16[1,128,128]{2,1,0:T(8,128)(2,1)S(1)}, bf16[1,128,128]{2,1,0:T(8,128)(2,1)}, u32[]{:S(2)}) copy-start(bf16[1,128,128]{2,1,0:T(8,128)(2,1)} %param.10) | copy-start | bytes 98308
  1.4 5.7 %collective-permute-start = (bf16[256,128]{1,0:T(8,128)(2,1)S(1)}, bf16[256,128]{1,0:T(8,128)(2,1)S(1)}, u32[]{:S(2)}, u32[]{:S(2)}) collective-permute-start(bf16[256,128]{1,0:T(8,128)(2,1)S(1)} %pad_maximum_fusion), channel_id=1, source_target_pairs={{0,7},{1,0},{2,1},{3,2},{4,3},{5,4},{6,5},{7,6},{8,15},{9,8},{10,9... | collective-permute-start | bytes 196616 | tf_op jit(solution)/shard_map/ppermute | solution.py:28
  3.3 7.8 %collective-permute-start.3 = (bf16[256,128]{1,0:T(8,128)(2,1)S(1)}, bf16[256,128]{1,0:T(8,128)(2,1)S(1)}, u32[]{:S(2)}, u32[]{:S(2)}) collective-permute-start(bf16[256,128]{1,0:T(8,128)(2,1)S(1)} %pad_maximum_fusion), channel_id=1, source_target_pairs={{0,1},{1,2},{2,3},{3,4},{4,5},{5,6},{6,7},{7,0},{8,9},{9,10},{10,1... | collective-permute-start | bytes 196616 | tf_op jit(solution)/shard_map/ppermute | solution.py:28
  7.2 5.8 %collective-permute-start.1 = (bf16[256,128]{1,0:T(8,128)(2,1)S(1)}, bf16[256,128]{1,0:T(8,128)(2,1)S(1)}, u32[]{:S(2)}, u32[]{:S(2)}) collective-permute-start(bf16[256,128]{1,0:T(8,128)(2,1)S(1)} %collective-permute-done), channel_id=1, source_target_pairs={{0,7},{1,0},{2,1},{3,2},{4,3},{5,4},{6,5},{7,6},{8,15},{9,8},{10,9... | collective-permute-start | bytes 196616 | tf_op jit(solution)/shard_map/ppermute | solution.py:28
  11.1 5.5 %collective-permute-start.4 = (bf16[256,128]{1,0:T(8,128)(2,1)S(1)}, bf16[256,128]{1,0:T(8,128)(2,1)S(1)}, u32[]{:S(2)}, u32[]{:S(2)}) collective-permute-start(bf16[256,128]{1,0:T(8,128)(2,1)S(1)} %collective-permute-done.3), channel_id=1, source_target_pairs={{0,1},{1,2},{2,3},{3,4},{4,5},{5,6},{6,7},{7,0},{8,9},{9,10},{10,1... | collective-permute-start | bytes 196616 | tf_op jit(solution)/shard_map/ppermute | solution.py:28
  13.0 5.1 %collective-permute-start.2 = (bf16[256,128]{1,0:T(8,128)(2,1)S(1)}, bf16[256,128]{1,0:T(8,128)(2,1)S(1)}, u32[]{:S(2)}, u32[]{:S(2)}) collective-permute-start(bf16[256,128]{1,0:T(8,128)(2,1)S(1)} %collective-permute-done.1), channel_id=1, source_target_pairs={{0,7},{1,0},{2,1},{3,2},{4,3},{5,4},{6,5},{7,6},{8,15},{9,8},{10,9... | collective-permute-start | bytes 196616 | tf_op jit(solution)/shard_map/ppermute | solution.py:28
  16.6 5.5 %collective-permute-start.5 = (bf16[256,128]{1,0:T(8,128)(2,1)S(1)}, bf16[256,128]{1,0:T(8,128)(2,1)S(1)}, u32[]{:S(2)}, u32[]{:S(2)}) collective-permute-start(bf16[256,128]{1,0:T(8,128)(2,1)S(1)} %collective-permute-done.4), channel_id=1, source_target_pairs={{0,1},{1,2},{2,3},{3,4},{4,5},{5,6},{6,7},{7,0},{8,9},{9,10},{10,1... | collective-permute-start | bytes 196616 | tf_op jit(solution)/shard_map/ppermute | solution.py:28
  18.1 5.2 %collective-permute-start.7 = (bf16[128,128]{1,0:T(8,128)(2,1)S(1)}, bf16[128,128]{1,0:T(8,128)(2,1)S(1)}, u32[]{:S(2)}, u32[]{:S(2)}) collective-permute-start(bf16[128,128]{1,0:T(8,128)(2,1)S(1)} %slice.32), channel_id=1, source_target_pairs={{0,7},{1,0},{2,1},{3,2},{4,3},{5,4},{6,5},{7,6},{8,15},{9,8},{10,9... | collective-permute-start | bytes 98312 | tf_op jit(solution)/shard_map/ppermute | solution.py:28
  22.1 5.1 %collective-permute-start.6 = (bf16[128,128]{1,0:T(8,128)(2,1)S(1)}, bf16[128,128]{1,0:T(8,128)(2,1)S(1)}, u32[]{:S(2)}, u32[]{:S(2)}) collective-permute-start(bf16[128,128]{1,0:T(8,128)(2,1)S(1)} %slice.31), channel_id=1, source_target_pairs={{0,1},{1,2},{2,3},{3,4},{4,5},{5,6},{6,7},{7,0},{8,9},{9,10},{10,1... | collective-permute-start | bytes 98312 | tf_op jit(solution)/shard_map/ppermute | solution.py:28
  29.7 34.6 %all-to-all-start = ((bf16[32,136,128]{2,1,0:T(8,128)(2,1)}), bf16[32,136,128]{2,1,0:T(8,128)(2,1)S(1)}, u32[]{:S(2)}, u32[]{:S(2)}) async-start(bf16[32,136,128]{2,1,0:T(8,128)(2,1)} %pack.1), calls=%async_computation | async-start | bytes 2228224 | tf_op jit(solution)/shard_map/all_to_all | solution.py:369
  40.6 54.8 %copy-start.7 = (f32[64]{0:T(128)S(1)}, f32[64]{0:T(128)}, u32[]{:S(2)}) copy-start(f32[64]{0:T(128)} %param.15) | copy-start | bytes 772
  40.7 54.8 %copy-start.8 = (f32[64]{0:T(128)S(1)}, f32[64]{0:T(128)}, u32[]{:S(2)}) copy-start(f32[64]{0:T(128)} %param.14) | copy-start | bytes 772
  64.3 27.6 %copy-start.1 = (bf16[32,136,128]{2,1,0:T(8,128)(2,1)}, bf16[32,136,128]{2,1,0:T(8,128)(2,1)S(1)}, u32[]{:S(2)}) copy-start(bf16[32,136,128]{2,1,0:T(8,128)(2,1)S(1)} %all-to-all-done.in_ref) | copy-start | bytes 3342340
  64.3 46.3 %all-to-all-start.2 = ((bf16[32,128,128]{2,1,0:T(8,128)(2,1)}), bf16[32,128,128]{2,1,0:T(8,128)(2,1)S(1)}, u32[]{:S(2)}, u32[]{:S(2)}) async-start(bf16[32,128,128]{2,1,0:T(8,128)(2,1)} %split.1), calls=%async_computation.2 | async-start | bytes 2097152 | tf_op jit(solution)/shard_map/all_to_all | solution.py:370
  69.6 22.3 %collective-permute-start.9 = (bf16[8,256,128]{2,1,0:T(8,128)(2,1)}, bf16[8,256,128]{2,1,0:T(8,128)(2,1)S(1)}, u32[]{:S(2)}, u32[]{:S(2)}) collective-permute-start(bf16[8,256,128]{2,1,0:T(8,128)(2,1)} %bitcast_dynamic-update-slice_fusion.p0), channel_id=1, source_target_pairs={{0,8},{8,16},{16,24},{24,0},{1,9},{9,17},{17,25},{25,1},{2,10},{10... | collective-permute-start | bytes 1572872 | tf_op jit(solution)/shard_map/ppermute | solution.py:28
  71.1 21.8 %collective-permute-start.8 = (bf16[8,256,128]{2,1,0:T(8,128)(2,1)}, bf16[8,256,128]{2,1,0:T(8,128)(2,1)S(1)}, u32[]{:S(2)}, u32[]{:S(2)}) collective-permute-start(bf16[8,256,128]{2,1,0:T(8,128)(2,1)} %bitcast_dynamic-update-slice_fusion.p0), channel_id=1, source_target_pairs={{0,24},{8,0},{16,8},{24,16},{1,25},{9,1},{17,9},{25,17},{2,26},{10... | collective-permute-start | bytes 1572872 | tf_op jit(solution)/shard_map/ppermute | solution.py:28
  91.9 7.8 %copy-start.3 = (bf16[8,256,128]{2,1,0:T(8,128)(2,1)}, bf16[8,256,128]{2,1,0:T(8,128)(2,1)S(1)}, u32[]{:S(2)}) copy-start(bf16[8,256,128]{2,1,0:T(8,128)(2,1)S(1)} %collective-permute-done.9.p2) | copy-start | bytes 1572868
  91.9 7.8 %collective-permute-start.10 = (bf16[4,256,128]{2,1,0:T(8,128)(2,1)S(1)}, bf16[4,256,128]{2,1,0:T(8,128)(2,1)}, u32[]{:S(2)}, u32[]{:S(2)}) collective-permute-start(bf16[4,256,128]{2,1,0:T(8,128)(2,1)S(1)} %slice.33), channel_id=1, source_target_pairs={{0,8},{8,16},{16,24},{24,0},{1,9},{9,17},{17,25},{25,1},{2,10},{10... | collective-permute-start | bytes 786440 | tf_op jit(solution)/shard_map/ppermute | solution.py:28
  92.9 6.7 %copy-start.4 = (bf16[8,256,128]{2,1,0:T(8,128)(2,1)}, bf16[8,256,128]{2,1,0:T(8,128)(2,1)S(1)}, u32[]{:S(2)}) copy-start(bf16[8,256,128]{2,1,0:T(8,128)(2,1)S(1)} %collective-permute-done.8.p1) | copy-start | bytes 1572868
  92.9 6.7 %collective-permute-start.11 = (bf16[4,256,128]{2,1,0:T(8,128)(2,1)S(1)}, bf16[4,256,128]{2,1,0:T(8,128)(2,1)S(1)}, u32[]{:S(2)}, u32[]{:S(2)}) collective-permute-start(bf16[4,256,128]{2,1,0:T(8,128)(2,1)S(1)} %slice.34), channel_id=1, source_target_pairs={{0,24},{8,0},{16,8},{24,16},{1,25},{9,1},{17,9},{25,17},{2,26},{10... | collective-permute-start | bytes 786440 | tf_op jit(solution)/shard_map/ppermute | solution.py:28
  120.4 3.9 %collective-permute-start.12 = (f32[8,128]{1,0:T(8,128)}, f32[8,128]{1,0:T(8,128)S(1)}, u32[]{:S(2)}, u32[]{:S(2)}) collective-permute-start(f32[8,128]{1,0:T(8,128)} %rates.1), channel_id=1, source_target_pairs={{0,64},{64,0},{128,192},{192,128},{1,65},{65,1},{129,193},{193,129... | collective-permute-start | bytes 12296 | tf_op jit(solution)/shard_map/ppermute | solution.py:33
  125.0 5.1 %collective-permute-start.13 = (f32[8,128]{1,0:T(8,128)S(1)}, f32[8,128]{1,0:T(8,128)S(1)}, u32[]{:S(2)}, u32[]{:S(2)}) collective-permute-start(f32[8,128]{1,0:T(8,128)S(1)} %add.18), channel_id=1, source_target_pairs={{0,128},{64,192},{128,0},{192,64},{1,129},{65,193},{129,1},{193,65... | collective-permute-start | bytes 12296 | tf_op jit(solution)/shard_map/ppermute | solution.py:33
  130.1 1.2 collective-permute-start.14
  148.7 32.9 %all-to-all-start.1 = ((bf16[32,128,128]{2,1,0:T(8,128)(2,1)}), bf16[32,128,128]{2,1,0:T(8,128)(2,1)S(1)}, u32[]{:S(2)}, u32[]{:S(2)}) async-start(bf16[32,128,128]{2,1,0:T(8,128)(2,1)} %series.1.sum_ref), calls=%async_computation.1 | async-start | bytes 2097152 | tf_op jit(solution)/shard_map/all_to_all | solution.py:372
  (4 other events, 7.8 us)

commit v3 on v2

--- a/solution.py
+++ b/solution.py
@@ -75,25 +75,31 @@
     )(step, forget, cot)
 
 
-def split_kernel(in_ref, out_ref, sem):
-    copies = [
-        pltpu.make_async_copy(in_ref.at[:, pl.ds(j * 128, 128)], out_ref.at[j], sem) for j in range(GROUPS)
-    ]
+def split_kernel(pos_ref, in_ref, *refs):
+    outs, sem = refs[:NZ], refs[NZ]
+    my_y, my_z = pos_ref[0], pos_ref[1]
+    copies = []
+    for dz in range(NZ):
+        for dy in range(NY):
+            owner = ((my_y + dy) % NY) * NZ + (my_z + dz) % NZ
+            start = pl.multiple_of(owner * 128, 128)
+            copies.append(pltpu.make_async_copy(in_ref.at[:, pl.ds(start, 128)], outs[dz].at[dy], sem))
     for c in copies:
         c.start()
     for c in copies:
         c.wait()
 
 
-def split(x):
+def split(pos, x):
+    shape = (NY, Q, 128)
     return pl.pallas_call(
         split_kernel,
-        in_specs=[HBM],
-        out_specs=full((GROUPS, Q, 128)),
-        out_shape=jax.ShapeDtypeStruct((GROUPS, Q, 128), BF16),
+        in_specs=[SMEM, HBM],
+        out_specs=[full(shape)] * NZ,
+        out_shape=[jax.ShapeDtypeStruct(shape, BF16)] * NZ,
         scratch_shapes=[pltpu.SemaphoreType.DMA],
         name="split",
-    )(x)
+    )(pos, x)
 
 
 def join_kernel(in_ref, out_ref, sem):
@@ -233,7 +239,7 @@
         lax.fori_loop(0, GROUPS // UNROLL, step, 0)
 
 
-def rate_kernel(pos_ref, in_ref, sum_ref, fixed_ref, p0, p1, p2, p3, p4, rate_ref, out_ref, maps_ref, mat_ref, turn_ref, e_ref, g_ref, s_ref, m_ref, back_ref, acc_ref, sem):
+def tangent_kernel(pos_ref, in_ref, sum_ref, p0, p1, p2, p3, p4, rate_ref, out_ref, maps_ref, mat_ref, turn_ref, e_ref, g_ref, s_ref, m_ref, back_ref, sem):
     fetch_maps(pos_ref, (p0, p1, p2, p3, p4), maps_ref, sem)
     consts = constants()
 
@@ -244,7 +250,6 @@
 
     lax.fori_loop(0, GROUPS // PREP, prep, 0)
     back_ref[...] = jnp.zeros((N, 256), F32)
-    acc_ref[...] = jnp.zeros((2, 8, 128), F32)
 
     def step(i, _):
         groups = [GROUPS - 1 - (i * PAIRED + j) for j in range(PAIRED)]
@@ -265,25 +270,47 @@
         back_ref[:, :128] = back
         back_ref[:, 128:] = tangent
         mixed = [dot(mat_ref[c], jnp.concatenate([x, b], axis=0)) for c, x, b in zip(groups, turned, states)]
-        rate_sum, skip_sum = acc_ref[0], acc_ref[1]
-        for c, v, r in zip(groups, values, mixed):
+        for c, r in zip(groups, mixed):
+            out_ref[c] = g_ref[c] * (s_ref[c] * r[:, :128] - r[:, 128:])
+        return 0
+
+    lax.fori_loop(0, GROUPS // PAIRED, step, 0)
+
+
+def dots_kernel(pos_ref, sum_ref, change_ref, *refs):
+    lines, planes = refs[:NZ], refs[NZ : NZ + NY - 1]
+    out_ref, fixed_ref, sem = refs[NZ + NY - 1 :]
+    my_y, my_z = pos_ref[0], pos_ref[1]
+    copies = []
+    for dz in range(NZ):
+        for dy in range(NY):
+            source = lines[dz].at[0] if dy == 0 else planes[dy - 1].at[dz]
+            place = ((my_y + NY - dy) % NY) * NZ + (my_z + NZ - dz) % NZ
+            copies.append(pltpu.make_async_copy(source, fixed_ref.at[place], sem))
+    for c in copies:
+        c.start()
+    for c in copies:
+        c.wait()
+
+    def step(i, sums):
+        rate_sum, skip_sum = sums
+        for j in range(4):
+            c = i * 4 + j
             z = fixed_ref[c].astype(F32)
-            change = g_ref[c] * (r[:, 128:] - s_ref[c] * r[:, :128])
-            rate_sum = rate_sum + jnp.sum((z * change).reshape(16, 8, 128), axis=0)
+            v = sum_ref[c].astype(F32)
+            rate_sum = rate_sum + jnp.sum((z * change_ref[c]).reshape(16, 8, 128), axis=0)
             skip_sum = skip_sum + jnp.sum((z * v).reshape(16, 8, 128), axis=0)
-        acc_ref[0] = rate_sum
-        acc_ref[1] = skip_sum
-        return 0
-
-    lax.fori_loop(0, GROUPS // PAIRED, step, 0)
+        return rate_sum, skip_sum
+
+    zero = jnp.zeros((8, 128), F32)
+    sums = lax.fori_loop(0, GROUPS // 4, step, (zero, zero))
     lane = lax.broadcasted_iota(jnp.int32, (8, 128), 1)
-    first = (pos_ref[0] * NZ + pos_ref[1]) * 2
-    result = jnp.zeros((8, 128), F32)
+    first = (my_y * NZ + my_z) * 2
+    result = zero
     for kind in range(2):
         for head in range(2):
-            picked = jnp.where((lane >= HEAD) if head else (lane < HEAD), acc_ref[kind], 0.0)
+            picked = jnp.where((lane >= HEAD) if head else (lane < HEAD), sums[kind], 0.0)
             value = jnp.sum(picked, keepdims=True)
-            value = -value if kind == 0 else value
             result = jnp.where(lane == kind * H + first + head, value, result)
     out_ref[...] = result
 
@@ -319,33 +346,41 @@
     )(pos, rows, *pieces, rate)
 
 
-def rates(pos, rows, summed, fixed, pieces, rate):
-    return pl.pallas_call(
-        rate_kernel,
-        in_specs=[SMEM, full(rows.shape), full(summed.shape), full(fixed.shape), HBM, HBM, HBM, HBM, HBM, full(rate.shape)],
+def tangents(pos, rows, summed, pieces, rate):
+    return pl.pallas_call(
+        tangent_kernel,
+        in_specs=[SMEM, full(rows.shape), full(summed.shape), HBM, HBM, HBM, HBM, HBM, full(rate.shape)],
+        out_specs=full((GROUPS, Q, 128)),
+        out_shape=jax.ShapeDtypeStruct((GROUPS, Q, 128), F32),
+        scratch_shapes=[*table_scratch(True), pltpu.VMEM((N, 256), F32), pltpu.SemaphoreType.DMA],
+        name="tangents",
+        cost_estimate=pl.CostEstimate(flops=2_000_000_000, transcendentals=1_000_000, bytes_accessed=5_000_000),
+    )(pos, rows, summed, *pieces, rate)
+
+
+def dots(pos, summed, change, lines, planes):
+    return pl.pallas_call(
+        dots_kernel,
+        in_specs=[SMEM, full(summed.shape), full(change.shape), *[HBM] * (NZ + NY - 1)],
         out_specs=full((8, 128)),
         out_shape=jax.ShapeDtypeStruct((8, 128), F32),
-        scratch_shapes=[
-            *table_scratch(True),
-            pltpu.VMEM((N, 256), F32),
-            pltpu.VMEM((2, 8, 128), F32),
-            pltpu.SemaphoreType.DMA,
-        ],
-        name="rates",
-        cost_estimate=pl.CostEstimate(flops=2_000_000_000, transcendentals=1_000_000, bytes_accessed=5_000_000),
-    )(pos, rows, summed, fixed, *pieces, rate)
+        scratch_shapes=[pltpu.VMEM((GROUPS, Q, 128), BF16), pltpu.SemaphoreType.DMA],
+        name="dots",
+        cost_estimate=pl.CostEstimate(flops=2_000_000, transcendentals=0, bytes_accessed=4_000_000),
+    )(pos, summed, change, *lines, *planes)
+
+
+def near(by, size):
+    return by if by <= size // 2 else by - size
 
 
 def gather_line(input_map, output_map):
-    own = jnp.concatenate([input_map, output_map], axis=0)
-    up, down = [own], [own]
-    for _ in range(3):
-        up.append(shifted(up[-1], "seq_1", 1))
-        down.append(shifted(down[-1], "seq_1", -1))
-    far_first = shifted(up[3][:N], "seq_1", 1)
-    far_second = shifted(down[3][N:], "seq_1", -1)
-    far = jnp.concatenate([far_first, far_second], axis=0)
-    return jnp.stack([own, down[1], down[2], down[3], far, up[3], up[2], up[1]])
+    own = jnp.concatenate([input_map, output_map], axis=0)[None]
+    last, after = shifted(own, "seq_1", 1), shifted(own, "seq_1", -1)
+    far_last = shifted(jnp.concatenate([last, own]), "seq_1", 2)
+    far_after = shifted(jnp.concatenate([own, after]), "seq_1", -2)
+    far = shifted(own, "seq_1", 4)
+    return jnp.concatenate([own, after, far_after, far, far_last, last])
 
 
 def gather_plane(line):
@@ -367,10 +402,16 @@
     packed, line = lax.optimization_barrier((pack(cotangent[0], step_size[0], forget), line))
     pieces = gather_plane(line)
     rows = lax.all_to_all(packed, SEQ, split_axis=0, concat_axis=0, tiled=True)
-    fixed = lax.all_to_all(split(fixed_point[0]), SEQ, split_axis=0, concat_axis=0, tiled=True)
+    own_lines = split(pos, fixed_point[0])
+    lines = [own_lines[0]] + [shifted(own_lines[d], "seq_1", near(d, NZ)) for d in range(1, NZ)]
     summed = series(pos, rows, pieces, rate)
     result = lax.all_to_all(summed, SEQ, split_axis=0, concat_axis=0, tiled=True)
-    totals = rates(pos, rows, summed, fixed, pieces, rate)
+    change = tangents(pos, rows, summed, pieces, rate)
+    planes = []
+    for d in range(1, NY):
+        stacked = jnp.concatenate([x[d : d + 1] for x in lines])
+        planes.append(shifted(stacked, "seq_0", near(d, NY)))
+    totals = dots(pos, summed, change, lines, planes)
     for axis in BATCH:
         bit = 1
         while bit < lax.axis_size(axis):

time: 186 us -> 201 us (1.081)
  starting transfers between devices: 43.3 us -> 57.6 us
  waiting for transfers between devices: 85.6 us -> 71.3 us
  blocking collectives: 17.4 us -> 23.4 us
  Pallas kernels: 26.3 us -> 31.4 us
  local copies, waits for them, and re-layouts: 7.92 us -> 11.6 us
    all_to_all x1, waiting for transfers between devices: 23.7 us -> 0.01 us  [inner(): rows = lax.all_to_all(packed, SEQ, split_axis=0, concat_axis=0, tiled=True)]
    ppermute x12 -> x19, starting transfers between devices: 19.7 us -> 38.7 us  [shifted(): return lax.ppermute(x, axis, [(i, (i + by) % size) for i in range(size)])]
    ppermute x12 -> x19, waiting for transfers between devices: 29.1 us -> 38.4 us  [shifted(): return lax.ppermute(x, axis, [(i, (i + by) % size) for i in range(size)])]
    all_to_all x1, blocking collectives: 17.4 us -> 23.4 us  [inner(): lax.all_to_all(copies, SEQ, split_axis=0, concat_axis=0, tiled=True)]
    all_to_all x1 -> x0, starting transfers between devices: 5.25 us -> none  [inner(): lax.all_to_all(split(fixed_point[0]), SEQ, split_axis=0, concat_axis=0, t...]
    pallas_call x2 -> x3, Pallas kernels: 10.9 us -> 16.1 us  [the longest x1 8.95 us: tangents(): pl.pallas_call(tangent_kernel, in_specs=[SMEM, full(rows.shape), full(sum...]
    unnamed x25 -> x47, local copies, waits for them, and re-layouts: 5.84 us -> 9.51 us
  transfers between devices with their start and end apart: 18 -> 24, of which waited for: 13 -> 11; matrix products, arithmetic and copies ran while one was open for 2% -> 4% of each run, Pallas kernels for 8% -> 13%
where the time goes in v3:
time: 201 us; the launch traced here: 199 us
  waiting for transfers between devices  71.3 us (35%)
  starting transfers between devices  57.6 us (29%)
  Pallas kernels  31.4 us (16%)
  blocking collectives  23.4 us (12%)
  local copies, waits for them, and re-layouts  11.6 us (6%)
  other arithmetic  2.96 us (1%)
    ppermute x19, starting transfers between devices, shifted(): return lax.ppermute(x, axis, [(i, (i + by) % size) for i in range(size)])  38.7 us
    ppermute x19, waiting for transfers between devices, shifted(): return lax.ppermute(x, axis, [(i, (i + by) % size) for i in range(size)])  38.4 us
    all_to_all x1, waiting for transfers between devices, inner(): lax.all_to_all(summed, SEQ, split_axis=0, concat_axis=0, tiled=True)  27.3 us
    all_to_all x1, blocking collectives, inner(): lax.all_to_all(copies, SEQ, split_axis=0, concat_axis=0, tiled=True)  23.4 us
    pallas_call x1, Pallas kernels, series(): pl.pallas_call(series_kernel, in_specs=[SMEM, full(rows.shape), HBM, HBM,...  10.2 us
    unnamed x47, local copies, waits for them, and re-layouts  9.51 us
    all_to_all x1, starting transfers between devices, inner(): rows = lax.all_to_all(packed, SEQ, split_axis=0, concat_axis=0, tiled=True)  9.36 us
    pallas_call x1, Pallas kernels, tangents(): pl.pallas_call(tangent_kernel, in_specs=[SMEM, full(rows.shape), full(sum...  8.95 us
  transfers between devices with their start and end apart: 24, of which 11 were waited for; matrix products, arithmetic and copies ran while one was open for 4% of the time, Pallas kernels for 13%

profile of v3, /device:TPU:32, one launch (start us, length us, event | category | flops | bytes accessed | tf_op | source)
XLA Modules:
  0.0 199.4 jit_solution(7931265314213259195)
XLA Ops:
  3.4 6.3 %collective-permute-start.2 = (bf16[1,256,128]{2,1,0:T(8,128)(2,1)S(1)}, bf16[1,256,128]{2,1,0:T(8,128)(2,1)S(1)}, u32[]{:S(2)}, u32[]{:S(2)}) collective-permute-start(bf16[1,256,128]{2,1,0:T(8,128)(2,1)S(1)} %maximum_bitcast_fusion), channel_id=1, source_target_pairs={{0,4},{1,5},{2,6},{3,7},{4,0},{5,1},{6,2},{7,3},{8,12},{9,13},{10,... | collective-permute-start | bytes 196616 | tf_op jit(solution)/shard_map/ppermute | solution.py:28
  9.8 2.8 %collective-permute-start.1 = (bf16[2,256,128]{2,1,0:T(8,128)(2,1)S(1)}, bf16[2,256,128]{2,1,0:T(8,128)(2,1)S(1)}, u32[]{:S(2)}, u32[]{:S(2)}) collective-permute-start(bf16[2,256,128]{2,1,0:T(8,128)(2,1)S(1)} %get-tuple-element.48), channel_id=1, source_target_pairs={{0,6},{1,7},{2,0},{3,1},{4,2},{5,3},{6,4},{7,5},{8,14},{9,15},{10,... | collective-permute-start | bytes 393224 | tf_op jit(solution)/shard_map/ppermute | solution.py:28
  13.4 3.0 %pack.1 = bf16[32,136,128]{2,1,0:T(8,128)(2,1)} custom-call(f32[64,128]{1,0:T(8,128)} %bitcast.27, f32[1,128]{1,0:T(1,128)} %forget_ref.1, bf16[128,4096]{1,0:T(8,128)(2,1)} %bitcast.19), custom_call_target="tpu_custom_call" | custom-call | tf_op jit(solution)/shard_map/pack/pallas_call | solution.py:68
  18.7 5.7 %collective-permute-done.4 = bf16[2,256,128]{2,1,0:T(8,128)(2,1)S(1)} collective-permute-done((bf16[2,256,128]{2,1,0:T(8,128)(2,1)S(1)}, bf16[2,256,128]{2,1,0:T(8,128)(2,1)S(1)}, u32[]{:S(2)}, u32[]{:S(2)}) %collective-permute-start.4) | collective-permute-done | bytes 131104 | tf_op jit(solution)/shard_map/ppermute | solution.py:28
  24.4 9.4 %all-to-all-start = ((bf16[32,136,128]{2,1,0:T(8,128)(2,1)}), bf16[32,136,128]{2,1,0:T(8,128)(2,1)S(1)}, u32[]{:S(2)}, u32[]{:S(2)}) async-start(bf16[32,136,128]{2,1,0:T(8,128)(2,1)} %pack.1), calls=%async_computation | async-start | bytes 2228224 | tf_op jit(solution)/shard_map/all_to_all | solution.py:404
  34.4 2.8 %split.1 = (bf16[4,128,128]{2,1,0:T(8,128)(2,1)}, bf16[4,128,128]{2,1,0:T(8,128)(2,1)}, bf16[4,128,128]{2,1,0:T(8,128)(2,1)}, bf16[4,128,128]{2,1,0:T(8,128)(2,1...) custom-call(s32[2]{0:T(128)} %pad_add_fusion.pos_ref, ...), custom_call_target="tpu_custom_call" | custom-call | tf_op jit(solution)/shard_map/split/pallas_call | solution.py:95
  38.8 3.6 %collective-permute-start.10 = (bf16[4,128,128]{2,1,0:T(8,128)(2,1)}, bf16[4,128,128]{2,1,0:T(8,128)(2,1)S(1)}, u32[]{:S(2)}, u32[]{:S(2)}) collective-permute-start(bf16[4,128,128]{2,1,0:T(8,128)(2,1)} %get-tuple-element.17), channel_id=1, source_target_pairs={{0,2},{1,3},{2,4},{3,5},{4,6},{5,7},{6,0},{7,1},{8,10},{9,11},{10,... | collective-permute-start | bytes 393224 | tf_op jit(solution)/shard_map/ppermute | solution.py:28
  42.9 3.3 %collective-permute-start.12 = (bf16[4,128,128]{2,1,0:T(8,128)(2,1)}, bf16[4,128,128]{2,1,0:T(8,128)(2,1)S(1)}, u32[]{:S(2)}, u32[]{:S(2)}) collective-permute-start(bf16[4,128,128]{2,1,0:T(8,128)(2,1)} %get-tuple-element.19), channel_id=1, source_target_pairs={{0,4},{1,5},{2,6},{3,7},{4,0},{5,1},{6,2},{7,3},{8,12},{9,13},{10,... | collective-permute-start | bytes 393224 | tf_op jit(solution)/shard_map/ppermute | solution.py:28
  49.9 12.7 %collective-permute-done.9.refs_1_ = bf16[4,128,128]{2,1,0:T(8,128)(2,1)S(1)} collective-permute-done((bf16[4,128,128]{2,1,0:T(8,128)(2,1)}, bf16[4,128,128]{2,1,0:T(8,128)(2,1)S(1)}, u32[]{:S(2)}, u32[]{:S(2)}) %collective-permute-start.9) | collective-permute-done | bytes 131104 | tf_op jit(solution)/shard_map/ppermute | solution.py:28
  62.5 3.8 %collective-permute-start.14 = (bf16[4,128,128]{2,1,0:T(8,128)(2,1)}, bf16[4,128,128]{2,1,0:T(8,128)(2,1)S(1)}, u32[]{:S(2)}, u32[]{:S(2)}) collective-permute-start(bf16[4,128,128]{2,1,0:T(8,128)(2,1)} %get-tuple-element.21), channel_id=1, source_target_pairs={{0,6},{1,7},{2,0},{3,1},{4,2},{5,3},{6,4},{7,5},{8,14},{9,15},{10,... | collective-permute-start | bytes 393224 | tf_op jit(solution)/shard_map/ppermute | solution.py:28
  67.0 4.1 %collective-permute-done.10.refs_2_ = bf16[4,128,128]{2,1,0:T(8,128)(2,1)S(1)} collective-permute-done((bf16[4,128,128]{2,1,0:T(8,128)(2,1)}, bf16[4,128,128]{2,1,0:T(8,128)(2,1)S(1)}, u32[]{:S(2)}, u32[]{:S(2)}) %collective-permute-start.10) | collective-permute-done | bytes 131104 | tf_op jit(solution)/shard_map/ppermute | solution.py:28
  71.8 2.8 %collective-permute-start.5 = (bf16[8,256,128]{2,1,0:T(8,128)(2,1)S(1)}, bf16[8,256,128]{2,1,0:T(8,128)(2,1)S(1)}, u32[]{:S(2)}, u32[]{:S(2)}) collective-permute-start(bf16[8,256,128]{2,1,0:T(8,128)(2,1)S(1)} %constant_dynamic-update-slice_fusion.p0), channel_id=1, source_target_pairs={{0,24},{8,0},{16,8},{24,16},{1,25},{9,1},{17,9},{25,17},{2,26},{10... | collective-permute-start | bytes 1572872 | tf_op jit(solution)/shard_map/ppermute | solution.py:28
  74.5 4.8 %collective-permute-done.11.refs_3_ = bf16[4,128,128]{2,1,0:T(8,128)(2,1)S(1)} collective-permute-done((bf16[4,128,128]{2,1,0:T(8,128)(2,1)}, bf16[4,128,128]{2,1,0:T(8,128)(2,1)S(1)}, u32[]{:S(2)}, u32[]{:S(2)}) %collective-permute-start.11) | collective-permute-done | bytes 131104 | tf_op jit(solution)/shard_map/ppermute | solution.py:28
  84.8 7.6 %collective-permute-done.6.p2 = bf16[8,256,128]{2,1,0:T(8,128)(2,1)S(1)} collective-permute-done((bf16[8,256,128]{2,1,0:T(8,128)(2,1)S(1)}, bf16[8,256,128]{2,1,0:T(8,128)(2,1)S(1)}, u32[]{:S(2)}, u32[]{:S(2)}) %collective-permute-start.6) | collective-permute-done | bytes 524320 | tf_op jit(solution)/shard_map/ppermute | solution.py:28
  92.6 3.4 %collective-permute-start.8 = (bf16[4,256,128]{2,1,0:T(8,128)(2,1)S(1)}, bf16[4,256,128]{2,1,0:T(8,128)(2,1)}, u32[]{:S(2)}, u32[]{:S(2)}) collective-permute-start(bf16[4,256,128]{2,1,0:T(8,128)(2,1)S(1)} %slice.120), channel_id=1, source_target_pairs={{0,24},{8,0},{16,8},{24,16},{1,25},{9,1},{17,9},{25,17},{2,26},{10... | collective-permute-start | bytes 786440 | tf_op jit(solution)/shard_map/ppermute | solution.py:28
  103.9 10.2 %series.1.sum_ref = bf16[32,128,128]{2,1,0:T(8,128)(2,1)} custom-call(s32[2]{0:T(128)} %pad_add_fusion.pos_ref, bf16[32,136,128]{2,1,0:T(8,128)(2,1)} %copy-done.1, bf16[8,256,128]{2,1,0:T(8,128)(2,1)} %copy-done.14, bf16[8,256,128]{2,1,0:T(8,128)(2,1)} %copy-done.12, bf16[8,256,128]{2,1,0:T(8,128)(2,1)} %copy-done.13, bf16[4,256,128]{2,1,0:T(8,128)(2,1)} %copy-done.17, ...), custom_call_target="tpu_custom_call" | custom-call | flops 3000000000 | bytes 5000000 | tf_op jit(solution)/shard_map/series/pallas_call | solution.py:332
  114.1 9.0 %tangents.1.change_ref = f32[32,128,128]{2,1,0:T(8,128)} custom-call(s32[2]{0:T(128)} %pad_add_fusion.pos_ref, bf16[32,136,128]{2,1,0:T(8,128)(2,1)} %copy-done.1, bf16[32,128,128]{2,1,0:T(8,128)(2,1)} %series.1.sum_ref, bf16[8,256,128]{2,1,0:T(8,128)(2,1)} %copy-done.14, bf16[8,256,128]{2,1,0:T(8,128)(2,1)} %copy-done.12, bf16[8,256,128]{2,1,0:T(8,128)(2,1)} %copy-done.13, ...), custom_call_target="tpu_custom_call" | custom-call | flops 2000000000 | bytes 5000000 | tf_op jit(solution)/shard_map/tangents/pallas_call | solution.py:350
  124.6 4.3 %dots.1 = f32[8,128]{1,0:T(8,128)} custom-call(s32[2]{0:T(128)} %pad_add_fusion.pos_ref, bf16[32,128,128]{2,1,0:T(8,128)(2,1)} %series.1.sum_ref, f32[32,128,128]{2,1,0:T(8,128)} %tangents.1.change_ref, bf16[4,128,128]{2,1,0:T(8,128)(2,1)} %get-tuple-element.15.refs_0_, bf16[4,128,128]{2,1,0:T(8,128)(2,1)} %copy-done.2, bf16[4,128,128]{2,1,0:T(8,128)(2,1)} %copy-done.3, ...), custom_call_target="tpu_custom_call" | custom-call | flops 2000000 | bytes 4000000 | tf_op jit(solution)/shard_map/dots/pallas_call | solution.py:362
  130.5 2.3 %collective-permute-done.19 = f32[8,128]{1,0:T(8,128)S(1)} collective-permute-done((f32[8,128]{1,0:T(8,128)}, f32[8,128]{1,0:T(8,128)S(1)}, u32[]{:S(2)}, u32[]{:S(2)}) %collective-permute-start.19) | collective-permute-done | bytes 4128 | tf_op jit(solution)/shard_map/ppermute | solution.py:33
  133.5 3.0 %collective-permute-start.20 = (f32[8,128]{1,0:T(8,128)S(1)}, f32[8,128]{1,0:T(8,128)S(1)}, u32[]{:S(2)}, u32[]{:S(2)}) collective-permute-start(f32[8,128]{1,0:T(8,128)S(1)} %add.18), channel_id=1, source_target_pairs={{0,128},{64,192},{128,0},{192,64},{1,129},{65,193},{129,1},{193,65... | collective-permute-start | bytes 12296 | tf_op jit(solution)/shard_map/ppermute | solution.py:33
  139.8 23.4 %all_to_all.15 = f32[32,1,128]{2,1,0:T(1,128)S(1)} all-to-all(f32[32,1,128]{2,1,0:T(1,128)S(1)} %broadcast_in_dim.15), channel_id=1, replica_groups=mesh['batch_0'=4,'batch_1'=2,'seq_0'=4,'seq_1'=8] {'seq_0','seq_1'}, dimensions={0} | all-to-all | bytes 32768 | tf_op jit(solution)/shard_map/all_to_all | solution.py:421
  163.2 5.0 %all-to-all-start.1 = ((bf16[32,128,128]{2,1,0:T(8,128)(2,1)}), bf16[32,128,128]{2,1,0:T(8,128)(2,1)S(1)}, u32[]{:S(2)}, u32[]{:S(2)}) async-start(bf16[32,128,128]{2,1,0:T(8,128)(2,1)} %series.1.sum_ref), calls=%async_computation.1 | async-start | bytes 2097152 | tf_op jit(solution)/shard_map/all_to_all | solution.py:408
  168.8 27.3 %all-to-all-done.1.in_ref = bf16[32,128,128]{2,1,0:T(8,128)(2,1)S(1)} async-done(((bf16[32,128,128]{2,1,0:T(8,128)(2,1)}), bf16[32,128,128]{2,1,0:T(8,128)(2,1)S(1)}, u32[]{:S(2)}, u32[]{:S(2)}) %all-to-all-start.1) | async-done | bytes 1048608 | tf_op jit(solution)/shard_map/all_to_all | solution.py:408
  197.1 2.2 %join.1 = bf16[128,4096]{1,0:T(8,128)(2,1)} custom-call(bf16[32,128,128]{2,1,0:T(8,128)(2,1)} %copy-done), custom_call_target="tpu_custom_call" | custom-call | tf_op jit(solution)/shard_map/join/pallas_call | solution.py:116
  (98 shorter events, 35.7 us)
Async XLA Ops:
  1.4 8.3 %collective-permute-start = (bf16[1,256,128]{2,1,0:T(8,128)(2,1)S(1)}, bf16[1,256,128]{2,1,0:T(8,128)(2,1)S(1)}, u32[]{:S(2)}, u32[]{:S(2)}) collective-permute-start(bf16[1,256,128]{2,1,0:T(8,128)(2,1)S(1)} %maximum_bitcast_fusion), channel_id=1, source_target_pairs={{0,7},{1,0},{2,1},{3,2},{4,3},{5,4},{6,5},{7,6},{8,15},{9,8},{10,9... | collective-permute-start | bytes 196616 | tf_op jit(solution)/shard_map/ppermute | solution.py:28
  3.2 6.5 %collective-permute-start.3 = (bf16[1,256,128]{2,1,0:T(8,128)(2,1)S(1)}, bf16[1,256,128]{2,1,0:T(8,128)(2,1)S(1)}, u32[]{:S(2)}, u32[]{:S(2)}) collective-permute-start(bf16[1,256,128]{2,1,0:T(8,128)(2,1)S(1)} %maximum_bitcast_fusion), channel_id=1, source_target_pairs={{0,1},{1,2},{2,3},{3,4},{4,5},{5,6},{6,7},{7,0},{8,9},{9,10},{10,1... | collective-permute-start | bytes 196616 | tf_op jit(solution)/shard_map/ppermute | solution.py:28
  3.4 15.2 %collective-permute-start.2 = (bf16[1,256,128]{2,1,0:T(8,128)(2,1)S(1)}, bf16[1,256,128]{2,1,0:T(8,128)(2,1)S(1)}, u32[]{:S(2)}, u32[]{:S(2)}) collective-permute-start(bf16[1,256,128]{2,1,0:T(8,128)(2,1)S(1)} %maximum_bitcast_fusion), channel_id=1, source_target_pairs={{0,4},{1,5},{2,6},{3,7},{4,0},{5,1},{6,2},{7,3},{8,12},{9,13},{10,... | collective-permute-start | bytes 196616 | tf_op jit(solution)/shard_map/ppermute | solution.py:28
  9.8 8.9 %collective-permute-start.1 = (bf16[2,256,128]{2,1,0:T(8,128)(2,1)S(1)}, bf16[2,256,128]{2,1,0:T(8,128)(2,1)S(1)}, u32[]{:S(2)}, u32[]{:S(2)}) collective-permute-start(bf16[2,256,128]{2,1,0:T(8,128)(2,1)S(1)} %get-tuple-element.48), channel_id=1, source_target_pairs={{0,6},{1,7},{2,0},{3,1},{4,2},{5,3},{6,4},{7,5},{8,14},{9,15},{10,... | collective-permute-start | bytes 393224 | tf_op jit(solution)/shard_map/ppermute | solution.py:28
  16.4 7.9 %collective-permute-start.4 = (bf16[2,256,128]{2,1,0:T(8,128)(2,1)S(1)}, bf16[2,256,128]{2,1,0:T(8,128)(2,1)S(1)}, u32[]{:S(2)}, u32[]{:S(2)}) collective-permute-start(bf16[2,256,128]{2,1,0:T(8,128)(2,1)S(1)} %get-tuple-element.47), channel_id=1, source_target_pairs={{0,2},{1,3},{2,4},{3,5},{4,6},{5,7},{6,0},{7,1},{8,10},{9,11},{10,... | collective-permute-start | bytes 393224 | tf_op jit(solution)/shard_map/ppermute | solution.py:28
  24.4 78.5 %all-to-all-start = ((bf16[32,136,128]{2,1,0:T(8,128)(2,1)}), bf16[32,136,128]{2,1,0:T(8,128)(2,1)S(1)}, u32[]{:S(2)}, u32[]{:S(2)}) async-start(bf16[32,136,128]{2,1,0:T(8,128)(2,1)} %pack.1), calls=%async_computation | async-start | bytes 2228224 | tf_op jit(solution)/shard_map/all_to_all | solution.py:404
  37.2 25.3 %collective-permute-start.9 = (bf16[4,128,128]{2,1,0:T(8,128)(2,1)}, bf16[4,128,128]{2,1,0:T(8,128)(2,1)S(1)}, u32[]{:S(2)}, u32[]{:S(2)}) collective-permute-start(bf16[4,128,128]{2,1,0:T(8,128)(2,1)} %get-tuple-element.16), channel_id=1, source_target_pairs={{0,1},{1,2},{2,3},{3,4},{4,5},{5,6},{6,7},{7,0},{8,9},{9,10},{10,1... | collective-permute-start | bytes 393224 | tf_op jit(solution)/shard_map/ppermute | solution.py:28
  38.8 32.3 %collective-permute-start.10 = (bf16[4,128,128]{2,1,0:T(8,128)(2,1)}, bf16[4,128,128]{2,1,0:T(8,128)(2,1)S(1)}, u32[]{:S(2)}, u32[]{:S(2)}) collective-permute-start(bf16[4,128,128]{2,1,0:T(8,128)(2,1)} %get-tuple-element.17), channel_id=1, source_target_pairs={{0,2},{1,3},{2,4},{3,5},{4,6},{5,7},{6,0},{7,1},{8,10},{9,11},{10,... | collective-permute-start | bytes 393224 | tf_op jit(solution)/shard_map/ppermute | solution.py:28
  42.4 37.0 %collective-permute-start.11 = (bf16[4,128,128]{2,1,0:T(8,128)(2,1)}, bf16[4,128,128]{2,1,0:T(8,128)(2,1)S(1)}, u32[]{:S(2)}, u32[]{:S(2)}) collective-permute-start(bf16[4,128,128]{2,1,0:T(8,128)(2,1)} %get-tuple-element.18), channel_id=1, source_target_pairs={{0,3},{1,4},{2,5},{3,6},{4,7},{5,0},{6,1},{7,2},{8,11},{9,12},{10,... | collective-permute-start | bytes 393224 | tf_op jit(solution)/shard_map/ppermute | solution.py:28
  42.9 38.5 %collective-permute-start.12 = (bf16[4,128,128]{2,1,0:T(8,128)(2,1)}, bf16[4,128,128]{2,1,0:T(8,128)(2,1)S(1)}, u32[]{:S(2)}, u32[]{:S(2)}) collective-permute-start(bf16[4,128,128]{2,1,0:T(8,128)(2,1)} %get-tuple-element.19), channel_id=1, source_target_pairs={{0,4},{1,5},{2,6},{3,7},{4,0},{5,1},{6,2},{7,3},{8,12},{9,13},{10,... | collective-permute-start | bytes 393224 | tf_op jit(solution)/shard_map/ppermute | solution.py:28
  46.2 38.0 %collective-permute-start.13 = (bf16[4,128,128]{2,1,0:T(8,128)(2,1)}, bf16[4,128,128]{2,1,0:T(8,128)(2,1)S(1)}, u32[]{:S(2)}, u32[]{:S(2)}) collective-permute-start(bf16[4,128,128]{2,1,0:T(8,128)(2,1)} %get-tuple-element.20), channel_id=1, source_target_pairs={{0,5},{1,6},{2,7},{3,0},{4,1},{5,2},{6,3},{7,4},{8,13},{9,14},{10,... | collective-permute-start | bytes 393224 | tf_op jit(solution)/shard_map/ppermute | solution.py:28
  62.5 33.5 %collective-permute-start.14 = (bf16[4,128,128]{2,1,0:T(8,128)(2,1)}, bf16[4,128,128]{2,1,0:T(8,128)(2,1)S(1)}, u32[]{:S(2)}, u32[]{:S(2)}) collective-permute-start(bf16[4,128,128]{2,1,0:T(8,128)(2,1)} %get-tuple-element.21), channel_id=1, source_target_pairs={{0,6},{1,7},{2,0},{3,1},{4,2},{5,3},{6,4},{7,5},{8,14},{9,15},{10,... | collective-permute-start | bytes 393224 | tf_op jit(solution)/shard_map/ppermute | solution.py:28
  71.8 20.8 %collective-permute-start.5 = (bf16[8,256,128]{2,1,0:T(8,128)(2,1)S(1)}, bf16[8,256,128]{2,1,0:T(8,128)(2,1)S(1)}, u32[]{:S(2)}, u32[]{:S(2)}) collective-permute-start(bf16[8,256,128]{2,1,0:T(8,128)(2,1)S(1)} %constant_dynamic-update-slice_fusion.p0), channel_id=1, source_target_pairs={{0,24},{8,0},{16,8},{24,16},{1,25},{9,1},{17,9},{25,17},{2,26},{10... | collective-permute-start | bytes 1572872 | tf_op jit(solution)/shard_map/ppermute | solution.py:28
  79.4 13.0 %collective-permute-start.6 = (bf16[8,256,128]{2,1,0:T(8,128)(2,1)S(1)}, bf16[8,256,128]{2,1,0:T(8,128)(2,1)S(1)}, u32[]{:S(2)}, u32[]{:S(2)}) collective-permute-start(bf16[8,256,128]{2,1,0:T(8,128)(2,1)S(1)} %constant_dynamic-update-slice_fusion.p0), channel_id=1, source_target_pairs={{0,8},{8,16},{16,24},{24,0},{1,9},{9,17},{17,25},{25,1},{2,10},{10... | collective-permute-start | bytes 1572872 | tf_op jit(solution)/shard_map/ppermute | solution.py:28
  81.4 15.2 %collective-permute-start.15 = (bf16[4,128,128]{2,1,0:T(8,128)(2,1)}, bf16[4,128,128]{2,1,0:T(8,128)(2,1)S(1)}, u32[]{:S(2)}, u32[]{:S(2)}) collective-permute-start(bf16[4,128,128]{2,1,0:T(8,128)(2,1)} %get-tuple-element.22), channel_id=1, source_target_pairs={{0,7},{1,0},{2,1},{3,2},{4,3},{5,4},{6,5},{7,6},{8,15},{9,8},{10,9... | collective-permute-start | bytes 393224 | tf_op jit(solution)/shard_map/ppermute | solution.py:28
  92.4 9.7 %collective-permute-start.7 = (bf16[4,256,128]{2,1,0:T(8,128)(2,1)S(1)}, bf16[4,256,128]{2,1,0:T(8,128)(2,1)S(1)}, u32[]{:S(2)}, u32[]{:S(2)}) collective-permute-start(bf16[4,256,128]{2,1,0:T(8,128)(2,1)S(1)} %slice.119), channel_id=1, source_target_pairs={{0,8},{8,16},{16,24},{24,0},{1,9},{9,17},{17,25},{25,1},{2,10},{10... | collective-permute-start | bytes 786440 | tf_op jit(solution)/shard_map/ppermute | solution.py:28
  92.6 10.3 %collective-permute-start.8 = (bf16[4,256,128]{2,1,0:T(8,128)(2,1)S(1)}, bf16[4,256,128]{2,1,0:T(8,128)(2,1)}, u32[]{:S(2)}, u32[]{:S(2)}) collective-permute-start(bf16[4,256,128]{2,1,0:T(8,128)(2,1)S(1)} %slice.120), channel_id=1, source_target_pairs={{0,24},{8,0},{16,8},{24,16},{1,25},{9,1},{17,9},{25,17},{2,26},{10... | collective-permute-start | bytes 786440 | tf_op jit(solution)/shard_map/ppermute | solution.py:28
  97.3 25.8 %collective-permute-start.16 = (bf16[8,128,128]{2,1,0:T(8,128)(2,1)}, bf16[8,128,128]{2,1,0:T(8,128)(2,1)S(1)}, u32[]{:S(2)}, u32[]{:S(2)}) collective-permute-start(bf16[8,128,128]{2,1,0:T(8,128)(2,1)} %get-tuple-element.25), channel_id=1, source_target_pairs={{0,8},{8,16},{16,24},{24,0},{1,9},{9,17},{17,25},{25,1},{2,10},{10... | collective-permute-start | bytes 786440 | tf_op jit(solution)/shard_map/ppermute | solution.py:28
  97.4 25.8 %collective-permute-start.17 = (bf16[8,128,128]{2,1,0:T(8,128)(2,1)}, bf16[8,128,128]{2,1,0:T(8,128)(2,1)S(1)}, u32[]{:S(2)}, u32[]{:S(2)}) collective-permute-start(bf16[8,128,128]{2,1,0:T(8,128)(2,1)} %get-tuple-element.24), channel_id=1, source_target_pairs={{0,16},{8,24},{16,0},{24,8},{1,17},{9,25},{17,1},{25,9},{2,18},{10... | collective-permute-start | bytes 786440 | tf_op jit(solution)/shard_map/ppermute | solution.py:28
  99.0 24.2 %collective-permute-start.18 = (bf16[8,128,128]{2,1,0:T(8,128)(2,1)S(1)}, bf16[8,128,128]{2,1,0:T(8,128)(2,1)S(1)}, u32[]{:S(2)}, u32[]{:S(2)}) collective-permute-start(bf16[8,128,128]{2,1,0:T(8,128)(2,1)S(1)} %get-tuple-element.23), channel_id=1, source_target_pairs={{0,24},{8,0},{16,8},{24,16},{1,25},{9,1},{17,9},{25,17},{2,26},{10... | collective-permute-start | bytes 786440 | tf_op jit(solution)/shard_map/ppermute | solution.py:28
  128.9 3.9 %collective-permute-start.19 = (f32[8,128]{1,0:T(8,128)}, f32[8,128]{1,0:T(8,128)S(1)}, u32[]{:S(2)}, u32[]{:S(2)}) collective-permute-start(f32[8,128]{1,0:T(8,128)} %dots.1), channel_id=1, source_target_pairs={{0,64},{64,0},{128,192},{192,128},{1,65},{65,1},{129,193},{193,129... | collective-permute-start | bytes 12296 | tf_op jit(solution)/shard_map/ppermute | solution.py:33
  133.5 5.1 %collective-permute-start.20 = (f32[8,128]{1,0:T(8,128)S(1)}, f32[8,128]{1,0:T(8,128)S(1)}, u32[]{:S(2)}, u32[]{:S(2)}) collective-permute-start(f32[8,128]{1,0:T(8,128)S(1)} %add.18), channel_id=1, source_target_pairs={{0,128},{64,192},{128,0},{192,64},{1,129},{65,193},{129,1},{193,65... | collective-permute-start | bytes 12296 | tf_op jit(solution)/shard_map/ppermute | solution.py:33
  138.6 1.2 collective-permute-start.21
  163.2 32.9 %all-to-all-start.1 = ((bf16[32,128,128]{2,1,0:T(8,128)(2,1)}), bf16[32,128,128]{2,1,0:T(8,128)(2,1)S(1)}, u32[]{:S(2)}, u32[]{:S(2)}) async-start(bf16[32,128,128]{2,1,0:T(8,128)(2,1)} %series.1.sum_ref), calls=%async_computation.1 | async-start | bytes 2097152 | tf_op jit(solution)/shard_map/all_to_all | solution.py:408
  (18 other events, 315.0 us)

commit v4 on v2

--- a/solution.py
+++ b/solution.py
@@ -337,15 +337,12 @@
 
 
 def gather_line(input_map, output_map):
-    own = jnp.concatenate([input_map, output_map], axis=0)
-    up, down = [own], [own]
-    for _ in range(3):
-        up.append(shifted(up[-1], "seq_1", 1))
-        down.append(shifted(down[-1], "seq_1", -1))
-    far_first = shifted(up[3][:N], "seq_1", 1)
-    far_second = shifted(down[3][N:], "seq_1", -1)
-    far = jnp.concatenate([far_first, far_second], axis=0)
-    return jnp.stack([own, down[1], down[2], down[3], far, up[3], up[2], up[1]])
+    own = jnp.concatenate([input_map, output_map], axis=0)[None]
+    last, after = shifted(own, "seq_1", 1), shifted(own, "seq_1", -1)
+    far_last = shifted(jnp.concatenate([last, own]), "seq_1", 2)
+    far_after = shifted(jnp.concatenate([own, after]), "seq_1", -2)
+    far = shifted(own, "seq_1", 4)
+    return jnp.concatenate([own, after, far_after, far, far_last, last])
 
 
 def gather_plane(line):
@@ -364,7 +361,7 @@
     rate = jnp.repeat(own, HEAD, axis=1)
 
     line = gather_line(input_map[0], output_map[0])
-    packed, line = lax.optimization_barrier((pack(cotangent[0], step_size[0], forget), line))
+    packed = pack(cotangent[0], step_size[0], forget)
     pieces = gather_plane(line)
     rows = lax.all_to_all(packed, SEQ, split_axis=0, concat_axis=0, tiled=True)
     fixed = lax.all_to_all(split(fixed_point[0]), SEQ, split_axis=0, concat_axis=0, tiled=True)

time: 186 us -> 194 us (1.043)
  waiting for transfers between devices: 85.6 us -> 96.8 us
  local copies, waits for them, and re-layouts: 7.92 us -> 4.13 us
  other arithmetic: 3.35 us -> 1.39 us
    ppermute x12 -> x9, waiting for transfers between devices: 29.1 us -> 36.3 us  [shifted(): return lax.ppermute(x, axis, [(i, (i + by) % size) for i in range(size)])]
    all_to_all x1, waiting for transfers between devices: 23.7 us -> 27.7 us  [inner(): rows = lax.all_to_all(packed, SEQ, split_axis=0, concat_axis=0, tiled=True)]
    unnamed x25 -> x26, local copies, waits for them, and re-layouts: 5.84 us -> 2.73 us
    all_to_all x1, starting transfers between devices: 8.73 us -> 11.4 us  [inner(): rows = lax.all_to_all(packed, SEQ, split_axis=0, concat_axis=0, tiled=True)]
    ppermute x12 -> x9, starting transfers between devices: 19.7 us -> 19 us  [shifted(): return lax.ppermute(x, axis, [(i, (i + by) % size) for i in range(size)])]
  transfers between devices with their start and end apart: 18 -> 15, of which waited for: 13 -> 11; matrix products, arithmetic and copies ran while one was open for 2% -> 1% of each run, Pallas kernels for 8% -> 6%
where the time goes in v4:
time: 194 us; the launch traced here: 193 us
  waiting for transfers between devices  96.8 us (50%)
  starting transfers between devices  45.2 us (23%)
  Pallas kernels  26.3 us (14%)
  blocking collectives  17.8 us (9%)
  local copies, waits for them, and re-layouts  4.13 us (2%)
    ppermute x9, waiting for transfers between devices, shifted(): return lax.ppermute(x, axis, [(i, (i + by) % size) for i in range(size)])  36.3 us
    all_to_all x1, waiting for transfers between devices, inner(): rows = lax.all_to_all(packed, SEQ, split_axis=0, concat_axis=0, tiled=True)  27.7 us
    all_to_all x1, waiting for transfers between devices, inner(): lax.all_to_all(summed, SEQ, split_axis=0, concat_axis=0, tiled=True)  27.3 us
    ppermute x9, starting transfers between devices, shifted(): return lax.ppermute(x, axis, [(i, (i + by) % size) for i in range(size)])  19 us
    all_to_all x1, blocking collectives, inner(): lax.all_to_all(copies, SEQ, split_axis=0, concat_axis=0, tiled=True)  17.8 us
    all_to_all x1, starting transfers between devices, inner(): rows = lax.all_to_all(packed, SEQ, split_axis=0, concat_axis=0, tiled=True)  11.4 us
    pallas_call x1, Pallas kernels, series(): pl.pallas_call(series_kernel, in_specs=[SMEM, full(rows.shape), HBM, HBM,...  10.2 us
    pallas_call x1, Pallas kernels, rates(): pl.pallas_call(rate_kernel, in_specs=[SMEM, full(rows.shape), full(summed...  8.77 us
  transfers between devices with their start and end apart: 15, of which 11 were waited for; matrix products, arithmetic and copies ran while one was open for 1% of the time, Pallas kernels for 6%

profile of v4, /device:TPU:32, one launch (start us, length us, event | category | flops | bytes accessed | tf_op | source)
XLA Modules:
  0.0 192.7 jit_solution(11200986805665761950)
XLA Ops:
  0.6 3.0 %pack.1 = bf16[32,136,128]{2,1,0:T(8,128)(2,1)} custom-call(f32[64,128]{1,0:T(8,128)} %bitcast.27, f32[1,128]{1,0:T(1,128)} %forget_ref.1, bf16[128,4096]{1,0:T(8,128)(2,1)} %bitcast.19), custom_call_target="tpu_custom_call" | custom-call | tf_op jit(solution)/shard_map/pack/pallas_call | solution.py:68
  3.6 11.4 %all-to-all-start = ((bf16[32,136,128]{2,1,0:T(8,128)(2,1)}), bf16[32,136,128]{2,1,0:T(8,128)(2,1)S(1)}, u32[]{:S(2)}, u32[]{:S(2)}) async-start(bf16[32,136,128]{2,1,0:T(8,128)(2,1)} %pack.1), calls=%async_computation | async-start | bytes 2228224 | tf_op jit(solution)/shard_map/all_to_all | solution.py:366
  15.0 2.2 %split.1 = bf16[32,128,128]{2,1,0:T(8,128)(2,1)} custom-call(bf16[128,4096]{1,0:T(8,128)(2,1)} %bitcast.20), custom_call_target="tpu_custom_call" | custom-call | tf_op jit(solution)/shard_map/split/pallas_call | solution.py:89
  17.2 27.7 %all-to-all-done.in_ref = bf16[32,136,128]{2,1,0:T(8,128)(2,1)S(1)} async-done(((bf16[32,136,128]{2,1,0:T(8,128)(2,1)}), bf16[32,136,128]{2,1,0:T(8,128)(2,1)S(1)}, u32[]{:S(2)}, u32[]{:S(2)}) %all-to-all-start) | async-done | bytes 1114144 | tf_op jit(solution)/shard_map/all_to_all | solution.py:366
  44.8 5.3 %all-to-all-start.2 = ((bf16[32,128,128]{2,1,0:T(8,128)(2,1)}), bf16[32,128,128]{2,1,0:T(8,128)(2,1)S(1)}, u32[]{:S(2)}, u32[]{:S(2)}) async-start(bf16[32,128,128]{2,1,0:T(8,128)(2,1)} %split.1), calls=%async_computation.2 | async-start | bytes 2097152 | tf_op jit(solution)/shard_map/all_to_all | solution.py:367
  50.2 1.5 collective-permute-start.3
  52.3 4.5 %collective-permute-start.2 = (bf16[1,256,128]{2,1,0:T(8,128)(2,1)S(1)}, bf16[1,256,128]{2,1,0:T(8,128)(2,1)S(1)}, u32[]{:S(2)}, u32[]{:S(2)}) collective-permute-start(bf16[1,256,128]{2,1,0:T(8,128)(2,1)S(1)} %maximum_bitcast_fusion), channel_id=1, source_target_pairs={{0,4},{1,5},{2,6},{3,7},{4,0},{5,1},{6,2},{7,3},{8,12},{9,13},{10,... | collective-permute-start | bytes 196616 | tf_op jit(solution)/shard_map/ppermute | solution.py:28
  56.7 18.0 %collective-permute-done.3 = bf16[1,256,128]{2,1,0:T(8,128)(2,1)S(1)} collective-permute-done((bf16[1,256,128]{2,1,0:T(8,128)(2,1)S(1)}, bf16[1,256,128]{2,1,0:T(8,128)(2,1)S(1)}, u32[]{:S(2)}, u32[]{:S(2)}) %collective-permute-start.3) | collective-permute-done | bytes 65568 | tf_op jit(solution)/shard_map/ppermute | solution.py:28
  75.3 3.8 %collective-permute-start.1 = (bf16[2,256,128]{2,1,0:T(8,128)(2,1)S(1)}, bf16[2,256,128]{2,1,0:T(8,128)(2,1)S(1)}, u32[]{:S(2)}, u32[]{:S(2)}) collective-permute-start(bf16[2,256,128]{2,1,0:T(8,128)(2,1)S(1)} %get-tuple-element.4), channel_id=1, source_target_pairs={{0,6},{1,7},{2,0},{3,1},{4,2},{5,3},{6,4},{7,5},{8,14},{9,15},{10,... | collective-permute-start | bytes 393224 | tf_op jit(solution)/shard_map/ppermute | solution.py:28
  80.5 5.1 %collective-permute-done.1 = bf16[2,256,128]{2,1,0:T(8,128)(2,1)S(1)} collective-permute-done((bf16[2,256,128]{2,1,0:T(8,128)(2,1)S(1)}, bf16[2,256,128]{2,1,0:T(8,128)(2,1)S(1)}, u32[]{:S(2)}, u32[]{:S(2)}) %collective-permute-start.1) | collective-permute-done | bytes 131104 | tf_op jit(solution)/shard_map/ppermute | solution.py:28
  88.2 2.4 %collective-permute-start.5 = (bf16[8,256,128]{2,1,0:T(8,128)(2,1)S(1)}, bf16[8,256,128]{2,1,0:T(8,128)(2,1)S(1)}, u32[]{:S(2)}, u32[]{:S(2)}) collective-permute-start(bf16[8,256,128]{2,1,0:T(8,128)(2,1)S(1)} %constant_dynamic-update-slice_fusion.p0), channel_id=1, source_target_pairs={{0,24},{8,0},{16,8},{24,16},{1,25},{9,1},{17,9},{25,17},{2,26},{10... | collective-permute-start | bytes 1572872 | tf_op jit(solution)/shard_map/ppermute | solution.py:28
  90.6 8.9 %collective-permute-done.6.p2 = bf16[8,256,128]{2,1,0:T(8,128)(2,1)S(1)} collective-permute-done((bf16[8,256,128]{2,1,0:T(8,128)(2,1)S(1)}, bf16[8,256,128]{2,1,0:T(8,128)(2,1)S(1)}, u32[]{:S(2)}, u32[]{:S(2)}) %collective-permute-start.6) | collective-permute-done | bytes 524320 | tf_op jit(solution)/shard_map/ppermute | solution.py:28
  100.4 2.7 %collective-permute-start.8 = (bf16[4,256,128]{2,1,0:T(8,128)(2,1)S(1)}, bf16[4,256,128]{2,1,0:T(8,128)(2,1)}, u32[]{:S(2)}, u32[]{:S(2)}) collective-permute-start(bf16[4,256,128]{2,1,0:T(8,128)(2,1)S(1)} %slice.24), channel_id=1, source_target_pairs={{0,24},{8,0},{16,8},{24,16},{1,25},{9,1},{17,9},{25,17},{2,26},{10... | collective-permute-start | bytes 786440 | tf_op jit(solution)/shard_map/ppermute | solution.py:28
  104.5 2.7 %collective-permute-done.7.p3 = bf16[4,256,128]{2,1,0:T(8,128)(2,1)S(1)} collective-permute-done((bf16[4,256,128]{2,1,0:T(8,128)(2,1)S(1)}, bf16[4,256,128]{2,1,0:T(8,128)(2,1)S(1)}, u32[]{:S(2)}, u32[]{:S(2)}) %collective-permute-start.7) | collective-permute-done | bytes 262176 | tf_op jit(solution)/shard_map/ppermute | solution.py:28
  107.8 10.2 %series.1.sum_ref = bf16[32,128,128]{2,1,0:T(8,128)(2,1)} custom-call(s32[2]{0:T(128)} %pad_add_fusion.pos_ref, bf16[32,136,128]{2,1,0:T(8,128)(2,1)} %copy-done.1, bf16[8,256,128]{2,1,0:T(8,128)(2,1)} %copy-done.7, bf16[8,256,128]{2,1,0:T(8,128)(2,1)} %copy-done.4, bf16[8,256,128]{2,1,0:T(8,128)(2,1)} %copy-done.3, bf16[4,256,128]{2,1,0:T(8,128)(2,1)} %copy-done.10, ...), custom_call_target="tpu_custom_call" | custom-call | flops 3000000000 | bytes 5000000 | tf_op jit(solution)/shard_map/series/pallas_call | solution.py:305
  119.0 8.8 %rates.1 = f32[8,128]{1,0:T(8,128)} custom-call(s32[2]{0:T(128)} %pad_add_fusion.pos_ref, bf16[32,136,128]{2,1,0:T(8,128)(2,1)} %copy-done.1, bf16[32,128,128]{2,1,0:T(8,128)(2,1)} %series.1.sum_ref, bf16[32,128,128]{2,1,0:T(8,128)(2,1)} %copy-done.2, bf16[8,256,128]{2,1,0:T(8,128)(2,1)} %copy-done.7, bf16[8,256,128]{2,1,0:T(8,128)(2,1)} %copy-done.4, ...), custom_call_target="tpu_custom_call" | custom-call | flops 2000000000 | bytes 5000000 | tf_op jit(solution)/shard_map/rates/pallas_call | solution.py:323
  127.8 1.6 collective-permute-start.9
  129.4 2.3 %collective-permute-done.9 = f32[8,128]{1,0:T(8,128)S(1)} collective-permute-done((f32[8,128]{1,0:T(8,128)}, f32[8,128]{1,0:T(8,128)S(1)}, u32[]{:S(2)}, u32[]{:S(2)}) %collective-permute-start.9) | collective-permute-done | bytes 4128 | tf_op jit(solution)/shard_map/ppermute | solution.py:33
  132.4 3.0 %collective-permute-start.10 = (f32[8,128]{1,0:T(8,128)S(1)}, f32[8,128]{1,0:T(8,128)S(1)}, u32[]{:S(2)}, u32[]{:S(2)}) collective-permute-start(f32[8,128]{1,0:T(8,128)S(1)} %add.18), channel_id=1, source_target_pairs={{0,128},{64,192},{128,0},{192,64},{1,129},{65,193},{129,1},{193,65... | collective-permute-start | bytes 12296 | tf_op jit(solution)/shard_map/ppermute | solution.py:33
  135.4 2.1 %collective-permute-done.10 = f32[8,128]{1,0:T(8,128)S(1)} collective-permute-done((f32[8,128]{1,0:T(8,128)S(1)}, f32[8,128]{1,0:T(8,128)S(1)}, u32[]{:S(2)}, u32[]{:S(2)}) %collective-permute-start.10) | collective-permute-done | bytes 4128 | tf_op jit(solution)/shard_map/ppermute | solution.py:33
  138.7 17.8 %all_to_all.20 = f32[32,1,128]{2,1,0:T(1,128)S(1)} all-to-all(f32[32,1,128]{2,1,0:T(1,128)S(1)} %broadcast_in_dim.15), channel_id=1, replica_groups=mesh['batch_0'=4,'batch_1'=2,'seq_0'=4,'seq_1'=8] {'seq_0','seq_1'}, dimensions={0} | all-to-all | bytes 32768 | tf_op jit(solution)/shard_map/all_to_all | solution.py:377
  156.5 5.0 %all-to-all-start.1 = ((bf16[32,128,128]{2,1,0:T(8,128)(2,1)}), bf16[32,128,128]{2,1,0:T(8,128)(2,1)S(1)}, u32[]{:S(2)}, u32[]{:S(2)}) async-start(bf16[32,128,128]{2,1,0:T(8,128)(2,1)} %series.1.sum_ref), calls=%async_computation.1 | async-start | bytes 2097152 | tf_op jit(solution)/shard_map/all_to_all | solution.py:369
  162.1 27.3 %all-to-all-done.1.in_ref = bf16[32,128,128]{2,1,0:T(8,128)(2,1)S(1)} async-done(((bf16[32,128,128]{2,1,0:T(8,128)(2,1)}), bf16[32,128,128]{2,1,0:T(8,128)(2,1)S(1)}, u32[]{:S(2)}, u32[]{:S(2)}) %all-to-all-start.1) | async-done | bytes 1048608 | tf_op jit(solution)/shard_map/all_to_all | solution.py:369
  190.4 2.2 %join.1 = bf16[128,4096]{1,0:T(8,128)(2,1)} custom-call(bf16[32,128,128]{2,1,0:T(8,128)(2,1)} %copy-done), custom_call_target="tpu_custom_call" | custom-call | tf_op jit(solution)/shard_map/join/pallas_call | solution.py:110
  (57 shorter events, 12.5 us)
Async XLA Ops:
  3.6 41.2 %all-to-all-start = ((bf16[32,136,128]{2,1,0:T(8,128)(2,1)}), bf16[32,136,128]{2,1,0:T(8,128)(2,1)S(1)}, u32[]{:S(2)}, u32[]{:S(2)}) async-start(bf16[32,136,128]{2,1,0:T(8,128)(2,1)} %pack.1), calls=%async_computation | async-start | bytes 2228224 | tf_op jit(solution)/shard_map/all_to_all | solution.py:366
  17.2 33.0 %copy-start.5 = (bf16[1,128,128]{2,1,0:T(8,128)(2,1)S(1)}, bf16[1,128,128]{2,1,0:T(8,128)(2,1)}, u32[]{:S(2)}) copy-start(bf16[1,128,128]{2,1,0:T(8,128)(2,1)} %param.11) | copy-start | bytes 98308
  17.2 33.0 %copy-start.6 = (bf16[1,128,128]{2,1,0:T(8,128)(2,1)S(1)}, bf16[1,128,128]{2,1,0:T(8,128)(2,1)}, u32[]{:S(2)}) copy-start(bf16[1,128,128]{2,1,0:T(8,128)(2,1)} %param.10) | copy-start | bytes 98308
  44.8 5.3 %copy-start.1 = (bf16[32,136,128]{2,1,0:T(8,128)(2,1)}, bf16[32,136,128]{2,1,0:T(8,128)(2,1)S(1)}, u32[]{:S(2)}) copy-start(bf16[32,136,128]{2,1,0:T(8,128)(2,1)S(1)} %all-to-all-done.in_ref) | copy-start | bytes 3342340
  44.8 73.2 %all-to-all-start.2 = ((bf16[32,128,128]{2,1,0:T(8,128)(2,1)}), bf16[32,128,128]{2,1,0:T(8,128)(2,1)S(1)}, u32[]{:S(2)}, u32[]{:S(2)}) async-start(bf16[32,128,128]{2,1,0:T(8,128)(2,1)} %split.1), calls=%async_computation.2 | async-start | bytes 2097152 | tf_op jit(solution)/shard_map/all_to_all | solution.py:367
  50.2 24.6 %collective-permute-start.3 = (bf16[1,256,128]{2,1,0:T(8,128)(2,1)S(1)}, bf16[1,256,128]{2,1,0:T(8,128)(2,1)S(1)}, u32[]{:S(2)}, u32[]{:S(2)}) collective-permute-start(bf16[1,256,128]{2,1,0:T(8,128)(2,1)S(1)} %maximum_bitcast_fusion), channel_id=1, source_target_pairs={{0,1},{1,2},{2,3},{3,4},{4,5},{5,6},{6,7},{7,0},{8,9},{9,10},{10,1... | collective-permute-start | bytes 196616 | tf_op jit(solution)/shard_map/ppermute | solution.py:28
  51.7 23.6 %collective-permute-start = (bf16[1,256,128]{2,1,0:T(8,128)(2,1)S(1)}, bf16[1,256,128]{2,1,0:T(8,128)(2,1)S(1)}, u32[]{:S(2)}, u32[]{:S(2)}) collective-permute-start(bf16[1,256,128]{2,1,0:T(8,128)(2,1)S(1)} %maximum_bitcast_fusion), channel_id=1, source_target_pairs={{0,7},{1,0},{2,1},{3,2},{4,3},{5,4},{6,5},{7,6},{8,15},{9,8},{10,9... | collective-permute-start | bytes 196616 | tf_op jit(solution)/shard_map/ppermute | solution.py:28
  52.3 33.3 %collective-permute-start.2 = (bf16[1,256,128]{2,1,0:T(8,128)(2,1)S(1)}, bf16[1,256,128]{2,1,0:T(8,128)(2,1)S(1)}, u32[]{:S(2)}, u32[]{:S(2)}) collective-permute-start(bf16[1,256,128]{2,1,0:T(8,128)(2,1)S(1)} %maximum_bitcast_fusion), channel_id=1, source_target_pairs={{0,4},{1,5},{2,6},{3,7},{4,0},{5,1},{6,2},{7,3},{8,12},{9,13},{10,... | collective-permute-start | bytes 196616 | tf_op jit(solution)/shard_map/ppermute | solution.py:28
  75.3 27.8 %copy-start.8 = (f32[64]{0:T(128)S(1)}, f32[64]{0:T(128)}, u32[]{:S(2)}) copy-start(f32[64]{0:T(128)} %param.15) | copy-start | bytes 772
  75.3 27.8 %copy-start.9 = (f32[64]{0:T(128)S(1)}, f32[64]{0:T(128)}, u32[]{:S(2)}) copy-start(f32[64]{0:T(128)} %param.14) | copy-start | bytes 772
  75.3 10.3 %collective-permute-start.1 = (bf16[2,256,128]{2,1,0:T(8,128)(2,1)S(1)}, bf16[2,256,128]{2,1,0:T(8,128)(2,1)S(1)}, u32[]{:S(2)}, u32[]{:S(2)}) collective-permute-start(bf16[2,256,128]{2,1,0:T(8,128)(2,1)S(1)} %get-tuple-element.4), channel_id=1, source_target_pairs={{0,6},{1,7},{2,0},{3,1},{4,2},{5,3},{6,4},{7,5},{8,14},{9,15},{10,... | collective-permute-start | bytes 393224 | tf_op jit(solution)/shard_map/ppermute | solution.py:28
  79.1 7.7 %collective-permute-start.4 = (bf16[2,256,128]{2,1,0:T(8,128)(2,1)S(1)}, bf16[2,256,128]{2,1,0:T(8,128)(2,1)S(1)}, u32[]{:S(2)}, u32[]{:S(2)}) collective-permute-start(bf16[2,256,128]{2,1,0:T(8,128)(2,1)S(1)} %get-tuple-element.3), channel_id=1, source_target_pairs={{0,2},{1,3},{2,4},{3,5},{4,6},{5,7},{6,0},{7,1},{8,10},{9,11},{10,... | collective-permute-start | bytes 393224 | tf_op jit(solution)/shard_map/ppermute | solution.py:28
  86.9 20.3 %copy-start.7 = (bf16[8,256,128]{2,1,0:T(8,128)(2,1)}, bf16[8,256,128]{2,1,0:T(8,128)(2,1)S(1)}, u32[]{:S(2)}) copy-start(bf16[8,256,128]{2,1,0:T(8,128)(2,1)S(1)} %constant_dynamic-update-slice_fusion.p0) | copy-start | bytes 1572868
  86.9 12.6 %collective-permute-start.6 = (bf16[8,256,128]{2,1,0:T(8,128)(2,1)S(1)}, bf16[8,256,128]{2,1,0:T(8,128)(2,1)S(1)}, u32[]{:S(2)}, u32[]{:S(2)}) collective-permute-start(bf16[8,256,128]{2,1,0:T(8,128)(2,1)S(1)} %constant_dynamic-update-slice_fusion.p0), channel_id=1, source_target_pairs={{0,8},{8,16},{16,24},{24,0},{1,9},{9,17},{17,25},{25,1},{2,10},{10... | collective-permute-start | bytes 1572872 | tf_op jit(solution)/shard_map/ppermute | solution.py:28
  88.2 12.2 %collective-permute-start.5 = (bf16[8,256,128]{2,1,0:T(8,128)(2,1)S(1)}, bf16[8,256,128]{2,1,0:T(8,128)(2,1)S(1)}, u32[]{:S(2)}, u32[]{:S(2)}) collective-permute-start(bf16[8,256,128]{2,1,0:T(8,128)(2,1)S(1)} %constant_dynamic-update-slice_fusion.p0), channel_id=1, source_target_pairs={{0,24},{8,0},{16,8},{24,16},{1,25},{9,1},{17,9},{25,17},{2,26},{10... | collective-permute-start | bytes 1572872 | tf_op jit(solution)/shard_map/ppermute | solution.py:28
  99.4 7.7 %copy-start.3 = (bf16[8,256,128]{2,1,0:T(8,128)(2,1)}, bf16[8,256,128]{2,1,0:T(8,128)(2,1)S(1)}, u32[]{:S(2)}) copy-start(bf16[8,256,128]{2,1,0:T(8,128)(2,1)S(1)} %collective-permute-done.6.p2) | copy-start | bytes 1572868
  99.5 7.7 %collective-permute-start.7 = (bf16[4,256,128]{2,1,0:T(8,128)(2,1)S(1)}, bf16[4,256,128]{2,1,0:T(8,128)(2,1)S(1)}, u32[]{:S(2)}, u32[]{:S(2)}) collective-permute-start(bf16[4,256,128]{2,1,0:T(8,128)(2,1)S(1)} %slice.23), channel_id=1, source_target_pairs={{0,8},{8,16},{16,24},{24,0},{1,9},{9,17},{17,25},{25,1},{2,10},{10... | collective-permute-start | bytes 786440 | tf_op jit(solution)/shard_map/ppermute | solution.py:28
  100.3 6.8 %copy-start.4 = (bf16[8,256,128]{2,1,0:T(8,128)(2,1)}, bf16[8,256,128]{2,1,0:T(8,128)(2,1)S(1)}, u32[]{:S(2)}) copy-start(bf16[8,256,128]{2,1,0:T(8,128)(2,1)S(1)} %collective-permute-done.5.p1) | copy-start | bytes 1572868
  100.4 6.8 %collective-permute-start.8 = (bf16[4,256,128]{2,1,0:T(8,128)(2,1)S(1)}, bf16[4,256,128]{2,1,0:T(8,128)(2,1)}, u32[]{:S(2)}, u32[]{:S(2)}) collective-permute-start(bf16[4,256,128]{2,1,0:T(8,128)(2,1)S(1)} %slice.24), channel_id=1, source_target_pairs={{0,24},{8,0},{16,8},{24,16},{1,25},{9,1},{17,9},{25,17},{2,26},{10... | collective-permute-start | bytes 786440 | tf_op jit(solution)/shard_map/ppermute | solution.py:28
  127.8 3.9 %collective-permute-start.9 = (f32[8,128]{1,0:T(8,128)}, f32[8,128]{1,0:T(8,128)S(1)}, u32[]{:S(2)}, u32[]{:S(2)}) collective-permute-start(f32[8,128]{1,0:T(8,128)} %rates.1), channel_id=1, source_target_pairs={{0,64},{64,0},{128,192},{192,128},{1,65},{65,1},{129,193},{193,129... | collective-permute-start | bytes 12296 | tf_op jit(solution)/shard_map/ppermute | solution.py:33
  132.4 5.1 %collective-permute-start.10 = (f32[8,128]{1,0:T(8,128)S(1)}, f32[8,128]{1,0:T(8,128)S(1)}, u32[]{:S(2)}, u32[]{:S(2)}) collective-permute-start(f32[8,128]{1,0:T(8,128)S(1)} %add.18), channel_id=1, source_target_pairs={{0,128},{64,192},{128,0},{192,64},{1,129},{65,193},{129,1},{193,65... | collective-permute-start | bytes 12296 | tf_op jit(solution)/shard_map/ppermute | solution.py:33
  137.5 1.2 collective-permute-start.11
  156.5 32.9 %all-to-all-start.1 = ((bf16[32,128,128]{2,1,0:T(8,128)(2,1)}), bf16[32,128,128]{2,1,0:T(8,128)(2,1)S(1)}, u32[]{:S(2)}, u32[]{:S(2)}) async-start(bf16[32,128,128]{2,1,0:T(8,128)(2,1)} %series.1.sum_ref), calls=%async_computation.1 | async-start | bytes 2097152 | tf_op jit(solution)/shard_map/all_to_all | solution.py:369
  189.4 1.0 copy-start
  (2 other events, 1.7 us)

commit v5 on v4

--- a/solution.py
+++ b/solution.py
@@ -12,7 +12,6 @@
 Q = 128
 EXTRA = 8
 GROUPS = 32
-NY = 4
 NZ = 8
 UNROLL = 16
 PREP = 16
@@ -23,11 +22,6 @@
 BF16 = jnp.bfloat16
 
 
-def shifted(x, axis, by):
-    size = lax.axis_size(axis)
-    return lax.ppermute(x, axis, [(i, (i + by) % size) for i in range(size)])
-
-
 def swapped(x, axis, bit):
     size = lax.axis_size(axis)
     return lax.ppermute(x, axis, [(i, i ^ bit) for i in range(size)])
@@ -123,27 +117,6 @@
 
 def dot_t(a, b):
     return lax.dot_general(a, b, (((1,), (1,)), ((), ())), preferred_element_type=F32)
-
-
-def fetch_maps(pos_ref, pieces, maps_ref, sem):
-    my_y, my_z = pos_ref[0], pos_ref[1]
-    copies = []
-    for dy in range(NY):
-        for dz in range(NZ):
-            if dy == 0:
-                source = pieces[0].at[dz]
-            elif dy == 1:
-                source = pieces[1].at[dz]
-            elif dy == 3:
-                source = pieces[2].at[dz]
-            else:
-                source = pieces[3].at[dz] if dz < 4 else pieces[4].at[dz - 4]
-            place = ((my_y + dy) % NY) * NZ + (my_z + dz) % NZ
-            copies.append(pltpu.make_async_copy(source, maps_ref.at[place], sem))
-    for c in copies:
-        c.start()
-    for c in copies:
-        c.wait()
 
 
 def constants():
@@ -187,8 +160,7 @@
     m_ref[c] = jnp.broadcast_to(jnp.exp(middle), (8, 128))
 
 
-def series_kernel(pos_ref, in_ref, p0, p1, p2, p3, p4, rate_ref, out_ref, maps_ref, mat_ref, turn_ref, e_ref, g_ref, m_ref, v_ref, sum_ref, back_ref, sem):
-    fetch_maps(pos_ref, (p0, p1, p2, p3, p4), maps_ref, sem)
+def series_kernel(in_ref, maps_ref, rate_ref, out_ref, mat_ref, turn_ref, e_ref, g_ref, m_ref, v_ref, sum_ref, back_ref):
     consts = constants()
 
     def prep(i, _):
@@ -233,8 +205,7 @@
         lax.fori_loop(0, GROUPS // UNROLL, step, 0)
 
 
-def rate_kernel(pos_ref, in_ref, sum_ref, fixed_ref, p0, p1, p2, p3, p4, rate_ref, out_ref, maps_ref, mat_ref, turn_ref, e_ref, g_ref, s_ref, m_ref, back_ref, acc_ref, sem):
-    fetch_maps(pos_ref, (p0, p1, p2, p3, p4), maps_ref, sem)
+def rate_kernel(pos_ref, in_ref, sum_ref, fixed_ref, maps_ref, rate_ref, out_ref, mat_ref, turn_ref, e_ref, g_ref, s_ref, m_ref, back_ref, acc_ref):
     consts = constants()
 
     def prep(i, _):
@@ -291,7 +262,6 @@
 def table_scratch(with_sums):
     square = pltpu.VMEM((GROUPS, Q, 128), F32)
     return [
-        pltpu.VMEM((GROUPS, 2 * N, 128), BF16),
         pltpu.VMEM((GROUPS, Q, 256), BF16),
         pltpu.VMEM((GROUPS, N, Q), BF16),
         square,
@@ -301,10 +271,10 @@
     ]
 
 
-def series(pos, rows, pieces, rate):
+def series(rows, maps, rate):
     return pl.pallas_call(
         series_kernel,
-        in_specs=[SMEM, full(rows.shape), HBM, HBM, HBM, HBM, HBM, full(rate.shape)],
+        in_specs=[full(rows.shape), full(maps.shape), full(rate.shape)],
         out_specs=full((GROUPS, Q, 128)),
         out_shape=jax.ShapeDtypeStruct((GROUPS, Q, 128), BF16),
         scratch_shapes=[
@@ -312,45 +282,22 @@
             pltpu.VMEM((GROUPS, Q, 128), BF16),
             pltpu.VMEM((GROUPS, Q, 128), F32),
             pltpu.VMEM((N, 128), F32),
-            pltpu.SemaphoreType.DMA,
         ],
         name="series",
         cost_estimate=pl.CostEstimate(flops=3_000_000_000, transcendentals=1_000_000, bytes_accessed=5_000_000),
-    )(pos, rows, *pieces, rate)
-
-
-def rates(pos, rows, summed, fixed, pieces, rate):
+    )(rows, maps, rate)
+
+
+def rates(pos, rows, summed, fixed, maps, rate):
     return pl.pallas_call(
         rate_kernel,
-        in_specs=[SMEM, full(rows.shape), full(summed.shape), full(fixed.shape), HBM, HBM, HBM, HBM, HBM, full(rate.shape)],
+        in_specs=[SMEM, full(rows.shape), full(summed.shape), full(fixed.shape), full(maps.shape), full(rate.shape)],
         out_specs=full((8, 128)),
         out_shape=jax.ShapeDtypeStruct((8, 128), F32),
-        scratch_shapes=[
-            *table_scratch(True),
-            pltpu.VMEM((N, 256), F32),
-            pltpu.VMEM((2, 8, 128), F32),
-            pltpu.SemaphoreType.DMA,
-        ],
+        scratch_shapes=[*table_scratch(True), pltpu.VMEM((N, 256), F32), pltpu.VMEM((2, 8, 128), F32)],
         name="rates",
         cost_estimate=pl.CostEstimate(flops=2_000_000_000, transcendentals=1_000_000, bytes_accessed=5_000_000),
-    )(pos, rows, summed, fixed, *pieces, rate)
-
-
-def gather_line(input_map, output_map):
-    own = jnp.concatenate([input_map, output_map], axis=0)[None]
-    last, after = shifted(own, "seq_1", 1), shifted(own, "seq_1", -1)
-    far_last = shifted(jnp.concatenate([last, own]), "seq_1", 2)
-    far_after = shifted(jnp.concatenate([own, after]), "seq_1", -2)
-    far = shifted(own, "seq_1", 4)
-    return jnp.concatenate([own, after, far_after, far, far_last, last])
-
-
-def gather_plane(line):
-    from_next = shifted(line, "seq_0", -1)
-    from_last = shifted(line, "seq_0", 1)
-    low = shifted(from_last[:4], "seq_0", 1)
-    high = shifted(from_next[4:], "seq_0", -1)
-    return line, from_next, from_last, low, high
+    )(pos, rows, summed, fixed, maps, rate)
 
 
 def inner(cotangent, fixed_point, input_map, output_map, step_size, forget, decay_rate, skip_gain):
@@ -360,14 +307,14 @@
     own = jnp.stack([lax.dynamic_slice_in_dim(a, first, 2) for a in (decay_rate, skip_gain)])
     rate = jnp.repeat(own, HEAD, axis=1)
 
-    line = gather_line(input_map[0], output_map[0])
+    both_maps = jnp.concatenate([input_map[0], output_map[0]], axis=0)
+    maps = lax.all_gather(both_maps, SEQ, axis=0, tiled=True).reshape(GROUPS, 2 * N, 128)
     packed = pack(cotangent[0], step_size[0], forget)
-    pieces = gather_plane(line)
     rows = lax.all_to_all(packed, SEQ, split_axis=0, concat_axis=0, tiled=True)
     fixed = lax.all_to_all(split(fixed_point[0]), SEQ, split_axis=0, concat_axis=0, tiled=True)
-    summed = series(pos, rows, pieces, rate)
+    summed = series(rows, maps, rate)
     result = lax.all_to_all(summed, SEQ, split_axis=0, concat_axis=0, tiled=True)
-    totals = rates(pos, rows, summed, fixed, pieces, rate)
+    totals = rates(pos, rows, summed, fixed, maps, rate)
     for axis in BATCH:
         bit = 1
         while bit < lax.axis_size(axis):

time: 194 us -> 189 us (0.974)
  starting transfers between devices: 45.2 us -> 26.1 us
  between operations: 1.01 us -> 14.1 us
  waiting for transfers between devices: 96.8 us -> 101 us
    all_gather x0 -> x1, waiting for transfers between devices: none -> 37.6 us  [inner(): lax.all_gather(both_maps, SEQ, axis=0, tiled=True)]
    ppermute x9 -> x0, waiting for transfers between devices: 36.3 us -> none  [shifted(): return lax.ppermute(x, axis, [(i, (i + by) % size) for i in range(size)])]
    ppermute x9 -> x0, starting transfers between devices: 19 us -> none  [shifted(): return lax.ppermute(x, axis, [(i, (i + by) % size) for i in range(size)])]
    all_to_all x1, waiting for transfers between devices: 27.7 us -> 30 us  [inner(): rows = lax.all_to_all(packed, SEQ, split_axis=0, concat_axis=0, tiled=True)]
  transfers between devices with their start and end apart: 15 -> 7, of which waited for: 11 -> 6; matrix products, arithmetic and copies ran while one was open for 1% -> 1% of each run, Pallas kernels for 6% -> 8%
where the time goes in v5:
time: 189 us; the launch traced here: 188 us
  waiting for transfers between devices  101 us (53%)
  starting transfers between devices  26.1 us (14%)
  Pallas kernels  24.5 us (13%)
  blocking collectives  16.2 us (9%)
  between operations  14.1 us (7%)
  local copies, waits for them, and re-layouts  3.4 us (2%)
  other arithmetic  2.81 us (1%)
    all_gather x1, waiting for transfers between devices, inner(): lax.all_gather(both_maps, SEQ, axis=0, tiled=True)  37.6 us
    all_to_all x1, waiting for transfers between devices, inner(): rows = lax.all_to_all(packed, SEQ, split_axis=0, concat_axis=0, tiled=True)  30 us
    all_to_all x1, waiting for transfers between devices, inner(): lax.all_to_all(summed, SEQ, split_axis=0, concat_axis=0, tiled=True)  27.3 us
    all_to_all x1, blocking collectives, inner(): lax.all_to_all(copies, SEQ, split_axis=0, concat_axis=0, tiled=True)  16.2 us
    all_to_all x1, starting transfers between devices, inner(): rows = lax.all_to_all(packed, SEQ, split_axis=0, concat_axis=0, tiled=True)  11.4 us
    pallas_call x1, Pallas kernels, series(): pl.pallas_call(series_kernel, in_specs=[full(rows.shape), full(maps.shape...  9.29 us
    pallas_call x1, Pallas kernels, rates(): pl.pallas_call(rate_kernel, in_specs=[SMEM, full(rows.shape), full(summed...  7.87 us
    ppermute x3, waiting for transfers between devices, swapped(): return lax.ppermute(x, axis, [(i, i ^ bit) for i in range(size)])  5.63 us
  transfers between devices with their start and end apart: 7, of which 6 were waited for; matrix products, arithmetic and copies ran while one was open for 1% of the time, Pallas kernels for 8%

profile of v5, /device:TPU:32, one launch (start us, length us, event | category | flops | bytes accessed | tf_op | source)
XLA Modules:
  0.0 187.7 jit_solution(426163275016678916)
XLA Ops:
  7.2 1.4 pad_maximum_fusion
  8.6 3.0 %pack.1 = bf16[32,136,128]{2,1,0:T(8,128)(2,1)} custom-call(f32[64,128]{1,0:T(8,128)} %bitcast.20, f32[1,128]{1,0:T(1,128)} %forget_ref.1, bf16[128,4096]{1,0:T(8,128)(2,1)} %bitcast.16), custom_call_target="tpu_custom_call" | custom-call | tf_op jit(solution)/shard_map/pack/pallas_call | solution.py:62
  11.6 11.4 %all-to-all-start = ((bf16[32,136,128]{2,1,0:T(8,128)(2,1)}), bf16[32,136,128]{2,1,0:T(8,128)(2,1)S(1)}, u32[]{:S(2)}, u32[]{:S(2)}) async-start(bf16[32,136,128]{2,1,0:T(8,128)(2,1)} %pack.1), calls=%async_computation | async-start | bytes 2228224 | tf_op jit(solution)/shard_map/all_to_all | solution.py:313
  23.0 2.2 %split.1 = bf16[32,128,128]{2,1,0:T(8,128)(2,1)} custom-call(bf16[128,4096]{1,0:T(8,128)(2,1)} %bitcast.17), custom_call_target="tpu_custom_call" | custom-call | tf_op jit(solution)/shard_map/split/pallas_call | solution.py:83
  25.2 30.0 %all-to-all-done.in_ref = bf16[32,136,128]{2,1,0:T(8,128)(2,1)S(1)} async-done(((bf16[32,136,128]{2,1,0:T(8,128)(2,1)}), bf16[32,136,128]{2,1,0:T(8,128)(2,1)S(1)}, u32[]{:S(2)}, u32[]{:S(2)}) %all-to-all-start) | async-done | bytes 1114144 | tf_op jit(solution)/shard_map/all_to_all | solution.py:313
  55.2 5.3 %all-to-all-start.2 = ((bf16[32,128,128]{2,1,0:T(8,128)(2,1)}), bf16[32,128,128]{2,1,0:T(8,128)(2,1)S(1)}, u32[]{:S(2)}, u32[]{:S(2)}) async-start(bf16[32,128,128]{2,1,0:T(8,128)(2,1)} %split.1), calls=%async_computation.2 | async-start | bytes 2097152 | tf_op jit(solution)/shard_map/all_to_all | solution.py:314
  60.7 0.7 reshape.14.rate_ref
  61.3 0.7 pad_add_fusion.pos_ref
  62.0 37.6 %all-gather.2.cloned.1.call-done = bf16[8192,128]{1,0:T(8,128)(2,1)} async-done(((bf16[256,128]{1,0:T(8,128)(2,1)}), bf16[8192,128]{1,0:T(8,128)(2,1)}) %all-gather.2.cloned.1.call-update) | async-done | bytes 2097168 | tf_op jit(solution)/shard_map/all_gather | solution.py:311
  99.6 9.3 %series.1.sum_ref = bf16[32,128,128]{2,1,0:T(8,128)(2,1)} custom-call(bf16[32,136,128]{2,1,0:T(8,128)(2,1)} %copy-done.1, bf16[32,256,128]{2,1,0:T(8,128)(2,1)} %bitcast.23, f32[2,128]{1,0:T(2,128)} %reshape.14.rate_ref), custom_call_target="tpu_custom_call" | custom-call | flops 3000000000 | bytes 5000000 | tf_op jit(solution)/shard_map/series/pallas_call | solution.py:275
  108.9 1.0 copy-done.2
  109.9 7.9 %rates.1 = f32[8,128]{1,0:T(8,128)} custom-call(s32[2]{0:T(128)} %pad_add_fusion.pos_ref, bf16[32,136,128]{2,1,0:T(8,128)(2,1)} %copy-done.1, bf16[32,128,128]{2,1,0:T(8,128)(2,1)} %series.1.sum_ref, bf16[32,128,128]{2,1,0:T(8,128)(2,1)} %copy-done.2, bf16[32,256,128]{2,1,0:T(8,128)(2,1)} %bitcast.24, f32[2,128]{1,0:T(2,128)} %reshape.14.rate_ref), custom_call_target="tpu_custom_call" | custom-call | flops 2000000000 | bytes 5000000 | tf_op jit(solution)/shard_map/rates/pallas_call | solution.py:292
  117.8 1.5 collective-permute-start
  119.3 2.3 %collective-permute-done = f32[8,128]{1,0:T(8,128)S(1)} collective-permute-done((f32[8,128]{1,0:T(8,128)}, f32[8,128]{1,0:T(8,128)S(1)}, u32[]{:S(2)}, u32[]{:S(2)}) %collective-permute-start) | collective-permute-done | bytes 4128 | tf_op jit(solution)/shard_map/ppermute | solution.py:27
  121.6 0.7 add.18
  122.3 3.0 %collective-permute-start.1 = (f32[8,128]{1,0:T(8,128)S(1)}, f32[8,128]{1,0:T(8,128)S(1)}, u32[]{:S(2)}, u32[]{:S(2)}) collective-permute-start(f32[8,128]{1,0:T(8,128)S(1)} %add.18), channel_id=1, source_target_pairs={{0,128},{64,192},{128,0},{192,64},{1,129},{65,193},{129,1},{193,65... | collective-permute-start | bytes 12296 | tf_op jit(solution)/shard_map/ppermute | solution.py:27
  125.3 2.1 %collective-permute-done.1 = f32[8,128]{1,0:T(8,128)S(1)} collective-permute-done((f32[8,128]{1,0:T(8,128)S(1)}, f32[8,128]{1,0:T(8,128)S(1)}, u32[]{:S(2)}, u32[]{:S(2)}) %collective-permute-start.1) | collective-permute-done | bytes 4128 | tf_op jit(solution)/shard_map/ppermute | solution.py:27
  127.4 1.2 collective-permute-done.2
  128.6 16.2 %all_to_all.20 = f32[32,1,128]{2,1,0:T(1,128)S(1)} all-to-all(f32[32,1,128]{2,1,0:T(1,128)S(1)} %broadcast_in_dim.11), channel_id=1, replica_groups=mesh['batch_0'=4,'batch_1'=2,'seq_0'=4,'seq_1'=8] {'seq_0','seq_1'}, dimensions={0} | all-to-all | bytes 32768 | tf_op jit(solution)/shard_map/all_to_all | solution.py:324
  144.8 5.0 %all-to-all-start.1 = ((bf16[32,128,128]{2,1,0:T(8,128)(2,1)}), bf16[32,128,128]{2,1,0:T(8,128)(2,1)S(1)}, u32[]{:S(2)}, u32[]{:S(2)}) async-start(bf16[32,128,128]{2,1,0:T(8,128)(2,1)} %series.1.sum_ref), calls=%async_computation.1 | async-start | bytes 2097152 | tf_op jit(solution)/shard_map/all_to_all | solution.py:316
  149.8 0.6 fusion
  150.4 27.3 %all-to-all-done.1.in_ref = bf16[32,128,128]{2,1,0:T(8,128)(2,1)S(1)} async-done(((bf16[32,128,128]{2,1,0:T(8,128)(2,1)}), bf16[32,128,128]{2,1,0:T(8,128)(2,1)S(1)}, u32[]{:S(2)}, u32[]{:S(2)}) %all-to-all-start.1) | async-done | bytes 1048608 | tf_op jit(solution)/shard_map/all_to_all | solution.py:316
  177.7 1.0 copy-done
  178.6 2.2 %join.1 = bf16[128,4096]{1,0:T(8,128)(2,1)} custom-call(bf16[32,128,128]{2,1,0:T(8,128)(2,1)} %copy-done), custom_call_target="tpu_custom_call" | custom-call | tf_op jit(solution)/shard_map/join/pallas_call | solution.py:104
  (21 shorter events, 0.3 us)
Async XLA Ops:
  7.2 92.5 %all-gather.2.cloned.1.call-start = ((), (), s32[]{:S(2)}) async-start(), calls=%async_computation.4 | async-start | bytes 2162688 | tf_op jit(solution)/shard_map/all_gather | solution.py:311
  11.6 43.6 %all-to-all-start = ((bf16[32,136,128]{2,1,0:T(8,128)(2,1)}), bf16[32,136,128]{2,1,0:T(8,128)(2,1)S(1)}, u32[]{:S(2)}, u32[]{:S(2)}) async-start(bf16[32,136,128]{2,1,0:T(8,128)(2,1)} %pack.1), calls=%async_computation | async-start | bytes 2228224 | tf_op jit(solution)/shard_map/all_to_all | solution.py:313
  25.2 35.3 %copy-start.3 = (f32[64]{0:T(128)S(1)}, f32[64]{0:T(128)}, u32[]{:S(2)}) copy-start(f32[64]{0:T(128)} %param.15) | copy-start | bytes 772
  25.2 35.3 %copy-start.4 = (f32[64]{0:T(128)S(1)}, f32[64]{0:T(128)}, u32[]{:S(2)}) copy-start(f32[64]{0:T(128)} %param.14) | copy-start | bytes 772
  55.2 44.5 %copy-start.1 = (bf16[32,136,128]{2,1,0:T(8,128)(2,1)}, bf16[32,136,128]{2,1,0:T(8,128)(2,1)S(1)}, u32[]{:S(2)}) copy-start(bf16[32,136,128]{2,1,0:T(8,128)(2,1)S(1)} %all-to-all-done.in_ref) | copy-start | bytes 3342340
  55.2 53.8 %all-to-all-start.2 = ((bf16[32,128,128]{2,1,0:T(8,128)(2,1)}), bf16[32,128,128]{2,1,0:T(8,128)(2,1)S(1)}, u32[]{:S(2)}, u32[]{:S(2)}) async-start(bf16[32,128,128]{2,1,0:T(8,128)(2,1)} %split.1), calls=%async_computation.2 | async-start | bytes 2097152 | tf_op jit(solution)/shard_map/all_to_all | solution.py:314
  108.9 1.0 copy-start.2
  117.8 3.8 %collective-permute-start = (f32[8,128]{1,0:T(8,128)}, f32[8,128]{1,0:T(8,128)S(1)}, u32[]{:S(2)}, u32[]{:S(2)}) collective-permute-start(f32[8,128]{1,0:T(8,128)} %rates.1), channel_id=1, source_target_pairs={{0,64},{64,0},{128,192},{192,128},{1,65},{65,1},{129,193},{193,129... | collective-permute-start | bytes 12296 | tf_op jit(solution)/shard_map/ppermute | solution.py:27
  122.3 5.1 %collective-permute-start.1 = (f32[8,128]{1,0:T(8,128)S(1)}, f32[8,128]{1,0:T(8,128)S(1)}, u32[]{:S(2)}, u32[]{:S(2)}) collective-permute-start(f32[8,128]{1,0:T(8,128)S(1)} %add.18), channel_id=1, source_target_pairs={{0,128},{64,192},{128,0},{192,64},{1,129},{65,193},{129,1},{193,65... | collective-permute-start | bytes 12296 | tf_op jit(solution)/shard_map/ppermute | solution.py:27
  127.4 1.2 collective-permute-start.2
  144.8 32.9 %all-to-all-start.1 = ((bf16[32,128,128]{2,1,0:T(8,128)(2,1)}), bf16[32,128,128]{2,1,0:T(8,128)(2,1)S(1)}, u32[]{:S(2)}, u32[]{:S(2)}) async-start(bf16[32,128,128]{2,1,0:T(8,128)(2,1)} %series.1.sum_ref), calls=%async_computation.1 | async-start | bytes 2097152 | tf_op jit(solution)/shard_map/all_to_all | solution.py:316
  177.7 1.0 copy-start
Sparse Core Ops, SparseCore 0:
  11.1 88.4 all-gather.1

commit v6 on v4

--- a/solution.py
+++ b/solution.py
@@ -46,11 +46,12 @@
     return high, (x - high.astype(F32)).astype(BF16)
 
 
-def pack_kernel(step_ref, forget_ref, cot_ref, out_ref, sem):
-    copies = [
-        pltpu.make_async_copy(cot_ref.at[:, pl.ds(j * 128, 128)], out_ref.at[j, pl.ds(0, Q), :], sem)
-        for j in range(GROUPS)
-    ]
+def pack_kernel(step_ref, forget_ref, cot_ref, fixed_ref, out_ref, sem):
+    copies = []
+    for j in range(GROUPS):
+        lanes = pl.ds(j * 128, 128)
+        copies.append(pltpu.make_async_copy(cot_ref.at[:, lanes], out_ref.at[j, pl.ds(0, Q), :], sem))
+        copies.append(pltpu.make_async_copy(fixed_ref.at[:, lanes], out_ref.at[j, pl.ds(Q + EXTRA, Q), :], sem))
     for c in copies:
         c.start()
     step_high, step_low = halves(step_ref[...])
@@ -64,36 +65,16 @@
         c.wait()
 
 
-def pack(cot, step, forget):
+def pack(cot, fixed, step, forget):
+    shape = (GROUPS, 2 * Q + EXTRA, 128)
     return pl.pallas_call(
         pack_kernel,
-        in_specs=[full(step.shape), full(forget.shape), HBM],
-        out_specs=full((GROUPS, Q + EXTRA, 128)),
-        out_shape=jax.ShapeDtypeStruct((GROUPS, Q + EXTRA, 128), BF16),
+        in_specs=[full(step.shape), full(forget.shape), HBM, HBM],
+        out_specs=full(shape),
+        out_shape=jax.ShapeDtypeStruct(shape, BF16),
         scratch_shapes=[pltpu.SemaphoreType.DMA],
         name="pack",
-    )(step, forget, cot)
-
-
-def split_kernel(in_ref, out_ref, sem):
-    copies = [
-        pltpu.make_async_copy(in_ref.at[:, pl.ds(j * 128, 128)], out_ref.at[j], sem) for j in range(GROUPS)
-    ]
-    for c in copies:
-        c.start()
-    for c in copies:
-        c.wait()
-
-
-def split(x):
-    return pl.pallas_call(
-        split_kernel,
-        in_specs=[HBM],
-        out_specs=full((GROUPS, Q, 128)),
-        out_shape=jax.ShapeDtypeStruct((GROUPS, Q, 128), BF16),
-        scratch_shapes=[pltpu.SemaphoreType.DMA],
-        name="split",
-    )(x)
+    )(step, forget, cot, fixed)
 
 
 def join_kernel(in_ref, out_ref, sem):
@@ -233,7 +214,7 @@
         lax.fori_loop(0, GROUPS // UNROLL, step, 0)
 
 
-def rate_kernel(pos_ref, in_ref, sum_ref, fixed_ref, p0, p1, p2, p3, p4, rate_ref, out_ref, maps_ref, mat_ref, turn_ref, e_ref, g_ref, s_ref, m_ref, back_ref, acc_ref, sem):
+def rate_kernel(pos_ref, in_ref, sum_ref, p0, p1, p2, p3, p4, rate_ref, out_ref, maps_ref, mat_ref, turn_ref, e_ref, g_ref, s_ref, m_ref, back_ref, acc_ref, sem):
     fetch_maps(pos_ref, (p0, p1, p2, p3, p4), maps_ref, sem)
     consts = constants()
 
@@ -267,7 +248,7 @@
         mixed = [dot(mat_ref[c], jnp.concatenate([x, b], axis=0)) for c, x, b in zip(groups, turned, states)]
         rate_sum, skip_sum = acc_ref[0], acc_ref[1]
         for c, v, r in zip(groups, values, mixed):
-            z = fixed_ref[c].astype(F32)
+            z = in_ref[c, Q + EXTRA :, :].astype(F32)
             change = g_ref[c] * (r[:, 128:] - s_ref[c] * r[:, :128])
             rate_sum = rate_sum + jnp.sum((z * change).reshape(16, 8, 128), axis=0)
             skip_sum = skip_sum + jnp.sum((z * v).reshape(16, 8, 128), axis=0)
@@ -304,7 +285,8 @@
 def series(pos, rows, pieces, rate):
     return pl.pallas_call(
         series_kernel,
-        in_specs=[SMEM, full(rows.shape), HBM, HBM, HBM, HBM, HBM, full(rate.shape)],
+        grid=(1,),
+        in_specs=[SMEM, full((GROUPS, Q + EXTRA, 128)), HBM, HBM, HBM, HBM, HBM, full(rate.shape)],
         out_specs=full((GROUPS, Q, 128)),
         out_shape=jax.ShapeDtypeStruct((GROUPS, Q, 128), BF16),
         scratch_shapes=[
@@ -319,10 +301,10 @@
     )(pos, rows, *pieces, rate)
 
 
-def rates(pos, rows, summed, fixed, pieces, rate):
+def rates(pos, rows, summed, pieces, rate):
     return pl.pallas_call(
         rate_kernel,
-        in_specs=[SMEM, full(rows.shape), full(summed.shape), full(fixed.shape), HBM, HBM, HBM, HBM, HBM, full(rate.shape)],
+        in_specs=[SMEM, full(rows.shape), full(summed.shape), HBM, HBM, HBM, HBM, HBM, full(rate.shape)],
         out_specs=full((8, 128)),
         out_shape=jax.ShapeDtypeStruct((8, 128), F32),
         scratch_shapes=[
@@ -333,7 +315,7 @@
         ],
         name="rates",
         cost_estimate=pl.CostEstimate(flops=2_000_000_000, transcendentals=1_000_000, bytes_accessed=5_000_000),
-    )(pos, rows, summed, fixed, *pieces, rate)
+    )(pos, rows, summed, *pieces, rate)
 
 
 def gather_line(input_map, output_map):
@@ -361,13 +343,12 @@
     rate = jnp.repeat(own, HEAD, axis=1)
 
     line = gather_line(input_map[0], output_map[0])
-    packed = pack(cotangent[0], step_size[0], forget)
+    packed = pack(cotangent[0], fixed_point[0], step_size[0], forget)
     pieces = gather_plane(line)
     rows = lax.all_to_all(packed, SEQ, split_axis=0, concat_axis=0, tiled=True)
-    fixed = lax.all_to_all(split(fixed_point[0]), SEQ, split_axis=0, concat_axis=0, tiled=True)
     summed = series(pos, rows, pieces, rate)
     result = lax.all_to_all(summed, SEQ, split_axis=0, concat_axis=0, tiled=True)
-    totals = rates(pos, rows, summed, fixed, pieces, rate)
+    totals = rates(pos, rows, summed, pieces, rate)
     for axis in BATCH:
         bit = 1
         while bit < lax.axis_size(axis):

time: 194 us -> 191 us (0.985)
  starting transfers between devices: 45.2 us -> 39.1 us
  local copies, waits for them, and re-layouts: 4.13 us -> 8 us
    all_to_all x1, waiting for transfers between devices: 27.7 us -> 0.01 us  [inner(): rows = lax.all_to_all(packed, SEQ, split_axis=0, concat_axis=0, tiled=True)]
    ppermute x9, waiting for transfers between devices: 36.3 us -> 62.2 us  [shifted(): return lax.ppermute(x, axis, [(i, (i + by) % size) for i in range(size)])]
    all_to_all x1 -> x0, starting transfers between devices: 5.25 us -> none  [inner(): lax.all_to_all(split(fixed_point[0]), SEQ, split_axis=0, concat_axis=0, t...]
    unnamed x26 -> x20, local copies, waits for them, and re-layouts: 2.73 us -> 4.96 us
    pallas_call x2 -> x1, Pallas kernels: 12.4 us -> 10.2 us  [series(): pl.pallas_call(series_kernel, grid=(1,), in_specs=[SMEM, full((GROUPS, Q...]
  transfers between devices with their start and end apart: 15 -> 14, of which waited for: 11 -> 10; matrix products, arithmetic and copies ran while one was open for 1% -> 4% of each run, Pallas kernels for 6% -> 0%
where the time goes in v6:
time: 191 us; the launch traced here: 190 us
  waiting for transfers between devices  95.1 us (50%)
  starting transfers between devices  39.1 us (20%)
  Pallas kernels  24.9 us (13%)
  blocking collectives  19.6 us (10%)
  local copies, waits for them, and re-layouts  8 us (4%)
  other arithmetic  1.96 us (1%)
    ppermute x9, waiting for transfers between devices, shifted(): return lax.ppermute(x, axis, [(i, (i + by) % size) for i in range(size)])  62.2 us
    all_to_all x1, waiting for transfers between devices, inner(): lax.all_to_all(summed, SEQ, split_axis=0, concat_axis=0, tiled=True)  27.3 us
    all_to_all x1, blocking collectives, inner(): lax.all_to_all(copies, SEQ, split_axis=0, concat_axis=0, tiled=True)  19.6 us
    ppermute x9, starting transfers between devices, shifted(): return lax.ppermute(x, axis, [(i, (i + by) % size) for i in range(size)])  18.2 us
    all_to_all x1, starting transfers between devices, inner(): rows = lax.all_to_all(packed, SEQ, split_axis=0, concat_axis=0, tiled=True)  11.4 us
    pallas_call x1, Pallas kernels, series(): pl.pallas_call(series_kernel, grid=(1,), in_specs=[SMEM, full((GROUPS, Q...  10.2 us
    pallas_call x1, Pallas kernels, rates(): pl.pallas_call(rate_kernel, in_specs=[SMEM, full(rows.shape), full(summed...  8.84 us
    ppermute x3, waiting for transfers between devices, swapped(): return lax.ppermute(x, axis, [(i, i ^ bit) for i in range(size)])  5.57 us
  transfers between devices with their start and end apart: 14, of which 10 were waited for; matrix products, arithmetic and copies ran while one was open for 4% of the time, Pallas kernels for 0%

profile of v6, /device:TPU:32, one launch (start us, length us, event | category | flops | bytes accessed | tf_op | source)
XLA Modules:
  0.0 189.5 jit_solution(2461676895701500046)
XLA Ops:
  0.6 3.7 %pack.1 = bf16[32,264,128]{2,1,0:T(8,128)(2,1)} custom-call(f32[64,128]{1,0:T(8,128)} %bitcast.27, f32[1,128]{1,0:T(1,128)} %forget_ref.1, bf16[128,4096]{1,0:T(8,128)(2,1)} %bitcast.19, bf16[128,4096]{1,0:T(8,128)(2,1)} %bitcast.20), custom_call_target="tpu_custom_call" | custom-call | tf_op jit(solution)/shard_map/pack/pallas_call | solution.py:70
  4.3 11.4 %all-to-all-start = ((bf16[32,264,128]{2,1,0:T(8,128)(2,1)}), bf16[32,264,128]{2,1,0:T(8,128)(2,1)S(1)}, u32[]{:S(2)}, u32[]{:S(2)}) async-start(bf16[32,264,128]{2,1,0:T(8,128)(2,1)} %pack.1), calls=%async_computation | async-start | bytes 4325376 | tf_op jit(solution)/shard_map/all_to_all | solution.py:348
  15.8 1.5 collective-permute-start.3
  17.9 4.5 %collective-permute-start.2 = (bf16[1,256,128]{2,1,0:T(8,128)(2,1)S(1)}, bf16[1,256,128]{2,1,0:T(8,128)(2,1)S(1)}, u32[]{:S(2)}, u32[]{:S(2)}) collective-permute-start(bf16[1,256,128]{2,1,0:T(8,128)(2,1)S(1)} %maximum_bitcast_fusion), channel_id=1, source_target_pairs={{0,4},{1,5},{2,6},{3,7},{4,0},{5,1},{6,2},{7,3},{8,12},{9,13},{10,... | collective-permute-start | bytes 196616 | tf_op jit(solution)/shard_map/ppermute | solution.py:28
  22.3 42.3 %collective-permute-done.3 = bf16[1,256,128]{2,1,0:T(8,128)(2,1)S(1)} collective-permute-done((bf16[1,256,128]{2,1,0:T(8,128)(2,1)S(1)}, bf16[1,256,128]{2,1,0:T(8,128)(2,1)S(1)}, u32[]{:S(2)}, u32[]{:S(2)}) %collective-permute-start.3) | collective-permute-done | bytes 65568 | tf_op jit(solution)/shard_map/ppermute | solution.py:28
  64.7 3.9 %collective-permute-start.1 = (bf16[2,256,128]{2,1,0:T(8,128)(2,1)S(1)}, bf16[2,256,128]{2,1,0:T(8,128)(2,1)S(1)}, u32[]{:S(2)}, u32[]{:S(2)}) collective-permute-start(bf16[2,256,128]{2,1,0:T(8,128)(2,1)S(1)} %get-tuple-element.4), channel_id=1, source_target_pairs={{0,6},{1,7},{2,0},{3,1},{4,2},{5,3},{6,4},{7,5},{8,14},{9,15},{10,... | collective-permute-start | bytes 393224 | tf_op jit(solution)/shard_map/ppermute | solution.py:28
  70.7 4.7 %collective-permute-done.1 = bf16[2,256,128]{2,1,0:T(8,128)(2,1)S(1)} collective-permute-done((bf16[2,256,128]{2,1,0:T(8,128)(2,1)S(1)}, bf16[2,256,128]{2,1,0:T(8,128)(2,1)S(1)}, u32[]{:S(2)}, u32[]{:S(2)}) %collective-permute-start.1) | collective-permute-done | bytes 131104 | tf_op jit(solution)/shard_map/ppermute | solution.py:28
  76.7 1.6 collective-permute-done.4
  80.7 2.2 %collective-permute-start.5 = (bf16[8,256,128]{2,1,0:T(8,128)(2,1)}, bf16[8,256,128]{2,1,0:T(8,128)(2,1)}, u32[]{:S(2)}, u32[]{:S(2)}) collective-permute-start(bf16[8,256,128]{2,1,0:T(8,128)(2,1)} %constant_dynamic-update-slice_fusion.p0), channel_id=1, source_target_pairs={{0,24},{8,0},{16,8},{24,16},{1,25},{9,1},{17,9},{25,17},{2,26},{10... | collective-permute-start | bytes 1572872 | tf_op jit(solution)/shard_map/ppermute | solution.py:28
  82.9 11.1 %collective-permute-done.6.p2 = bf16[8,256,128]{2,1,0:T(8,128)(2,1)S(1)} collective-permute-done((bf16[8,256,128]{2,1,0:T(8,128)(2,1)}, bf16[8,256,128]{2,1,0:T(8,128)(2,1)S(1)}, u32[]{:S(2)}, u32[]{:S(2)}) %collective-permute-start.6) | collective-permute-done | bytes 524320 | tf_op jit(solution)/shard_map/ppermute | solution.py:28
  95.2 3.4 %collective-permute-start.8 = (bf16[4,256,128]{2,1,0:T(8,128)(2,1)S(1)}, bf16[4,256,128]{2,1,0:T(8,128)(2,1)}, u32[]{:S(2)}, u32[]{:S(2)}) collective-permute-start(bf16[4,256,128]{2,1,0:T(8,128)(2,1)S(1)} %slice.24), channel_id=1, source_target_pairs={{0,24},{8,0},{16,8},{24,16},{1,25},{9,1},{17,9},{25,17},{2,26},{10... | collective-permute-start | bytes 786440 | tf_op jit(solution)/shard_map/ppermute | solution.py:28
  99.9 1.7 collective-permute-done.7.p3
  102.4 1.4 copy-done.1
  103.8 10.2 %series.1.sum_ref = bf16[32,128,128]{2,1,0:T(8,128)(2,1)} custom-call(s32[2]{0:T(128)} %pad_add_fusion.pos_ref, bf16[32,264,128]{2,1,0:T(8,128)(2,1)} %copy-done.1, bf16[8,256,128]{2,1,0:T(8,128)(2,1)} %constant_dynamic-update-slice_fusion.p0, bf16[8,256,128]{2,1,0:T(8,128)(2,1)} %collective-permute-done.5.p1, bf16[8,256,128]{2,1,0:T(8,128)(2,1)} %copy-done.2, ...), custom_call_target="tpu_custom_call" | custom-call | flops 3000000000 | bytes 5000000 | tf_op jit(solution)/shard_map/series/pallas_call | solution.py:286
  114.0 8.8 %rates.1 = f32[8,128]{1,0:T(8,128)} custom-call(s32[2]{0:T(128)} %pad_add_fusion.pos_ref, bf16[32,264,128]{2,1,0:T(8,128)(2,1)} %copy-done.1, bf16[32,128,128]{2,1,0:T(8,128)(2,1)} %series.1.sum_ref, bf16[8,256,128]{2,1,0:T(8,128)(2,1)} %constant_dynamic-update-slice_fusion.p0, bf16[8,256,128]{2,1,0:T(8,128)(2,1)} %collective-permute-done.5.p1, ...), custom_call_target="tpu_custom_call" | custom-call | flops 2000000000 | bytes 5000000 | tf_op jit(solution)/shard_map/rates/pallas_call | solution.py:305
  122.9 1.6 collective-permute-start.9
  124.5 2.3 %collective-permute-done.9 = f32[8,128]{1,0:T(8,128)S(1)} collective-permute-done((f32[8,128]{1,0:T(8,128)}, f32[8,128]{1,0:T(8,128)S(1)}, u32[]{:S(2)}, u32[]{:S(2)}) %collective-permute-start.9) | collective-permute-done | bytes 4128 | tf_op jit(solution)/shard_map/ppermute | solution.py:33
  127.5 3.0 %collective-permute-start.10 = (f32[8,128]{1,0:T(8,128)S(1)}, f32[8,128]{1,0:T(8,128)S(1)}, u32[]{:S(2)}, u32[]{:S(2)}) collective-permute-start(f32[8,128]{1,0:T(8,128)S(1)} %add.18), channel_id=1, source_target_pairs={{0,128},{64,192},{128,0},{192,64},{1,129},{65,193},{129,1},{193,65... | collective-permute-start | bytes 12296 | tf_op jit(solution)/shard_map/ppermute | solution.py:33
  130.5 2.1 %collective-permute-done.10 = f32[8,128]{1,0:T(8,128)S(1)} collective-permute-done((f32[8,128]{1,0:T(8,128)S(1)}, f32[8,128]{1,0:T(8,128)S(1)}, u32[]{:S(2)}, u32[]{:S(2)}) %collective-permute-start.10) | collective-permute-done | bytes 4128 | tf_op jit(solution)/shard_map/ppermute | solution.py:33
  132.6 1.2 collective-permute-done.11
  133.8 19.6 %all_to_all.15 = f32[32,1,128]{2,1,0:T(1,128)S(1)} all-to-all(f32[32,1,128]{2,1,0:T(1,128)S(1)} %broadcast_in_dim.15), channel_id=1, replica_groups=mesh['batch_0'=4,'batch_1'=2,'seq_0'=4,'seq_1'=8] {'seq_0','seq_1'}, dimensions={0} | all-to-all | bytes 32768 | tf_op jit(solution)/shard_map/all_to_all | solution.py:358
  153.3 5.0 %all-to-all-start.1 = ((bf16[32,128,128]{2,1,0:T(8,128)(2,1)}), bf16[32,128,128]{2,1,0:T(8,128)(2,1)S(1)}, u32[]{:S(2)}, u32[]{:S(2)}) async-start(bf16[32,128,128]{2,1,0:T(8,128)(2,1)} %series.1.sum_ref), calls=%async_computation.1 | async-start | bytes 2097152 | tf_op jit(solution)/shard_map/all_to_all | solution.py:350
  158.9 27.3 %all-to-all-done.1.in_ref = bf16[32,128,128]{2,1,0:T(8,128)(2,1)S(1)} async-done(((bf16[32,128,128]{2,1,0:T(8,128)(2,1)}), bf16[32,128,128]{2,1,0:T(8,128)(2,1)S(1)}, u32[]{:S(2)}, u32[]{:S(2)}) %all-to-all-start.1) | async-done | bytes 1048608 | tf_op jit(solution)/shard_map/all_to_all | solution.py:350
  187.2 2.2 %join.1 = bf16[128,4096]{1,0:T(8,128)(2,1)} custom-call(bf16[32,128,128]{2,1,0:T(8,128)(2,1)} %copy-done), custom_call_target="tpu_custom_call" | custom-call | tf_op jit(solution)/shard_map/join/pallas_call | solution.py:91
  (48 shorter events, 12.0 us)
Async XLA Ops:
  4.3 11.4 %copy-start.3 = (bf16[1,128,128]{2,1,0:T(8,128)(2,1)S(1)}, bf16[1,128,128]{2,1,0:T(8,128)(2,1)}, u32[]{:S(2)}) copy-start(bf16[1,128,128]{2,1,0:T(8,128)(2,1)} %param.11) | copy-start | bytes 98308
  4.3 11.4 %copy-start.4 = (bf16[1,128,128]{2,1,0:T(8,128)(2,1)S(1)}, bf16[1,128,128]{2,1,0:T(8,128)(2,1)}, u32[]{:S(2)}) copy-start(bf16[1,128,128]{2,1,0:T(8,128)(2,1)} %param.10) | copy-start | bytes 98308
  4.3 98.1 %all-to-all-start = ((bf16[32,264,128]{2,1,0:T(8,128)(2,1)}), bf16[32,264,128]{2,1,0:T(8,128)(2,1)S(1)}, u32[]{:S(2)}, u32[]{:S(2)}) async-start(bf16[32,264,128]{2,1,0:T(8,128)(2,1)} %pack.1), calls=%async_computation | async-start | bytes 4325376 | tf_op jit(solution)/shard_map/all_to_all | solution.py:348
  15.7 82.8 %copy-start.5 = (f32[64]{0:T(128)S(1)}, f32[64]{0:T(128)}, u32[]{:S(2)}) copy-start(f32[64]{0:T(128)} %param.15) | copy-start | bytes 772
  15.7 82.8 %copy-start.6 = (f32[64]{0:T(128)S(1)}, f32[64]{0:T(128)}, u32[]{:S(2)}) copy-start(f32[64]{0:T(128)} %param.14) | copy-start | bytes 772
  15.8 48.9 %collective-permute-start.3 = (bf16[1,256,128]{2,1,0:T(8,128)(2,1)S(1)}, bf16[1,256,128]{2,1,0:T(8,128)(2,1)S(1)}, u32[]{:S(2)}, u32[]{:S(2)}) collective-permute-start(bf16[1,256,128]{2,1,0:T(8,128)(2,1)S(1)} %maximum_bitcast_fusion), channel_id=1, source_target_pairs={{0,1},{1,2},{2,3},{3,4},{4,5},{5,6},{6,7},{7,0},{8,9},{9,10},{10,1... | collective-permute-start | bytes 196616 | tf_op jit(solution)/shard_map/ppermute | solution.py:28
  17.3 47.4 %collective-permute-start = (bf16[1,256,128]{2,1,0:T(8,128)(2,1)S(1)}, bf16[1,256,128]{2,1,0:T(8,128)(2,1)S(1)}, u32[]{:S(2)}, u32[]{:S(2)}) collective-permute-start(bf16[1,256,128]{2,1,0:T(8,128)(2,1)S(1)} %maximum_bitcast_fusion), channel_id=1, source_target_pairs={{0,7},{1,0},{2,1},{3,2},{4,3},{5,4},{6,5},{7,6},{8,15},{9,8},{10,9... | collective-permute-start | bytes 196616 | tf_op jit(solution)/shard_map/ppermute | solution.py:28
  17.9 58.3 %collective-permute-start.2 = (bf16[1,256,128]{2,1,0:T(8,128)(2,1)S(1)}, bf16[1,256,128]{2,1,0:T(8,128)(2,1)S(1)}, u32[]{:S(2)}, u32[]{:S(2)}) collective-permute-start(bf16[1,256,128]{2,1,0:T(8,128)(2,1)S(1)} %maximum_bitcast_fusion), channel_id=1, source_target_pairs={{0,4},{1,5},{2,6},{3,7},{4,0},{5,1},{6,2},{7,3},{8,12},{9,13},{10,... | collective-permute-start | bytes 196616 | tf_op jit(solution)/shard_map/ppermute | solution.py:28
  64.7 10.7 %collective-permute-start.1 = (bf16[2,256,128]{2,1,0:T(8,128)(2,1)S(1)}, bf16[2,256,128]{2,1,0:T(8,128)(2,1)S(1)}, u32[]{:S(2)}, u32[]{:S(2)}) collective-permute-start(bf16[2,256,128]{2,1,0:T(8,128)(2,1)S(1)} %get-tuple-element.4), channel_id=1, source_target_pairs={{0,6},{1,7},{2,0},{3,1},{4,2},{5,3},{6,4},{7,5},{8,14},{9,15},{10,... | collective-permute-start | bytes 393224 | tf_op jit(solution)/shard_map/ppermute | solution.py:28
  69.3 9.1 %collective-permute-start.4 = (bf16[2,256,128]{2,1,0:T(8,128)(2,1)S(1)}, bf16[2,256,128]{2,1,0:T(8,128)(2,1)S(1)}, u32[]{:S(2)}, u32[]{:S(2)}) collective-permute-start(bf16[2,256,128]{2,1,0:T(8,128)(2,1)S(1)} %get-tuple-element.3), channel_id=1, source_target_pairs={{0,2},{1,3},{2,4},{3,5},{4,6},{5,7},{6,0},{7,1},{8,10},{9,11},{10,... | collective-permute-start | bytes 393224 | tf_op jit(solution)/shard_map/ppermute | solution.py:28
  79.6 14.3 %collective-permute-start.6 = (bf16[8,256,128]{2,1,0:T(8,128)(2,1)}, bf16[8,256,128]{2,1,0:T(8,128)(2,1)S(1)}, u32[]{:S(2)}, u32[]{:S(2)}) collective-permute-start(bf16[8,256,128]{2,1,0:T(8,128)(2,1)} %constant_dynamic-update-slice_fusion.p0), channel_id=1, source_target_pairs={{0,8},{8,16},{16,24},{24,0},{1,9},{9,17},{17,25},{25,1},{2,10},{10... | collective-permute-start | bytes 1572872 | tf_op jit(solution)/shard_map/ppermute | solution.py:28
  80.7 13.5 %collective-permute-start.5 = (bf16[8,256,128]{2,1,0:T(8,128)(2,1)}, bf16[8,256,128]{2,1,0:T(8,128)(2,1)}, u32[]{:S(2)}, u32[]{:S(2)}) collective-permute-start(bf16[8,256,128]{2,1,0:T(8,128)(2,1)} %constant_dynamic-update-slice_fusion.p0), channel_id=1, source_target_pairs={{0,24},{8,0},{16,8},{24,16},{1,25},{9,1},{17,9},{25,17},{2,26},{10... | collective-permute-start | bytes 1572872 | tf_op jit(solution)/shard_map/ppermute | solution.py:28
  94.0 8.5 %copy-start.2 = (bf16[8,256,128]{2,1,0:T(8,128)(2,1)}, bf16[8,256,128]{2,1,0:T(8,128)(2,1)S(1)}, u32[]{:S(2)}) copy-start(bf16[8,256,128]{2,1,0:T(8,128)(2,1)S(1)} %collective-permute-done.6.p2) | copy-start | bytes 1572868
  94.0 7.7 %collective-permute-start.7 = (bf16[4,256,128]{2,1,0:T(8,128)(2,1)S(1)}, bf16[4,256,128]{2,1,0:T(8,128)(2,1)S(1)}, u32[]{:S(2)}, u32[]{:S(2)}) collective-permute-start(bf16[4,256,128]{2,1,0:T(8,128)(2,1)S(1)} %slice.23), channel_id=1, source_target_pairs={{0,8},{8,16},{16,24},{24,0},{1,9},{9,17},{17,25},{25,1},{2,10},{10... | collective-permute-start | bytes 786440 | tf_op jit(solution)/shard_map/ppermute | solution.py:28
  95.2 7.3 %collective-permute-start.8 = (bf16[4,256,128]{2,1,0:T(8,128)(2,1)S(1)}, bf16[4,256,128]{2,1,0:T(8,128)(2,1)}, u32[]{:S(2)}, u32[]{:S(2)}) collective-permute-start(bf16[4,256,128]{2,1,0:T(8,128)(2,1)S(1)} %slice.24), channel_id=1, source_target_pairs={{0,24},{8,0},{16,8},{24,16},{1,25},{9,1},{17,9},{25,17},{2,26},{10... | collective-permute-start | bytes 786440 | tf_op jit(solution)/shard_map/ppermute | solution.py:28
  101.7 0.7 copy-start.7
  102.4 1.4 copy-start.1
  122.9 3.9 %collective-permute-start.9 = (f32[8,128]{1,0:T(8,128)}, f32[8,128]{1,0:T(8,128)S(1)}, u32[]{:S(2)}, u32[]{:S(2)}) collective-permute-start(f32[8,128]{1,0:T(8,128)} %rates.1), channel_id=1, source_target_pairs={{0,64},{64,0},{128,192},{192,128},{1,65},{65,1},{129,193},{193,129... | collective-permute-start | bytes 12296 | tf_op jit(solution)/shard_map/ppermute | solution.py:33
  127.5 5.1 %collective-permute-start.10 = (f32[8,128]{1,0:T(8,128)S(1)}, f32[8,128]{1,0:T(8,128)S(1)}, u32[]{:S(2)}, u32[]{:S(2)}) collective-permute-start(f32[8,128]{1,0:T(8,128)S(1)} %add.18), channel_id=1, source_target_pairs={{0,128},{64,192},{128,0},{192,64},{1,129},{65,193},{129,1},{193,65... | collective-permute-start | bytes 12296 | tf_op jit(solution)/shard_map/ppermute | solution.py:33
  132.6 1.2 collective-permute-start.11
  153.3 32.9 %all-to-all-start.1 = ((bf16[32,128,128]{2,1,0:T(8,128)(2,1)}), bf16[32,128,128]{2,1,0:T(8,128)(2,1)S(1)}, u32[]{:S(2)}, u32[]{:S(2)}) async-start(bf16[32,128,128]{2,1,0:T(8,128)(2,1)} %series.1.sum_ref), calls=%async_computation.1 | async-start | bytes 2097152 | tf_op jit(solution)/shard_map/all_to_all | solution.py:350
  186.2 1.0 copy-start

commit v7 on v6

--- a/solution.py
+++ b/solution.py
@@ -135,14 +135,39 @@
     return rows <= cols, lower, same
 
 
-def prepare(c, in_ref, maps_ref, rate_ref, consts, mat_ref, turn_ref, e_ref, g_ref, s_ref, m_ref):
-    upper, lower, same = consts
-    both = maps_ref[c]
-    b_rows, c_rows = both[:N], both[N:]
-    prod = dot_t(jnp.concatenate([b_rows, same], axis=0), c_rows)
-    mat_ref[c, :, :N] = jnp.where(upper, prod[:Q], 0.0).astype(BF16)
-    mat_ref[c, :, N:] = b_rows
-    turn_ref[c] = prod[Q:].astype(BF16)
+def tables_kernel(pos_ref, p0, p1, p2, p3, p4, mat_ref, turn_ref, maps_ref, sem):
+    fetch_maps(pos_ref, (p0, p1, p2, p3, p4), maps_ref, sem)
+    upper, _, same = constants()
+
+    def step(i, _):
+        for j in range(PREP):
+            c = i * PREP + j
+            both = maps_ref[c]
+            b_rows, c_rows = both[:N], both[N:]
+            prod = dot_t(jnp.concatenate([b_rows, same], axis=0), c_rows)
+            mat_ref[c, :, :N] = jnp.where(upper, prod[:Q], 0.0).astype(BF16)
+            mat_ref[c, :, N:] = b_rows
+            turn_ref[c] = prod[Q:].astype(BF16)
+        return 0
+
+    lax.fori_loop(0, GROUPS // PREP, step, 0)
+
+
+def tables(pos, pieces):
+    shapes = ((GROUPS, Q, 256), (GROUPS, N, Q))
+    return pl.pallas_call(
+        tables_kernel,
+        in_specs=[SMEM, HBM, HBM, HBM, HBM, HBM],
+        out_specs=[full(shape) for shape in shapes],
+        out_shape=[jax.ShapeDtypeStruct(shape, BF16) for shape in shapes],
+        scratch_shapes=[pltpu.VMEM((GROUPS, 2 * N, 128), BF16), pltpu.SemaphoreType.DMA],
+        name="tables",
+        cost_estimate=pl.CostEstimate(flops=300_000_000, transcendentals=0, bytes_accessed=5_000_000),
+    )(pos, *pieces)
+
+
+def prepare(c, in_ref, rate_ref, consts, e_ref, g_ref, s_ref, m_ref):
+    _, lower, same = consts
     rows = in_ref[c, Q : Q + EXTRA, :].astype(F32)
 
     def wide(first, second):
@@ -168,13 +193,12 @@
     m_ref[c] = jnp.broadcast_to(jnp.exp(middle), (8, 128))
 
 
-def series_kernel(pos_ref, in_ref, p0, p1, p2, p3, p4, rate_ref, out_ref, maps_ref, mat_ref, turn_ref, e_ref, g_ref, m_ref, v_ref, sum_ref, back_ref, sem):
-    fetch_maps(pos_ref, (p0, p1, p2, p3, p4), maps_ref, sem)
+def series_kernel(in_ref, mat_ref, turn_ref, rate_ref, out_ref, e_ref, g_ref, m_ref, v_ref, sum_ref, back_ref):
     consts = constants()
 
     def prep(i, _):
         for j in range(PREP):
-            prepare(i * PREP + j, in_ref, maps_ref, rate_ref, consts, mat_ref, turn_ref, e_ref, g_ref, None, m_ref)
+            prepare(i * PREP + j, in_ref, rate_ref, consts, e_ref, g_ref, None, m_ref)
         return 0
 
     lax.fori_loop(0, GROUPS // PREP, prep, 0)
@@ -214,13 +238,12 @@
         lax.fori_loop(0, GROUPS // UNROLL, step, 0)
 
 
-def rate_kernel(pos_ref, in_ref, sum_ref, p0, p1, p2, p3, p4, rate_ref, out_ref, maps_ref, mat_ref, turn_ref, e_ref, g_ref, s_ref, m_ref, back_ref, acc_ref, sem):
-    fetch_maps(pos_ref, (p0, p1, p2, p3, p4), maps_ref, sem)
+def rate_kernel(pos_ref, in_ref, sum_ref, mat_ref, turn_ref, rate_ref, out_ref, e_ref, g_ref, s_ref, m_ref, back_ref, acc_ref):
     consts = constants()
 
     def prep(i, _):
         for j in range(PREP):
-            prepare(i * PREP + j, in_ref, maps_ref, rate_ref, consts, mat_ref, turn_ref, e_ref, g_ref, s_ref, m_ref)
+            prepare(i * PREP + j, in_ref, rate_ref, consts, e_ref, g_ref, s_ref, m_ref)
         return 0
 
     lax.fori_loop(0, GROUPS // PREP, prep, 0)
@@ -269,62 +292,46 @@
     out_ref[...] = result
 
 
-def table_scratch(with_sums):
+def decay_scratch(with_sums):
     square = pltpu.VMEM((GROUPS, Q, 128), F32)
-    return [
-        pltpu.VMEM((GROUPS, 2 * N, 128), BF16),
-        pltpu.VMEM((GROUPS, Q, 256), BF16),
-        pltpu.VMEM((GROUPS, N, Q), BF16),
-        square,
-        square,
-        *([square] if with_sums else []),
-        pltpu.VMEM((GROUPS, 8, 128), F32),
-    ]
-
-
-def series(pos, rows, pieces, rate):
+    return [*[square] * (3 if with_sums else 2), pltpu.VMEM((GROUPS, 8, 128), F32)]
+
+
+def series(rows, mat, turn, rate):
     return pl.pallas_call(
         series_kernel,
-        grid=(1,),
-        in_specs=[SMEM, full((GROUPS, Q + EXTRA, 128)), HBM, HBM, HBM, HBM, HBM, full(rate.shape)],
+        in_specs=[full(rows.shape), full(mat.shape), full(turn.shape), full(rate.shape)],
         out_specs=full((GROUPS, Q, 128)),
         out_shape=jax.ShapeDtypeStruct((GROUPS, Q, 128), BF16),
         scratch_shapes=[
-            *table_scratch(False),
+            *decay_scratch(False),
             pltpu.VMEM((GROUPS, Q, 128), BF16),
             pltpu.VMEM((GROUPS, Q, 128), F32),
             pltpu.VMEM((N, 128), F32),
-            pltpu.SemaphoreType.DMA,
         ],
         name="series",
         cost_estimate=pl.CostEstimate(flops=3_000_000_000, transcendentals=1_000_000, bytes_accessed=5_000_000),
-    )(pos, rows, *pieces, rate)
-
-
-def rates(pos, rows, summed, pieces, rate):
+    )(rows, mat, turn, rate)
+
+
+def rates(pos, rows, summed, mat, turn, rate):
     return pl.pallas_call(
         rate_kernel,
-        in_specs=[SMEM, full(rows.shape), full(summed.shape), HBM, HBM, HBM, HBM, HBM, full(rate.shape)],
+        in_specs=[SMEM, full(rows.shape), full(summed.shape), full(mat.shape), full(turn.shape), full(rate.shape)],
         out_specs=full((8, 128)),
         out_shape=jax.ShapeDtypeStruct((8, 128), F32),
-        scratch_shapes=[
-            *table_scratch(True),
-            pltpu.VMEM((N, 256), F32),
-            pltpu.VMEM((2, 8, 128), F32),
-            pltpu.SemaphoreType.DMA,
-        ],
+        scratch_shapes=[*decay_scratch(True), pltpu.VMEM((N, 256), F32), pltpu.VMEM((2, 8, 128), F32)],
         name="rates",
         cost_estimate=pl.CostEstimate(flops=2_000_000_000, transcendentals=1_000_000, bytes_accessed=5_000_000),
-    )(pos, rows, summed, *pieces, rate)
+    )(pos, rows, summed, mat, turn, rate)
 
 
 def gather_line(input_map, output_map):
     own = jnp.concatenate([input_map, output_map], axis=0)[None]
     last, after = shifted(own, "seq_1", 1), shifted(own, "seq_1", -1)
-    far_last = shifted(jnp.concatenate([last, own]), "seq_1", 2)
-    far_after = shifted(jnp.concatenate([own, after]), "seq_1", -2)
-    far = shifted(own, "seq_1", 4)
-    return jnp.concatenate([own, after, far_after, far, far_last, last])
+    far_last = shifted(jnp.concatenate([last, own, after]), "seq_1", 3)
+    far_after = shifted(jnp.concatenate([last, own]), "seq_1", -3)
+    return jnp.concatenate([own, after, far_after, far_last, last])
 
 
 def gather_plane(line):
@@ -346,9 +353,10 @@
     packed = pack(cotangent[0], fixed_point[0], step_size[0], forget)
     pieces = gather_plane(line)
     rows = lax.all_to_all(packed, SEQ, split_axis=0, concat_axis=0, tiled=True)
-    summed = series(pos, rows, pieces, rate)
+    mat, turn = tables(pos, pieces)
+    summed = series(rows, mat, turn, rate)
     result = lax.all_to_all(summed, SEQ, split_axis=0, concat_axis=0, tiled=True)
-    totals = rates(pos, rows, summed, pieces, rate)
+    totals = rates(pos, rows, summed, mat, turn, rate)
     for axis in BATCH:
         bit = 1
         while bit < lax.axis_size(axis):

time: 191 us -> 198 us (1.037)
  waiting for transfers between devices: 95.1 us -> 102 us
  Pallas kernels: 24.9 us -> 27.7 us
    ppermute x9 -> x8, waiting for transfers between devices: 62.2 us -> 69.4 us  [shifted(): return lax.ppermute(x, axis, [(i, (i + by) % size) for i in range(size)])]
    pallas_call x1 -> x2, Pallas kernels: 10.2 us -> 14.2 us  [the longest x1 9.39 us: series(): pl.pallas_call(series_kernel, in_specs=[full(rows.shape), full(mat.shape)...]
    ppermute x9 -> x8, starting transfers between devices: 18.2 us -> 16.9 us  [shifted(): return lax.ppermute(x, axis, [(i, (i + by) % size) for i in range(size)])]
    unnamed x20 -> x21, local copies, waits for them, and re-layouts: 4.96 us -> 4.67 us
  transfers between devices with their start and end apart: 14 -> 13, of which waited for: 10 -> 10; matrix products, arithmetic and copies ran while one was open for 4% -> 3% of each run, Pallas kernels for 0% -> 2%
where the time goes in v7:
time: 198 us; the launch traced here: 197 us
  waiting for transfers between devices  102 us (52%)
  starting transfers between devices  37.7 us (19%)
  Pallas kernels  27.7 us (14%)
  blocking collectives  18.5 us (9%)
  local copies, waits for them, and re-layouts  8.24 us (4%)
  other arithmetic  2.01 us (1%)
    ppermute x8, waiting for transfers between devices, shifted(): return lax.ppermute(x, axis, [(i, (i + by) % size) for i in range(size)])  69.4 us
    all_to_all x1, waiting for transfers between devices, inner(): lax.all_to_all(summed, SEQ, split_axis=0, concat_axis=0, tiled=True)  27.3 us
    all_to_all x1, blocking collectives, inner(): lax.all_to_all(copies, SEQ, split_axis=0, concat_axis=0, tiled=True)  18.5 us
    ppermute x8, starting transfers between devices, shifted(): return lax.ppermute(x, axis, [(i, (i + by) % size) for i in range(size)])  16.9 us
    all_to_all x1, starting transfers between devices, inner(): rows = lax.all_to_all(packed, SEQ, split_axis=0, concat_axis=0, tiled=True)  11.4 us
    pallas_call x1, Pallas kernels, series(): pl.pallas_call(series_kernel, in_specs=[full(rows.shape), full(mat.shape)...  9.39 us
    pallas_call x1, Pallas kernels, rates(): pl.pallas_call(rate_kernel, in_specs=[SMEM, full(rows.shape), full(summed...  7.68 us
    ppermute x3, waiting for transfers between devices, swapped(): return lax.ppermute(x, axis, [(i, i ^ bit) for i in range(size)])  5.58 us
  transfers between devices with their start and end apart: 13, of which 10 were waited for; matrix products, arithmetic and copies ran while one was open for 3% of the time, Pallas kernels for 2%

profile of v7, /device:TPU:32, one launch (start us, length us, event | category | flops | bytes accessed | tf_op | source)
XLA Modules:
  0.0 197.2 jit_solution(7077643669978780335)
XLA Ops:
  0.6 3.7 %pack.1 = bf16[32,264,128]{2,1,0:T(8,128)(2,1)} custom-call(f32[64,128]{1,0:T(8,128)} %bitcast.27, f32[1,128]{1,0:T(1,128)} %forget_ref.1, bf16[128,4096]{1,0:T(8,128)(2,1)} %bitcast.19, bf16[128,4096]{1,0:T(8,128)(2,1)} %bitcast.20), custom_call_target="tpu_custom_call" | custom-call | tf_op jit(solution)/shard_map/pack/pallas_call | solution.py:70
  4.3 11.4 %all-to-all-start = ((bf16[32,264,128]{2,1,0:T(8,128)(2,1)}), bf16[32,264,128]{2,1,0:T(8,128)(2,1)S(1)}, u32[]{:S(2)}, u32[]{:S(2)}) async-start(bf16[32,264,128]{2,1,0:T(8,128)(2,1)} %pack.1), calls=%async_computation | async-start | bytes 4325376 | tf_op jit(solution)/shard_map/all_to_all | solution.py:355
  15.8 1.5 collective-permute-start.1
  18.5 44.0 %collective-permute-done.1 = bf16[1,256,128]{2,1,0:T(8,128)(2,1)S(1)} collective-permute-done((bf16[1,256,128]{2,1,0:T(8,128)(2,1)S(1)}, bf16[1,256,128]{2,1,0:T(8,128)(2,1)S(1)}, u32[]{:S(2)}, u32[]{:S(2)}) %collective-permute-start.1) | collective-permute-done | bytes 65568 | tf_op jit(solution)/shard_map/ppermute | solution.py:28
  62.5 5.7 %collective-permute-start.2 = (bf16[2,256,128]{2,1,0:T(8,128)(2,1)S(1)}, bf16[2,256,128]{2,1,0:T(8,128)(2,1)S(1)}, u32[]{:S(2)}, u32[]{:S(2)}) collective-permute-start(bf16[2,256,128]{2,1,0:T(8,128)(2,1)S(1)} %pad_maximum_fusion.1), channel_id=1, source_target_pairs={{0,5},{1,6},{2,7},{3,0},{4,1},{5,2},{6,3},{7,4},{8,13},{9,14},{10,... | collective-permute-start | bytes 393224 | tf_op jit(solution)/shard_map/ppermute | solution.py:28
  69.6 3.4 %collective-permute-done.2 = bf16[2,256,128]{2,1,0:T(8,128)(2,1)S(1)} collective-permute-done((bf16[2,256,128]{2,1,0:T(8,128)(2,1)S(1)}, bf16[2,256,128]{2,1,0:T(8,128)(2,1)S(1)}, u32[]{:S(2)}, u32[]{:S(2)}) %collective-permute-start.2) | collective-permute-done | bytes 131104 | tf_op jit(solution)/shard_map/ppermute | solution.py:28
  73.6 8.7 %collective-permute-done.3 = bf16[3,256,128]{2,1,0:T(8,128)(2,1)S(1)} collective-permute-done((bf16[3,256,128]{2,1,0:T(8,128)(2,1)S(1)}, bf16[3,256,128]{2,1,0:T(8,128)(2,1)S(1)}, u32[]{:S(2)}, u32[]{:S(2)}) %collective-permute-start.3) | collective-permute-done | bytes 196640 | tf_op jit(solution)/shard_map/ppermute | solution.py:28
  83.7 3.8 %collective-permute-start.5 = (bf16[8,256,128]{2,1,0:T(8,128)(2,1)}, bf16[8,256,128]{2,1,0:T(8,128)(2,1)S(1)}, u32[]{:S(2)}, u32[]{:S(2)}) collective-permute-start(bf16[8,256,128]{2,1,0:T(8,128)(2,1)} %constant_dynamic-update-slice_fusion.p0), channel_id=1, source_target_pairs={{0,8},{8,16},{16,24},{24,0},{1,9},{9,17},{17,25},{25,1},{2,10},{10... | collective-permute-start | bytes 1572872 | tf_op jit(solution)/shard_map/ppermute | solution.py:28
  87.5 1.3 collective-permute-start.4
  88.8 10.5 %collective-permute-done.5.p2 = bf16[8,256,128]{2,1,0:T(8,128)(2,1)S(1)} collective-permute-done((bf16[8,256,128]{2,1,0:T(8,128)(2,1)}, bf16[8,256,128]{2,1,0:T(8,128)(2,1)S(1)}, u32[]{:S(2)}, u32[]{:S(2)}) %collective-permute-start.5) | collective-permute-done | bytes 524320 | tf_op jit(solution)/shard_map/ppermute | solution.py:28
  101.3 2.8 %collective-permute-start.7 = (bf16[4,256,128]{2,1,0:T(8,128)(2,1)}, bf16[4,256,128]{2,1,0:T(8,128)(2,1)}, u32[]{:S(2)}, u32[]{:S(2)}) collective-permute-start(bf16[4,256,128]{2,1,0:T(8,128)(2,1)} %slice.24), channel_id=1, source_target_pairs={{0,24},{8,0},{16,8},{24,16},{1,25},{9,1},{17,9},{25,17},{2,26},{10... | collective-permute-start | bytes 786440 | tf_op jit(solution)/shard_map/ppermute | solution.py:28
  105.6 2.3 %collective-permute-done.6.p3 = bf16[4,256,128]{2,1,0:T(8,128)(2,1)S(1)} collective-permute-done((bf16[4,256,128]{2,1,0:T(8,128)(2,1)}, bf16[4,256,128]{2,1,0:T(8,128)(2,1)S(1)}, u32[]{:S(2)}, u32[]{:S(2)}) %collective-permute-start.6) | collective-permute-done | bytes 262176 | tf_op jit(solution)/shard_map/ppermute | solution.py:28
  108.6 4.8 %tables.1 = (bf16[32,128,256]{2,1,0:T(8,128)(2,1)}, bf16[32,128,128]{2,1,0:T(8,128)(2,1)}) custom-call(s32[2]{0:T(128)} %pad_add_fusion.pos_ref, bf16[8,256,128]{2,1,0:T(8,128)(2,1)} %constant_dynamic-update-slice_fusion.p0, bf16[8,256,128]{2,1,0:T(8,128)(2,1)} %copy-done.3, bf16[8,256,128]{2,1,0:T(8,128)(2,1)} %copy-done.2, bf16[4,256,128]{2,1,0:T(8,128)(2,1)} %copy-done.4, ...), custom_call_target="tpu_custom_call" | custom-call | flops 300000000 | bytes 5000000 | tf_op jit(solution)/shard_map/tables/pallas_call | solution.py:158
  113.4 1.4 copy-done.1
  114.8 9.4 %series.1.sum_ref = bf16[32,128,128]{2,1,0:T(8,128)(2,1)} custom-call(bf16[32,264,128]{2,1,0:T(8,128)(2,1)} %copy-done.1, bf16[32,128,256]{2,1,0:T(8,128)(2,1)} %get-tuple-element.5.mat_ref, bf16[32,128,128]{2,1,0:T(8,128)(2,1)} %get-tuple-element.6.turn_ref, f32[2,128]{1,0:T(2,128)} %reshape.10.rate_ref), custom_call_target="tpu_custom_call" | custom-call | flops 3000000000 | bytes 5000000 | tf_op jit(solution)/shard_map/series/pallas_call | solution.py:301
  124.2 7.7 %rates.1 = f32[8,128]{1,0:T(8,128)} custom-call(s32[2]{0:T(128)} %pad_add_fusion.pos_ref, bf16[32,264,128]{2,1,0:T(8,128)(2,1)} %copy-done.1, bf16[32,128,128]{2,1,0:T(8,128)(2,1)} %series.1.sum_ref, bf16[32,128,256]{2,1,0:T(8,128)(2,1)} %get-tuple-element.5.mat_ref, bf16[32,128,128]{2,1,0:T(8,128)(2,1)} %get-tuple-element.6.turn_ref, f32[2,128]{1,0:T(2,128)} %reshape.10.rate_ref), custom_call_target="tpu_custom_call" | custom-call | flops 2000000000 | bytes 5000000 | tf_op jit(solution)/shard_map/rates/pallas_call | solution.py:318
  131.9 1.5 collective-permute-start.8
  133.4 2.3 %collective-permute-done.8 = f32[8,128]{1,0:T(8,128)S(1)} collective-permute-done((f32[8,128]{1,0:T(8,128)}, f32[8,128]{1,0:T(8,128)S(1)}, u32[]{:S(2)}, u32[]{:S(2)}) %collective-permute-start.8) | collective-permute-done | bytes 4128 | tf_op jit(solution)/shard_map/ppermute | solution.py:33
  136.4 3.0 %collective-permute-start.9 = (f32[8,128]{1,0:T(8,128)S(1)}, f32[8,128]{1,0:T(8,128)S(1)}, u32[]{:S(2)}, u32[]{:S(2)}) collective-permute-start(f32[8,128]{1,0:T(8,128)S(1)} %add.18), channel_id=1, source_target_pairs={{0,128},{64,192},{128,0},{192,64},{1,129},{65,193},{129,1},{193,65... | collective-permute-start | bytes 12296 | tf_op jit(solution)/shard_map/ppermute | solution.py:33
  139.4 2.1 %collective-permute-done.9 = f32[8,128]{1,0:T(8,128)S(1)} collective-permute-done((f32[8,128]{1,0:T(8,128)S(1)}, f32[8,128]{1,0:T(8,128)S(1)}, u32[]{:S(2)}, u32[]{:S(2)}) %collective-permute-start.9) | collective-permute-done | bytes 4128 | tf_op jit(solution)/shard_map/ppermute | solution.py:33
  142.7 18.5 %all_to_all.15 = f32[32,1,128]{2,1,0:T(1,128)S(1)} all-to-all(f32[32,1,128]{2,1,0:T(1,128)S(1)} %broadcast_in_dim.15), channel_id=1, replica_groups=mesh['batch_0'=4,'batch_1'=2,'seq_0'=4,'seq_1'=8] {'seq_0','seq_1'}, dimensions={0} | all-to-all | bytes 32768 | tf_op jit(solution)/shard_map/all_to_all | solution.py:366
  161.1 5.0 %all-to-all-start.1 = ((bf16[32,128,128]{2,1,0:T(8,128)(2,1)}), bf16[32,128,128]{2,1,0:T(8,128)(2,1)S(1)}, u32[]{:S(2)}, u32[]{:S(2)}) async-start(bf16[32,128,128]{2,1,0:T(8,128)(2,1)} %series.1.sum_ref), calls=%async_computation.1 | async-start | bytes 2097152 | tf_op jit(solution)/shard_map/all_to_all | solution.py:358
  166.7 27.3 %all-to-all-done.1.in_ref = bf16[32,128,128]{2,1,0:T(8,128)(2,1)S(1)} async-done(((bf16[32,128,128]{2,1,0:T(8,128)(2,1)}), bf16[32,128,128]{2,1,0:T(8,128)(2,1)S(1)}, u32[]{:S(2)}, u32[]{:S(2)}) %all-to-all-start.1) | async-done | bytes 1048608 | tf_op jit(solution)/shard_map/all_to_all | solution.py:358
  195.0 2.2 %join.1 = bf16[128,4096]{1,0:T(8,128)(2,1)} custom-call(bf16[32,128,128]{2,1,0:T(8,128)(2,1)} %copy-done), custom_call_target="tpu_custom_call" | custom-call | tf_op jit(solution)/shard_map/join/pallas_call | solution.py:91
  (49 shorter events, 12.2 us)
Async XLA Ops:
  4.3 11.4 %copy-start.5 = (bf16[1,128,128]{2,1,0:T(8,128)(2,1)S(1)}, bf16[1,128,128]{2,1,0:T(8,128)(2,1)}, u32[]{:S(2)}) copy-start(bf16[1,128,128]{2,1,0:T(8,128)(2,1)} %param.11) | copy-start | bytes 98308
  4.3 11.4 %copy-start.6 = (bf16[1,128,128]{2,1,0:T(8,128)(2,1)S(1)}, bf16[1,128,128]{2,1,0:T(8,128)(2,1)}, u32[]{:S(2)}) copy-start(bf16[1,128,128]{2,1,0:T(8,128)(2,1)} %param.10) | copy-start | bytes 98308
  4.3 109.1 %all-to-all-start = ((bf16[32,264,128]{2,1,0:T(8,128)(2,1)}), bf16[32,264,128]{2,1,0:T(8,128)(2,1)S(1)}, u32[]{:S(2)}, u32[]{:S(2)}) async-start(bf16[32,264,128]{2,1,0:T(8,128)(2,1)} %pack.1), calls=%async_computation | async-start | bytes 4325376 | tf_op jit(solution)/shard_map/all_to_all | solution.py:355
  15.7 88.4 %copy-start.7 = (f32[64]{0:T(128)S(1)}, f32[64]{0:T(128)}, u32[]{:S(2)}) copy-start(f32[64]{0:T(128)} %param.15) | copy-start | bytes 772
  15.7 88.4 %copy-start.8 = (f32[64]{0:T(128)S(1)}, f32[64]{0:T(128)}, u32[]{:S(2)}) copy-start(f32[64]{0:T(128)} %param.14) | copy-start | bytes 772
  15.8 46.7 %collective-permute-start.1 = (bf16[1,256,128]{2,1,0:T(8,128)(2,1)S(1)}, bf16[1,256,128]{2,1,0:T(8,128)(2,1)S(1)}, u32[]{:S(2)}, u32[]{:S(2)}) collective-permute-start(bf16[1,256,128]{2,1,0:T(8,128)(2,1)S(1)} %maximum_bitcast_fusion), channel_id=1, source_target_pairs={{0,1},{1,2},{2,3},{3,4},{4,5},{5,6},{6,7},{7,0},{8,9},{9,10},{10,1... | collective-permute-start | bytes 196616 | tf_op jit(solution)/shard_map/ppermute | solution.py:28
  17.3 50.9 %collective-permute-start = (bf16[1,256,128]{2,1,0:T(8,128)(2,1)S(1)}, bf16[1,256,128]{2,1,0:T(8,128)(2,1)S(1)}, u32[]{:S(2)}, u32[]{:S(2)}) collective-permute-start(bf16[1,256,128]{2,1,0:T(8,128)(2,1)S(1)} %maximum_bitcast_fusion), channel_id=1, source_target_pairs={{0,7},{1,0},{2,1},{3,2},{4,3},{5,4},{6,5},{7,6},{8,15},{9,8},{10,9... | collective-permute-start | bytes 196616 | tf_op jit(solution)/shard_map/ppermute | solution.py:28
  62.5 10.5 %collective-permute-start.2 = (bf16[2,256,128]{2,1,0:T(8,128)(2,1)S(1)}, bf16[2,256,128]{2,1,0:T(8,128)(2,1)S(1)}, u32[]{:S(2)}, u32[]{:S(2)}) collective-permute-start(bf16[2,256,128]{2,1,0:T(8,128)(2,1)S(1)} %pad_maximum_fusion.1), channel_id=1, source_target_pairs={{0,5},{1,6},{2,7},{3,0},{4,1},{5,2},{6,3},{7,4},{8,13},{9,14},{10,... | collective-permute-start | bytes 393224 | tf_op jit(solution)/shard_map/ppermute | solution.py:28
  68.2 14.2 %collective-permute-start.3 = (bf16[3,256,128]{2,1,0:T(8,128)(2,1)S(1)}, bf16[3,256,128]{2,1,0:T(8,128)(2,1)S(1)}, u32[]{:S(2)}, u32[]{:S(2)}) collective-permute-start(bf16[3,256,128]{2,1,0:T(8,128)(2,1)S(1)} %pad_maximum_fusion), channel_id=1, source_target_pairs={{0,3},{1,4},{2,5},{3,6},{4,7},{5,0},{6,1},{7,2},{8,11},{9,12},{10,... | collective-permute-start | bytes 589832 | tf_op jit(solution)/shard_map/ppermute | solution.py:28
  83.7 15.6 %collective-permute-start.5 = (bf16[8,256,128]{2,1,0:T(8,128)(2,1)}, bf16[8,256,128]{2,1,0:T(8,128)(2,1)S(1)}, u32[]{:S(2)}, u32[]{:S(2)}) collective-permute-start(bf16[8,256,128]{2,1,0:T(8,128)(2,1)} %constant_dynamic-update-slice_fusion.p0), channel_id=1, source_target_pairs={{0,8},{8,16},{16,24},{24,0},{1,9},{9,17},{17,25},{25,1},{2,10},{10... | collective-permute-start | bytes 1572872 | tf_op jit(solution)/shard_map/ppermute | solution.py:28
  87.5 13.0 %collective-permute-start.4 = (bf16[8,256,128]{2,1,0:T(8,128)(2,1)}, bf16[8,256,128]{2,1,0:T(8,128)(2,1)S(1)}, u32[]{:S(2)}, u32[]{:S(2)}) collective-permute-start(bf16[8,256,128]{2,1,0:T(8,128)(2,1)} %constant_dynamic-update-slice_fusion.p0), channel_id=1, source_target_pairs={{0,24},{8,0},{16,8},{24,16},{1,25},{9,1},{17,9},{25,17},{2,26},{10... | collective-permute-start | bytes 1572872 | tf_op jit(solution)/shard_map/ppermute | solution.py:28
  99.3 9.0 %copy-start.2 = (bf16[8,256,128]{2,1,0:T(8,128)(2,1)}, bf16[8,256,128]{2,1,0:T(8,128)(2,1)S(1)}, u32[]{:S(2)}) copy-start(bf16[8,256,128]{2,1,0:T(8,128)(2,1)S(1)} %collective-permute-done.5.p2) | copy-start | bytes 1572868
  100.1 7.8 %collective-permute-start.6 = (bf16[4,256,128]{2,1,0:T(8,128)(2,1)}, bf16[4,256,128]{2,1,0:T(8,128)(2,1)S(1)}, u32[]{:S(2)}, u32[]{:S(2)}) collective-permute-start(bf16[4,256,128]{2,1,0:T(8,128)(2,1)} %slice.23), channel_id=1, source_target_pairs={{0,8},{8,16},{16,24},{24,0},{1,9},{9,17},{17,25},{25,1},{2,10},{10... | collective-permute-start | bytes 786440 | tf_op jit(solution)/shard_map/ppermute | solution.py:28
  100.6 7.8 %copy-start.3 = (bf16[8,256,128]{2,1,0:T(8,128)(2,1)}, bf16[8,256,128]{2,1,0:T(8,128)(2,1)S(1)}, u32[]{:S(2)}) copy-start(bf16[8,256,128]{2,1,0:T(8,128)(2,1)S(1)} %collective-permute-done.4.p1) | copy-start | bytes 1572868
  101.3 7.0 %collective-permute-start.7 = (bf16[4,256,128]{2,1,0:T(8,128)(2,1)}, bf16[4,256,128]{2,1,0:T(8,128)(2,1)}, u32[]{:S(2)}, u32[]{:S(2)}) collective-permute-start(bf16[4,256,128]{2,1,0:T(8,128)(2,1)} %slice.24), channel_id=1, source_target_pairs={{0,24},{8,0},{16,8},{24,16},{1,25},{9,1},{17,9},{25,17},{2,26},{10... | collective-permute-start | bytes 786440 | tf_op jit(solution)/shard_map/ppermute | solution.py:28
  107.9 0.7 copy-start.4
  113.4 1.4 copy-start.1
  131.9 3.8 %collective-permute-start.8 = (f32[8,128]{1,0:T(8,128)}, f32[8,128]{1,0:T(8,128)S(1)}, u32[]{:S(2)}, u32[]{:S(2)}) collective-permute-start(f32[8,128]{1,0:T(8,128)} %rates.1), channel_id=1, source_target_pairs={{0,64},{64,0},{128,192},{192,128},{1,65},{65,1},{129,193},{193,129... | collective-permute-start | bytes 12296 | tf_op jit(solution)/shard_map/ppermute | solution.py:33
  136.4 5.1 %collective-permute-start.9 = (f32[8,128]{1,0:T(8,128)S(1)}, f32[8,128]{1,0:T(8,128)S(1)}, u32[]{:S(2)}, u32[]{:S(2)}) collective-permute-start(f32[8,128]{1,0:T(8,128)S(1)} %add.18), channel_id=1, source_target_pairs={{0,128},{64,192},{128,0},{192,64},{1,129},{65,193},{129,1},{193,65... | collective-permute-start | bytes 12296 | tf_op jit(solution)/shard_map/ppermute | solution.py:33
  141.5 1.2 collective-permute-start.10
  161.1 32.9 %all-to-all-start.1 = ((bf16[32,128,128]{2,1,0:T(8,128)(2,1)}), bf16[32,128,128]{2,1,0:T(8,128)(2,1)S(1)}, u32[]{:S(2)}, u32[]{:S(2)}) async-start(bf16[32,128,128]{2,1,0:T(8,128)(2,1)} %series.1.sum_ref), calls=%async_computation.1 | async-start | bytes 2097152 | tf_op jit(solution)/shard_map/all_to_all | solution.py:358
  194.0 1.0 copy-start

commit v8 on v6

--- a/solution.py
+++ b/solution.py
@@ -46,23 +46,36 @@
     return high, (x - high.astype(F32)).astype(BF16)
 
 
-def pack_kernel(step_ref, forget_ref, cot_ref, fixed_ref, out_ref, sem):
-    copies = []
-    for j in range(GROUPS):
-        lanes = pl.ds(j * 128, 128)
-        copies.append(pltpu.make_async_copy(cot_ref.at[:, lanes], out_ref.at[j, pl.ds(0, Q), :], sem))
-        copies.append(pltpu.make_async_copy(fixed_ref.at[:, lanes], out_ref.at[j, pl.ds(Q + EXTRA, Q), :], sem))
-    for c in copies:
-        c.start()
+def pack_kernel(step_ref, forget_ref, cot_ref, fixed_ref, out_ref, rows_ref, in_sems, out_sems):
+    chunks = []
+    for i in range(4):
+        copies = []
+        for j in range(8 * i, 8 * i + 8):
+            lanes = pl.ds(j * 128, 128)
+            copies.append(pltpu.make_async_copy(cot_ref.at[:, lanes], rows_ref.at[j, pl.ds(0, Q), :], in_sems.at[i]))
+            copies.append(
+                pltpu.make_async_copy(fixed_ref.at[:, lanes], rows_ref.at[j, pl.ds(Q + EXTRA, Q), :], in_sems.at[i])
+            )
+        chunks.append(copies)
+    for copies in chunks:
+        for c in copies:
+            c.start()
     step_high, step_low = halves(step_ref[...])
     step_high, step_low = step_high.astype(F32), step_low.astype(F32)
     tail = [f.astype(F32) for f in halves(forget_ref[...])] + [jnp.zeros((2, Q), F32)]
     for j in range(GROUPS):
         two = slice(2 * j, 2 * j + 2)
         rows = jnp.concatenate([step_high[two], step_low[two], *tail], axis=0)
-        out_ref[j, Q : Q + EXTRA, :] = rows.astype(BF16)
-    for c in copies:
-        c.wait()
+        rows_ref[j, Q : Q + EXTRA, :] = rows.astype(BF16)
+    results = []
+    for i, copies in enumerate(chunks):
+        for c in copies:
+            c.wait()
+        part = pl.ds(8 * i, 8)
+        results.append(pltpu.make_async_copy(rows_ref.at[part], out_ref.at[part], out_sems.at[i]))
+        results[-1].start()
+    for r in results:
+        r.wait()
 
 
 def pack(cot, fixed, step, forget):
@@ -70,9 +83,13 @@
     return pl.pallas_call(
         pack_kernel,
         in_specs=[full(step.shape), full(forget.shape), HBM, HBM],
-        out_specs=full(shape),
+        out_specs=HBM,
         out_shape=jax.ShapeDtypeStruct(shape, BF16),
-        scratch_shapes=[pltpu.SemaphoreType.DMA],
+        scratch_shapes=[
+            pltpu.VMEM(shape, BF16),
+            pltpu.SemaphoreType.DMA((4,)),
+            pltpu.SemaphoreType.DMA((4,)),
+        ],
         name="pack",
     )(step, forget, cot, fixed)
 
@@ -155,9 +172,10 @@
     forgets = jnp.concatenate([wide(4, 4), wide(5, 5)], axis=1)
     lower_twice = jnp.concatenate([lower, lower], axis=1)
     same_twice = jnp.concatenate([same, same], axis=1)
-    sums = dot_t(jnp.concatenate([lower_twice, same_twice], axis=0), steps)
-    step_sum, step_col = sums[:Q], sums[Q:]
-    forget_sum = dot_t(lower_twice, forgets)
+    sums = dot_t(
+        jnp.concatenate([lower_twice, same_twice], axis=0), jnp.concatenate([steps, forgets], axis=0)
+    )
+    step_sum, step_col, forget_sum = sums[:Q, :128], sums[Q:, :128], sums[:Q, 128:]
     log_decay = -(rate_ref[0:1, :] * step_sum + forget_sum)
     middle = 0.5 * log_decay[Q - 1 : Q, :]
     gap = log_decay - middle

time: 191 us -> 190 us (level)
  no operation moved by 1% of the time
where the time goes in v8:
time: 190 us; the launch traced here: 189 us
  waiting for transfers between devices  95.1 us (50%)
  starting transfers between devices  39.1 us (21%)
  Pallas kernels  24 us (13%)
  blocking collectives  19.5 us (10%)
  local copies, waits for them, and re-layouts  8 us (4%)
  other arithmetic  1.96 us (1%)
    ppermute x9, waiting for transfers between devices, shifted(): return lax.ppermute(x, axis, [(i, (i + by) % size) for i in range(size)])  62.2 us
    all_to_all x1, waiting for transfers between devices, inner(): lax.all_to_all(summed, SEQ, split_axis=0, concat_axis=0, tiled=True)  27.3 us
    all_to_all x1, blocking collectives, inner(): lax.all_to_all(copies, SEQ, split_axis=0, concat_axis=0, tiled=True)  19.5 us
    ppermute x9, starting transfers between devices, shifted(): return lax.ppermute(x, axis, [(i, (i + by) % size) for i in range(size)])  18.2 us
    all_to_all x1, starting transfers between devices, inner(): rows = lax.all_to_all(packed, SEQ, split_axis=0, concat_axis=0, tiled=True)  11.4 us
    pallas_call x1, Pallas kernels, series(): pl.pallas_call(series_kernel, grid=(1,), in_specs=[SMEM, full((GROUPS, Q...  10 us
    pallas_call x1, Pallas kernels, rates(): pl.pallas_call(rate_kernel, in_specs=[SMEM, full(rows.shape), full(summed...  8.6 us
    ppermute x3, waiting for transfers between devices, swapped(): return lax.ppermute(x, axis, [(i, i ^ bit) for i in range(size)])  5.57 us
  transfers between devices with their start and end apart: 14, of which 10 were waited for; matrix products, arithmetic and copies ran while one was open for 4% of the time, Pallas kernels for 0%

profile of v8, /device:TPU:32, one launch (start us, length us, event | category | flops | bytes accessed | tf_op | source)
XLA Modules:
  0.0 188.6 jit_solution(12111858610695196852)
XLA Ops:
  0.6 3.2 %pack.1 = bf16[32,264,128]{2,1,0:T(8,128)(2,1)} custom-call(f32[64,128]{1,0:T(8,128)} %bitcast.27, f32[1,128]{1,0:T(1,128)} %forget_ref.1, bf16[128,4096]{1,0:T(8,128)(2,1)} %bitcast.19, bf16[128,4096]{1,0:T(8,128)(2,1)} %bitcast.20), custom_call_target="tpu_custom_call" | custom-call | tf_op jit(solution)/shard_map/pack/pallas_call | solution.py:83
  3.9 11.4 %all-to-all-start = ((bf16[32,264,128]{2,1,0:T(8,128)(2,1)}), bf16[32,264,128]{2,1,0:T(8,128)(2,1)S(1)}, u32[]{:S(2)}, u32[]{:S(2)}) async-start(bf16[32,264,128]{2,1,0:T(8,128)(2,1)} %pack.1), calls=%async_computation | async-start | bytes 4325376 | tf_op jit(solution)/shard_map/all_to_all | solution.py:366
  15.3 1.5 collective-permute-start.3
  17.4 4.5 %collective-permute-start.2 = (bf16[1,256,128]{2,1,0:T(8,128)(2,1)S(1)}, bf16[1,256,128]{2,1,0:T(8,128)(2,1)S(1)}, u32[]{:S(2)}, u32[]{:S(2)}) collective-permute-start(bf16[1,256,128]{2,1,0:T(8,128)(2,1)S(1)} %maximum_bitcast_fusion), channel_id=1, source_target_pairs={{0,4},{1,5},{2,6},{3,7},{4,0},{5,1},{6,2},{7,3},{8,12},{9,13},{10,... | collective-permute-start | bytes 196616 | tf_op jit(solution)/shard_map/ppermute | solution.py:28
  21.9 42.3 %collective-permute-done.3 = bf16[1,256,128]{2,1,0:T(8,128)(2,1)S(1)} collective-permute-done((bf16[1,256,128]{2,1,0:T(8,128)(2,1)S(1)}, bf16[1,256,128]{2,1,0:T(8,128)(2,1)S(1)}, u32[]{:S(2)}, u32[]{:S(2)}) %collective-permute-start.3) | collective-permute-done | bytes 65568 | tf_op jit(solution)/shard_map/ppermute | solution.py:28
  64.3 3.9 %collective-permute-start.1 = (bf16[2,256,128]{2,1,0:T(8,128)(2,1)S(1)}, bf16[2,256,128]{2,1,0:T(8,128)(2,1)S(1)}, u32[]{:S(2)}, u32[]{:S(2)}) collective-permute-start(bf16[2,256,128]{2,1,0:T(8,128)(2,1)S(1)} %get-tuple-element.4), channel_id=1, source_target_pairs={{0,6},{1,7},{2,0},{3,1},{4,2},{5,3},{6,4},{7,5},{8,14},{9,15},{10,... | collective-permute-start | bytes 393224 | tf_op jit(solution)/shard_map/ppermute | solution.py:28
  70.3 4.7 %collective-permute-done.1 = bf16[2,256,128]{2,1,0:T(8,128)(2,1)S(1)} collective-permute-done((bf16[2,256,128]{2,1,0:T(8,128)(2,1)S(1)}, bf16[2,256,128]{2,1,0:T(8,128)(2,1)S(1)}, u32[]{:S(2)}, u32[]{:S(2)}) %collective-permute-start.1) | collective-permute-done | bytes 131104 | tf_op jit(solution)/shard_map/ppermute | solution.py:28
  76.3 1.6 collective-permute-done.4
  80.3 2.2 %collective-permute-start.5 = (bf16[8,256,128]{2,1,0:T(8,128)(2,1)}, bf16[8,256,128]{2,1,0:T(8,128)(2,1)}, u32[]{:S(2)}, u32[]{:S(2)}) collective-permute-start(bf16[8,256,128]{2,1,0:T(8,128)(2,1)} %constant_dynamic-update-slice_fusion.p0), channel_id=1, source_target_pairs={{0,24},{8,0},{16,8},{24,16},{1,25},{9,1},{17,9},{25,17},{2,26},{10... | collective-permute-start | bytes 1572872 | tf_op jit(solution)/shard_map/ppermute | solution.py:28
  82.4 11.1 %collective-permute-done.6.p2 = bf16[8,256,128]{2,1,0:T(8,128)(2,1)S(1)} collective-permute-done((bf16[8,256,128]{2,1,0:T(8,128)(2,1)}, bf16[8,256,128]{2,1,0:T(8,128)(2,1)S(1)}, u32[]{:S(2)}, u32[]{:S(2)}) %collective-permute-start.6) | collective-permute-done | bytes 524320 | tf_op jit(solution)/shard_map/ppermute | solution.py:28
  94.7 3.4 %collective-permute-start.8 = (bf16[4,256,128]{2,1,0:T(8,128)(2,1)S(1)}, bf16[4,256,128]{2,1,0:T(8,128)(2,1)}, u32[]{:S(2)}, u32[]{:S(2)}) collective-permute-start(bf16[4,256,128]{2,1,0:T(8,128)(2,1)S(1)} %slice.24), channel_id=1, source_target_pairs={{0,24},{8,0},{16,8},{24,16},{1,25},{9,1},{17,9},{25,17},{2,26},{10... | collective-permute-start | bytes 786440 | tf_op jit(solution)/shard_map/ppermute | solution.py:28
  99.5 1.7 collective-permute-done.7.p3
  102.0 1.4 copy-done.1
  103.3 10.0 %series.1.sum_ref = bf16[32,128,128]{2,1,0:T(8,128)(2,1)} custom-call(s32[2]{0:T(128)} %pad_add_fusion.pos_ref, bf16[32,264,128]{2,1,0:T(8,128)(2,1)} %copy-done.1, bf16[8,256,128]{2,1,0:T(8,128)(2,1)} %constant_dynamic-update-slice_fusion.p0, bf16[8,256,128]{2,1,0:T(8,128)(2,1)} %collective-permute-done.5.p1, bf16[8,256,128]{2,1,0:T(8,128)(2,1)} %copy-done.2, ...), custom_call_target="tpu_custom_call" | custom-call | flops 3000000000 | bytes 5000000 | tf_op jit(solution)/shard_map/series/pallas_call | solution.py:304
  113.4 8.6 %rates.1 = f32[8,128]{1,0:T(8,128)} custom-call(s32[2]{0:T(128)} %pad_add_fusion.pos_ref, bf16[32,264,128]{2,1,0:T(8,128)(2,1)} %copy-done.1, bf16[32,128,128]{2,1,0:T(8,128)(2,1)} %series.1.sum_ref, bf16[8,256,128]{2,1,0:T(8,128)(2,1)} %constant_dynamic-update-slice_fusion.p0, bf16[8,256,128]{2,1,0:T(8,128)(2,1)} %collective-permute-done.5.p1, ...), custom_call_target="tpu_custom_call" | custom-call | flops 2000000000 | bytes 5000000 | tf_op jit(solution)/shard_map/rates/pallas_call | solution.py:323
  122.0 1.6 collective-permute-start.9
  123.6 2.3 %collective-permute-done.9 = f32[8,128]{1,0:T(8,128)S(1)} collective-permute-done((f32[8,128]{1,0:T(8,128)}, f32[8,128]{1,0:T(8,128)S(1)}, u32[]{:S(2)}, u32[]{:S(2)}) %collective-permute-start.9) | collective-permute-done | bytes 4128 | tf_op jit(solution)/shard_map/ppermute | solution.py:33
  126.6 3.0 %collective-permute-start.10 = (f32[8,128]{1,0:T(8,128)S(1)}, f32[8,128]{1,0:T(8,128)S(1)}, u32[]{:S(2)}, u32[]{:S(2)}) collective-permute-start(f32[8,128]{1,0:T(8,128)S(1)} %add.18), channel_id=1, source_target_pairs={{0,128},{64,192},{128,0},{192,64},{1,129},{65,193},{129,1},{193,65... | collective-permute-start | bytes 12296 | tf_op jit(solution)/shard_map/ppermute | solution.py:33
  129.6 2.1 %collective-permute-done.10 = f32[8,128]{1,0:T(8,128)S(1)} collective-permute-done((f32[8,128]{1,0:T(8,128)S(1)}, f32[8,128]{1,0:T(8,128)S(1)}, u32[]{:S(2)}, u32[]{:S(2)}) %collective-permute-start.10) | collective-permute-done | bytes 4128 | tf_op jit(solution)/shard_map/ppermute | solution.py:33
  131.7 1.2 collective-permute-done.11
  132.9 19.5 %all_to_all.15 = f32[32,1,128]{2,1,0:T(1,128)S(1)} all-to-all(f32[32,1,128]{2,1,0:T(1,128)S(1)} %broadcast_in_dim.15), channel_id=1, replica_groups=mesh['batch_0'=4,'batch_1'=2,'seq_0'=4,'seq_1'=8] {'seq_0','seq_1'}, dimensions={0} | all-to-all | bytes 32768 | tf_op jit(solution)/shard_map/all_to_all | solution.py:376
  152.4 5.0 %all-to-all-start.1 = ((bf16[32,128,128]{2,1,0:T(8,128)(2,1)}), bf16[32,128,128]{2,1,0:T(8,128)(2,1)S(1)}, u32[]{:S(2)}, u32[]{:S(2)}) async-start(bf16[32,128,128]{2,1,0:T(8,128)(2,1)} %series.1.sum_ref), calls=%async_computation.1 | async-start | bytes 2097152 | tf_op jit(solution)/shard_map/all_to_all | solution.py:368
  158.0 27.3 %all-to-all-done.1.in_ref = bf16[32,128,128]{2,1,0:T(8,128)(2,1)S(1)} async-done(((bf16[32,128,128]{2,1,0:T(8,128)(2,1)}), bf16[32,128,128]{2,1,0:T(8,128)(2,1)S(1)}, u32[]{:S(2)}, u32[]{:S(2)}) %all-to-all-start.1) | async-done | bytes 1048608 | tf_op jit(solution)/shard_map/all_to_all | solution.py:368
  186.3 2.2 %join.1 = bf16[128,4096]{1,0:T(8,128)(2,1)} custom-call(bf16[32,128,128]{2,1,0:T(8,128)(2,1)} %copy-done), custom_call_target="tpu_custom_call" | custom-call | tf_op jit(solution)/shard_map/join/pallas_call | solution.py:108
  (48 shorter events, 12.0 us)
Async XLA Ops:
  3.9 11.4 %copy-start.3 = (bf16[1,128,128]{2,1,0:T(8,128)(2,1)S(1)}, bf16[1,128,128]{2,1,0:T(8,128)(2,1)}, u32[]{:S(2)}) copy-start(bf16[1,128,128]{2,1,0:T(8,128)(2,1)} %param.11) | copy-start | bytes 98308
  3.9 11.4 %copy-start.4 = (bf16[1,128,128]{2,1,0:T(8,128)(2,1)S(1)}, bf16[1,128,128]{2,1,0:T(8,128)(2,1)}, u32[]{:S(2)}) copy-start(bf16[1,128,128]{2,1,0:T(8,128)(2,1)} %param.10) | copy-start | bytes 98308
  3.9 98.1 %all-to-all-start = ((bf16[32,264,128]{2,1,0:T(8,128)(2,1)}), bf16[32,264,128]{2,1,0:T(8,128)(2,1)S(1)}, u32[]{:S(2)}, u32[]{:S(2)}) async-start(bf16[32,264,128]{2,1,0:T(8,128)(2,1)} %pack.1), calls=%async_computation | async-start | bytes 4325376 | tf_op jit(solution)/shard_map/all_to_all | solution.py:366
  15.3 82.8 %copy-start.5 = (f32[64]{0:T(128)S(1)}, f32[64]{0:T(128)}, u32[]{:S(2)}) copy-start(f32[64]{0:T(128)} %param.15) | copy-start | bytes 772
  15.3 82.8 %copy-start.6 = (f32[64]{0:T(128)S(1)}, f32[64]{0:T(128)}, u32[]{:S(2)}) copy-start(f32[64]{0:T(128)} %param.14) | copy-start | bytes 772
  15.3 48.9 %collective-permute-start.3 = (bf16[1,256,128]{2,1,0:T(8,128)(2,1)S(1)}, bf16[1,256,128]{2,1,0:T(8,128)(2,1)S(1)}, u32[]{:S(2)}, u32[]{:S(2)}) collective-permute-start(bf16[1,256,128]{2,1,0:T(8,128)(2,1)S(1)} %maximum_bitcast_fusion), channel_id=1, source_target_pairs={{0,1},{1,2},{2,3},{3,4},{4,5},{5,6},{6,7},{7,0},{8,9},{9,10},{10,1... | collective-permute-start | bytes 196616 | tf_op jit(solution)/shard_map/ppermute | solution.py:28
  16.9 47.4 %collective-permute-start = (bf16[1,256,128]{2,1,0:T(8,128)(2,1)S(1)}, bf16[1,256,128]{2,1,0:T(8,128)(2,1)S(1)}, u32[]{:S(2)}, u32[]{:S(2)}) collective-permute-start(bf16[1,256,128]{2,1,0:T(8,128)(2,1)S(1)} %maximum_bitcast_fusion), channel_id=1, source_target_pairs={{0,7},{1,0},{2,1},{3,2},{4,3},{5,4},{6,5},{7,6},{8,15},{9,8},{10,9... | collective-permute-start | bytes 196616 | tf_op jit(solution)/shard_map/ppermute | solution.py:28
  17.4 58.3 %collective-permute-start.2 = (bf16[1,256,128]{2,1,0:T(8,128)(2,1)S(1)}, bf16[1,256,128]{2,1,0:T(8,128)(2,1)S(1)}, u32[]{:S(2)}, u32[]{:S(2)}) collective-permute-start(bf16[1,256,128]{2,1,0:T(8,128)(2,1)S(1)} %maximum_bitcast_fusion), channel_id=1, source_target_pairs={{0,4},{1,5},{2,6},{3,7},{4,0},{5,1},{6,2},{7,3},{8,12},{9,13},{10,... | collective-permute-start | bytes 196616 | tf_op jit(solution)/shard_map/ppermute | solution.py:28
  64.3 10.7 %collective-permute-start.1 = (bf16[2,256,128]{2,1,0:T(8,128)(2,1)S(1)}, bf16[2,256,128]{2,1,0:T(8,128)(2,1)S(1)}, u32[]{:S(2)}, u32[]{:S(2)}) collective-permute-start(bf16[2,256,128]{2,1,0:T(8,128)(2,1)S(1)} %get-tuple-element.4), channel_id=1, source_target_pairs={{0,6},{1,7},{2,0},{3,1},{4,2},{5,3},{6,4},{7,5},{8,14},{9,15},{10,... | collective-permute-start | bytes 393224 | tf_op jit(solution)/shard_map/ppermute | solution.py:28
  68.8 9.1 %collective-permute-start.4 = (bf16[2,256,128]{2,1,0:T(8,128)(2,1)S(1)}, bf16[2,256,128]{2,1,0:T(8,128)(2,1)S(1)}, u32[]{:S(2)}, u32[]{:S(2)}) collective-permute-start(bf16[2,256,128]{2,1,0:T(8,128)(2,1)S(1)} %get-tuple-element.3), channel_id=1, source_target_pairs={{0,2},{1,3},{2,4},{3,5},{4,6},{5,7},{6,0},{7,1},{8,10},{9,11},{10,... | collective-permute-start | bytes 393224 | tf_op jit(solution)/shard_map/ppermute | solution.py:28
  79.2 14.3 %collective-permute-start.6 = (bf16[8,256,128]{2,1,0:T(8,128)(2,1)}, bf16[8,256,128]{2,1,0:T(8,128)(2,1)S(1)}, u32[]{:S(2)}, u32[]{:S(2)}) collective-permute-start(bf16[8,256,128]{2,1,0:T(8,128)(2,1)} %constant_dynamic-update-slice_fusion.p0), channel_id=1, source_target_pairs={{0,8},{8,16},{16,24},{24,0},{1,9},{9,17},{17,25},{25,1},{2,10},{10... | collective-permute-start | bytes 1572872 | tf_op jit(solution)/shard_map/ppermute | solution.py:28
  80.3 13.5 %collective-permute-start.5 = (bf16[8,256,128]{2,1,0:T(8,128)(2,1)}, bf16[8,256,128]{2,1,0:T(8,128)(2,1)}, u32[]{:S(2)}, u32[]{:S(2)}) collective-permute-start(bf16[8,256,128]{2,1,0:T(8,128)(2,1)} %constant_dynamic-update-slice_fusion.p0), channel_id=1, source_target_pairs={{0,24},{8,0},{16,8},{24,16},{1,25},{9,1},{17,9},{25,17},{2,26},{10... | collective-permute-start | bytes 1572872 | tf_op jit(solution)/shard_map/ppermute | solution.py:28
  93.5 8.5 %copy-start.2 = (bf16[8,256,128]{2,1,0:T(8,128)(2,1)}, bf16[8,256,128]{2,1,0:T(8,128)(2,1)S(1)}, u32[]{:S(2)}) copy-start(bf16[8,256,128]{2,1,0:T(8,128)(2,1)S(1)} %collective-permute-done.6.p2) | copy-start | bytes 1572868
  93.5 7.7 %collective-permute-start.7 = (bf16[4,256,128]{2,1,0:T(8,128)(2,1)S(1)}, bf16[4,256,128]{2,1,0:T(8,128)(2,1)S(1)}, u32[]{:S(2)}, u32[]{:S(2)}) collective-permute-start(bf16[4,256,128]{2,1,0:T(8,128)(2,1)S(1)} %slice.23), channel_id=1, source_target_pairs={{0,8},{8,16},{16,24},{24,0},{1,9},{9,17},{17,25},{25,1},{2,10},{10... | collective-permute-start | bytes 786440 | tf_op jit(solution)/shard_map/ppermute | solution.py:28
  94.7 7.3 %collective-permute-start.8 = (bf16[4,256,128]{2,1,0:T(8,128)(2,1)S(1)}, bf16[4,256,128]{2,1,0:T(8,128)(2,1)}, u32[]{:S(2)}, u32[]{:S(2)}) collective-permute-start(bf16[4,256,128]{2,1,0:T(8,128)(2,1)S(1)} %slice.24), channel_id=1, source_target_pairs={{0,24},{8,0},{16,8},{24,16},{1,25},{9,1},{17,9},{25,17},{2,26},{10... | collective-permute-start | bytes 786440 | tf_op jit(solution)/shard_map/ppermute | solution.py:28
  101.2 0.7 copy-start.7
  102.0 1.4 copy-start.1
  122.0 3.9 %collective-permute-start.9 = (f32[8,128]{1,0:T(8,128)}, f32[8,128]{1,0:T(8,128)S(1)}, u32[]{:S(2)}, u32[]{:S(2)}) collective-permute-start(f32[8,128]{1,0:T(8,128)} %rates.1), channel_id=1, source_target_pairs={{0,64},{64,0},{128,192},{192,128},{1,65},{65,1},{129,193},{193,129... | collective-permute-start | bytes 12296 | tf_op jit(solution)/shard_map/ppermute | solution.py:33
  126.6 5.1 %collective-permute-start.10 = (f32[8,128]{1,0:T(8,128)S(1)}, f32[8,128]{1,0:T(8,128)S(1)}, u32[]{:S(2)}, u32[]{:S(2)}) collective-permute-start(f32[8,128]{1,0:T(8,128)S(1)} %add.18), channel_id=1, source_target_pairs={{0,128},{64,192},{128,0},{192,64},{1,129},{65,193},{129,1},{193,65... | collective-permute-start | bytes 12296 | tf_op jit(solution)/shard_map/ppermute | solution.py:33
  131.7 1.2 collective-permute-start.11
  152.4 32.9 %all-to-all-start.1 = ((bf16[32,128,128]{2,1,0:T(8,128)(2,1)}), bf16[32,128,128]{2,1,0:T(8,128)(2,1)S(1)}, u32[]{:S(2)}, u32[]{:S(2)}) async-start(bf16[32,128,128]{2,1,0:T(8,128)(2,1)} %series.1.sum_ref), calls=%async_computation.1 | async-start | bytes 2097152 | tf_op jit(solution)/shard_map/all_to_all | solution.py:368
  185.3 1.0 copy-start

commit v9 on v8

--- a/solution.py
+++ b/solution.py
@@ -336,13 +336,34 @@
     )(pos, rows, summed, *pieces, rate)
 
 
+def assemble_kernel(own_ref, after_ref, far_after_ref, far_last_ref, last_ref, out_ref):
+    out_ref[0] = own_ref[...]
+    out_ref[1] = after_ref[...]
+    out_ref[2] = far_after_ref[0 : 2 * N]
+    out_ref[3] = far_after_ref[2 * N : 4 * N]
+    out_ref[4, :N] = far_last_ref[0:N]
+    out_ref[4, N:] = far_after_ref[4 * N : 5 * N]
+    out_ref[5] = far_last_ref[N : 3 * N]
+    out_ref[6] = far_last_ref[3 * N : 5 * N]
+    out_ref[7] = last_ref[...]
+
+
+def assemble(*parts):
+    return pl.pallas_call(
+        assemble_kernel,
+        in_specs=[full(p.shape) for p in parts],
+        out_specs=full((NZ, 2 * N, 128)),
+        out_shape=jax.ShapeDtypeStruct((NZ, 2 * N, 128), BF16),
+        name="assemble",
+    )(*parts)
+
+
 def gather_line(input_map, output_map):
-    own = jnp.concatenate([input_map, output_map], axis=0)[None]
+    own = jnp.concatenate([input_map, output_map], axis=0)
     last, after = shifted(own, "seq_1", 1), shifted(own, "seq_1", -1)
-    far_last = shifted(jnp.concatenate([last, own]), "seq_1", 2)
-    far_after = shifted(jnp.concatenate([own, after]), "seq_1", -2)
-    far = shifted(own, "seq_1", 4)
-    return jnp.concatenate([own, after, far_after, far, far_last, last])
+    far_last = shifted(jnp.concatenate([last[:N], own, after]), "seq_1", 3)
+    far_after = shifted(jnp.concatenate([last, own, after[N:]]), "seq_1", -3)
+    return assemble(own, after, far_after, far_last, last)
 
 
 def gather_plane(line):

time: 190 us -> 193 us (1.016)
  waiting for transfers between devices: 95.1 us -> 108 us
  blocking collectives: 19.5 us -> 14.8 us
  starting transfers between devices: 39.1 us -> 34.7 us
  local copies, waits for them, and re-layouts: 8 us -> 5.94 us
    ppermute x9 -> x8, waiting for transfers between devices: 62.2 us -> 75.1 us  [shifted(): return lax.ppermute(x, axis, [(i, (i + by) % size) for i in range(size)])]
    all_to_all x1, blocking collectives: 19.5 us -> 14.8 us  [inner(): lax.all_to_all(copies, SEQ, split_axis=0, concat_axis=0, tiled=True)]
    ppermute x9 -> x8, starting transfers between devices: 18.2 us -> 13.8 us  [shifted(): return lax.ppermute(x, axis, [(i, (i + by) % size) for i in range(size)])]
    unnamed x20 -> x26, local copies, waits for them, and re-layouts: 4.96 us -> 3.46 us
  transfers between devices with their start and end apart: 14 -> 13, of which waited for: 10 -> 11; matrix products, arithmetic and copies ran while one was open for 4% -> 2% of each run, Pallas kernels for 0% -> 1%
where the time goes in v9:
time: 193 us; the launch traced here: 191 us
  waiting for transfers between devices  108 us (56%)
  starting transfers between devices  34.7 us (18%)
  Pallas kernels  25.9 us (13%)
  blocking collectives  14.8 us (8%)
  local copies, waits for them, and re-layouts  5.94 us (3%)
    ppermute x8, waiting for transfers between devices, shifted(): return lax.ppermute(x, axis, [(i, (i + by) % size) for i in range(size)])  75.1 us
    all_to_all x1, waiting for transfers between devices, inner(): lax.all_to_all(summed, SEQ, split_axis=0, concat_axis=0, tiled=True)  27.3 us
    all_to_all x1, blocking collectives, inner(): lax.all_to_all(copies, SEQ, split_axis=0, concat_axis=0, tiled=True)  14.8 us
    ppermute x8, starting transfers between devices, shifted(): return lax.ppermute(x, axis, [(i, (i + by) % size) for i in range(size)])  13.8 us
    all_to_all x1, starting transfers between devices, inner(): rows = lax.all_to_all(packed, SEQ, split_axis=0, concat_axis=0, tiled=True)  11.4 us
    pallas_call x1, Pallas kernels, series(): pl.pallas_call(series_kernel, grid=(1,), in_specs=[SMEM, full((GROUPS, Q...  10 us
    pallas_call x1, Pallas kernels, rates(): pl.pallas_call(rate_kernel, in_specs=[SMEM, full(rows.shape), full(summed...  8.6 us
    ppermute x3, waiting for transfers between devices, swapped(): return lax.ppermute(x, axis, [(i, i ^ bit) for i in range(size)])  5.57 us
  transfers between devices with their start and end apart: 13, of which 11 were waited for; matrix products, arithmetic and copies ran while one was open for 2% of the time, Pallas kernels for 1%

profile of v9, /device:TPU:32, one launch (start us, length us, event | category | flops | bytes accessed | tf_op | source)
XLA Modules:
  0.0 191.4 jit_solution(15911961373949722446)
XLA Ops:
  0.6 3.2 %pack.1 = bf16[32,264,128]{2,1,0:T(8,128)(2,1)} custom-call(f32[64,128]{1,0:T(8,128)} %bitcast.23, f32[1,128]{1,0:T(1,128)} %forget_ref.1, bf16[128,4096]{1,0:T(8,128)(2,1)} %bitcast.15, bf16[128,4096]{1,0:T(8,128)(2,1)} %bitcast.16), custom_call_target="tpu_custom_call" | custom-call | tf_op jit(solution)/shard_map/pack/pallas_call | solution.py:83
  3.9 11.4 %all-to-all-start = ((bf16[32,264,128]{2,1,0:T(8,128)(2,1)}), bf16[32,264,128]{2,1,0:T(8,128)(2,1)S(1)}, u32[]{:S(2)}, u32[]{:S(2)}) async-start(bf16[32,264,128]{2,1,0:T(8,128)(2,1)} %pack.1), calls=%async_computation | async-start | bytes 4325376 | tf_op jit(solution)/shard_map/all_to_all | solution.py:387
  15.3 1.5 collective-permute-start.1
  17.4 44.6 %collective-permute-done.1.last_ref = bf16[256,128]{1,0:T(8,128)(2,1)S(1)} collective-permute-done((bf16[256,128]{1,0:T(8,128)(2,1)S(1)}, bf16[256,128]{1,0:T(8,128)(2,1)S(1)}, u32[]{:S(2)}, u32[]{:S(2)}) %collective-permute-start.1) | collective-permute-done | bytes 65568 | tf_op jit(solution)/shard_map/ppermute | solution.py:28
  62.0 2.0 %collective-permute-done.after_ref = bf16[256,128]{1,0:T(8,128)(2,1)S(1)} collective-permute-done((bf16[256,128]{1,0:T(8,128)(2,1)S(1)}, bf16[256,128]{1,0:T(8,128)(2,1)S(1)}, u32[]{:S(2)}, u32[]{:S(2)}) %collective-permute-start) | collective-permute-done | bytes 65568 | tf_op jit(solution)/shard_map/ppermute | solution.py:28
  64.1 4.3 %collective-permute-start.3 = (bf16[640,128]{1,0:T(8,128)(2,1)S(1)}, bf16[640,128]{1,0:T(8,128)(2,1)S(1)}, u32[]{:S(2)}, u32[]{:S(2)}) collective-permute-start(bf16[640,128]{1,0:T(8,128)(2,1)S(1)} %get-tuple-element.3), channel_id=1, source_target_pairs={{0,3},{1,4},{2,5},{3,6},{4,7},{5,0},{6,1},{7,2},{8,11},{9,12},{10,... | collective-permute-start | bytes 491528 | tf_op jit(solution)/shard_map/ppermute | solution.py:28
  69.2 9.0 %collective-permute-done.3.far_last_ref = bf16[640,128]{1,0:T(8,128)(2,1)S(1)} collective-permute-done((bf16[640,128]{1,0:T(8,128)(2,1)S(1)}, bf16[640,128]{1,0:T(8,128)(2,1)S(1)}, u32[]{:S(2)}, u32[]{:S(2)}) %collective-permute-start.3) | collective-permute-done | bytes 163872 | tf_op jit(solution)/shard_map/ppermute | solution.py:28
  78.2 5.1 %collective-permute-done.2.far_after_ref = bf16[640,128]{1,0:T(8,128)(2,1)S(1)} collective-permute-done((bf16[640,128]{1,0:T(8,128)(2,1)S(1)}, bf16[640,128]{1,0:T(8,128)(2,1)S(1)}, u32[]{:S(2)}, u32[]{:S(2)}) %collective-permute-start.2) | collective-permute-done | bytes 163872 | tf_op jit(solution)/shard_map/ppermute | solution.py:28
  84.0 1.9 assemble.1.p0
  87.2 1.9 %collective-permute-start.4 = (bf16[8,256,128]{2,1,0:T(8,128)(2,1)}, bf16[8,256,128]{2,1,0:T(8,128)(2,1)}, u32[]{:S(2)}, u32[]{:S(2)}) collective-permute-start(bf16[8,256,128]{2,1,0:T(8,128)(2,1)} %assemble.1.p0), channel_id=1, source_target_pairs={{0,24},{8,0},{16,8},{24,16},{1,25},{9,1},{17,9},{25,17},{2,26},{10... | collective-permute-start | bytes 1572872 | tf_op jit(solution)/shard_map/ppermute | solution.py:28
  89.1 11.6 %collective-permute-done.5.p2 = bf16[8,256,128]{2,1,0:T(8,128)(2,1)S(1)} collective-permute-done((bf16[8,256,128]{2,1,0:T(8,128)(2,1)}, bf16[8,256,128]{2,1,0:T(8,128)(2,1)S(1)}, u32[]{:S(2)}, u32[]{:S(2)}) %collective-permute-start.5) | collective-permute-done | bytes 524320 | tf_op jit(solution)/shard_map/ppermute | solution.py:28
  101.9 3.2 %collective-permute-start.7 = (bf16[4,256,128]{2,1,0:T(8,128)(2,1)S(1)}, bf16[4,256,128]{2,1,0:T(8,128)(2,1)}, u32[]{:S(2)}, u32[]{:S(2)}) collective-permute-start(bf16[4,256,128]{2,1,0:T(8,128)(2,1)S(1)} %slice.34), channel_id=1, source_target_pairs={{0,24},{8,0},{16,8},{24,16},{1,25},{9,1},{17,9},{25,17},{2,26},{10... | collective-permute-start | bytes 786440 | tf_op jit(solution)/shard_map/ppermute | solution.py:28
  106.5 2.4 %collective-permute-done.6.p3 = bf16[4,256,128]{2,1,0:T(8,128)(2,1)S(1)} collective-permute-done((bf16[4,256,128]{2,1,0:T(8,128)(2,1)S(1)}, bf16[4,256,128]{2,1,0:T(8,128)(2,1)S(1)}, u32[]{:S(2)}, u32[]{:S(2)}) %collective-permute-start.6) | collective-permute-done | bytes 262176 | tf_op jit(solution)/shard_map/ppermute | solution.py:28
  109.7 1.4 copy-done.1
  111.0 10.0 %series.1.sum_ref = bf16[32,128,128]{2,1,0:T(8,128)(2,1)} custom-call(s32[2]{0:T(128)} %pad_add_fusion.pos_ref, bf16[32,264,128]{2,1,0:T(8,128)(2,1)} %copy-done.1, bf16[8,256,128]{2,1,0:T(8,128)(2,1)} %assemble.1.p0, bf16[8,256,128]{2,1,0:T(8,128)(2,1)} %collective-permute-done.4.p1, bf16[8,256,128]{2,1,0:T(8,128)(2,1)} %copy-done.7, ...), custom_call_target="tpu_custom_call" | custom-call | flops 3000000000 | bytes 5000000 | tf_op jit(solution)/shard_map/series/pallas_call | solution.py:304
  121.1 8.6 %rates.1 = f32[8,128]{1,0:T(8,128)} custom-call(s32[2]{0:T(128)} %pad_add_fusion.pos_ref, bf16[32,264,128]{2,1,0:T(8,128)(2,1)} %copy-done.1, bf16[32,128,128]{2,1,0:T(8,128)(2,1)} %series.1.sum_ref, bf16[8,256,128]{2,1,0:T(8,128)(2,1)} %assemble.1.p0, bf16[8,256,128]{2,1,0:T(8,128)(2,1)} %collective-permute-done.4.p1, bf16[8,256,128]{2,1,0:T(8,128)(2,1)} %copy-done.7, ...), custom_call_target="tpu_custom_call" | custom-call | flops 2000000000 | bytes 5000000 | tf_op jit(solution)/shard_map/rates/pallas_call | solution.py:323
  129.7 1.6 collective-permute-start.8
  131.3 2.3 %collective-permute-done.8 = f32[8,128]{1,0:T(8,128)S(1)} collective-permute-done((f32[8,128]{1,0:T(8,128)}, f32[8,128]{1,0:T(8,128)S(1)}, u32[]{:S(2)}, u32[]{:S(2)}) %collective-permute-start.8) | collective-permute-done | bytes 4128 | tf_op jit(solution)/shard_map/ppermute | solution.py:33
  134.3 3.0 %collective-permute-start.9 = (f32[8,128]{1,0:T(8,128)S(1)}, f32[8,128]{1,0:T(8,128)S(1)}, u32[]{:S(2)}, u32[]{:S(2)}) collective-permute-start(f32[8,128]{1,0:T(8,128)S(1)} %add.18), channel_id=1, source_target_pairs={{0,128},{64,192},{128,0},{192,64},{1,129},{65,193},{129,1},{193,65... | collective-permute-start | bytes 12296 | tf_op jit(solution)/shard_map/ppermute | solution.py:33
  137.3 2.1 %collective-permute-done.9 = f32[8,128]{1,0:T(8,128)S(1)} collective-permute-done((f32[8,128]{1,0:T(8,128)S(1)}, f32[8,128]{1,0:T(8,128)S(1)}, u32[]{:S(2)}, u32[]{:S(2)}) %collective-permute-start.9) | collective-permute-done | bytes 4128 | tf_op jit(solution)/shard_map/ppermute | solution.py:33
  140.6 14.8 %all_to_all.15 = f32[32,1,128]{2,1,0:T(1,128)S(1)} all-to-all(f32[32,1,128]{2,1,0:T(1,128)S(1)} %broadcast_in_dim.11), channel_id=1, replica_groups=mesh['batch_0'=4,'batch_1'=2,'seq_0'=4,'seq_1'=8] {'seq_0','seq_1'}, dimensions={0} | all-to-all | bytes 32768 | tf_op jit(solution)/shard_map/all_to_all | solution.py:397
  155.3 5.0 %all-to-all-start.1 = ((bf16[32,128,128]{2,1,0:T(8,128)(2,1)}), bf16[32,128,128]{2,1,0:T(8,128)(2,1)S(1)}, u32[]{:S(2)}, u32[]{:S(2)}) async-start(bf16[32,128,128]{2,1,0:T(8,128)(2,1)} %series.1.sum_ref), calls=%async_computation.1 | async-start | bytes 2097152 | tf_op jit(solution)/shard_map/all_to_all | solution.py:389
  160.9 27.3 %all-to-all-done.1.in_ref = bf16[32,128,128]{2,1,0:T(8,128)(2,1)S(1)} async-done(((bf16[32,128,128]{2,1,0:T(8,128)(2,1)}), bf16[32,128,128]{2,1,0:T(8,128)(2,1)S(1)}, u32[]{:S(2)}, u32[]{:S(2)}) %all-to-all-start.1) | async-done | bytes 1048608 | tf_op jit(solution)/shard_map/all_to_all | solution.py:389
  189.2 2.2 %join.1 = bf16[128,4096]{1,0:T(8,128)(2,1)} custom-call(bf16[32,128,128]{2,1,0:T(8,128)(2,1)} %copy-done), custom_call_target="tpu_custom_call" | custom-call | tf_op jit(solution)/shard_map/join/pallas_call | solution.py:108
  (53 shorter events, 10.1 us)
Async XLA Ops:
  3.9 11.4 %copy-start.8 = (bf16[1,128,128]{2,1,0:T(8,128)(2,1)S(1)}, bf16[1,128,128]{2,1,0:T(8,128)(2,1)}, u32[]{:S(2)}) copy-start(bf16[1,128,128]{2,1,0:T(8,128)(2,1)} %param.11) | copy-start | bytes 98308
  3.9 11.4 %copy-start.9 = (bf16[1,128,128]{2,1,0:T(8,128)(2,1)S(1)}, bf16[1,128,128]{2,1,0:T(8,128)(2,1)}, u32[]{:S(2)}) copy-start(bf16[1,128,128]{2,1,0:T(8,128)(2,1)} %param.10) | copy-start | bytes 98308
  3.9 105.4 %all-to-all-start = ((bf16[32,264,128]{2,1,0:T(8,128)(2,1)}), bf16[32,264,128]{2,1,0:T(8,128)(2,1)S(1)}, u32[]{:S(2)}, u32[]{:S(2)}) async-start(bf16[32,264,128]{2,1,0:T(8,128)(2,1)} %pack.1), calls=%async_computation | async-start | bytes 4325376 | tf_op jit(solution)/shard_map/all_to_all | solution.py:387
  15.3 89.9 %copy-start.10 = (f32[64]{0:T(128)S(1)}, f32[64]{0:T(128)}, u32[]{:S(2)}) copy-start(f32[64]{0:T(128)} %param.15) | copy-start | bytes 772
  15.3 89.8 %copy-start.11 = (f32[64]{0:T(128)S(1)}, f32[64]{0:T(128)}, u32[]{:S(2)}) copy-start(f32[64]{0:T(128)} %param.14) | copy-start | bytes 772
  15.3 68.0 %copy-start.4 = (bf16[256,128]{1,0:T(8,128)(2,1)}, bf16[256,128]{1,0:T(8,128)(2,1)S(1)}, u32[]{:S(2)}) copy-start(bf16[256,128]{1,0:T(8,128)(2,1)S(1)} %pad_maximum_fusion.2.own_ref) | copy-start | bytes 196612
  15.3 46.7 %collective-permute-start.1 = (bf16[256,128]{1,0:T(8,128)(2,1)S(1)}, bf16[256,128]{1,0:T(8,128)(2,1)S(1)}, u32[]{:S(2)}, u32[]{:S(2)}) collective-permute-start(bf16[256,128]{1,0:T(8,128)(2,1)S(1)} %pad_maximum_fusion.2.own_ref), channel_id=1, source_target_pairs={{0,1},{1,2},{2,3},{3,4},{4,5},{5,6},{6,7},{7,0},{8,9},{9,10},{10,1... | collective-permute-start | bytes 196616 | tf_op jit(solution)/shard_map/ppermute | solution.py:28
  16.9 47.2 %collective-permute-start = (bf16[256,128]{1,0:T(8,128)(2,1)S(1)}, bf16[256,128]{1,0:T(8,128)(2,1)S(1)}, u32[]{:S(2)}, u32[]{:S(2)}) collective-permute-start(bf16[256,128]{1,0:T(8,128)(2,1)S(1)} %pad_maximum_fusion.2.own_ref), channel_id=1, source_target_pairs={{0,7},{1,0},{2,1},{3,2},{4,3},{5,4},{6,5},{7,6},{8,15},{9,8},{10,9... | collective-permute-start | bytes 196616 | tf_op jit(solution)/shard_map/ppermute | solution.py:28
  62.0 21.3 %copy-start.2 = (bf16[256,128]{1,0:T(8,128)(2,1)}, bf16[256,128]{1,0:T(8,128)(2,1)S(1)}, u32[]{:S(2)}) copy-start(bf16[256,128]{1,0:T(8,128)(2,1)S(1)} %collective-permute-done.1.last_ref) | copy-start | bytes 196612
  64.1 19.3 %copy-start.3 = (bf16[256,128]{1,0:T(8,128)(2,1)}, bf16[256,128]{1,0:T(8,128)(2,1)S(1)}, u32[]{:S(2)}) copy-start(bf16[256,128]{1,0:T(8,128)(2,1)S(1)} %collective-permute-done.after_ref) | copy-start | bytes 196612
  64.1 14.1 %collective-permute-start.3 = (bf16[640,128]{1,0:T(8,128)(2,1)S(1)}, bf16[640,128]{1,0:T(8,128)(2,1)S(1)}, u32[]{:S(2)}, u32[]{:S(2)}) collective-permute-start(bf16[640,128]{1,0:T(8,128)(2,1)S(1)} %get-tuple-element.3), channel_id=1, source_target_pairs={{0,3},{1,4},{2,5},{3,6},{4,7},{5,0},{6,1},{7,2},{8,11},{9,12},{10,... | collective-permute-start | bytes 491528 | tf_op jit(solution)/shard_map/ppermute | solution.py:28
  68.4 14.9 %collective-permute-start.2 = (bf16[640,128]{1,0:T(8,128)(2,1)S(1)}, bf16[640,128]{1,0:T(8,128)(2,1)S(1)}, u32[]{:S(2)}, u32[]{:S(2)}) collective-permute-start(bf16[640,128]{1,0:T(8,128)(2,1)S(1)} %get-tuple-element.4), channel_id=1, source_target_pairs={{0,5},{1,6},{2,7},{3,0},{4,1},{5,2},{6,3},{7,4},{8,13},{9,14},{10,... | collective-permute-start | bytes 491528 | tf_op jit(solution)/shard_map/ppermute | solution.py:28
  78.2 5.1 %copy-start.5 = (bf16[640,128]{1,0:T(8,128)(2,1)}, bf16[640,128]{1,0:T(8,128)(2,1)S(1)}, u32[]{:S(2)}) copy-start(bf16[640,128]{1,0:T(8,128)(2,1)S(1)} %collective-permute-done.3.far_last_ref) | copy-start | bytes 491524
  85.9 14.8 %collective-permute-start.5 = (bf16[8,256,128]{2,1,0:T(8,128)(2,1)}, bf16[8,256,128]{2,1,0:T(8,128)(2,1)S(1)}, u32[]{:S(2)}, u32[]{:S(2)}) collective-permute-start(bf16[8,256,128]{2,1,0:T(8,128)(2,1)} %assemble.1.p0), channel_id=1, source_target_pairs={{0,8},{8,16},{16,24},{24,0},{1,9},{9,17},{17,25},{25,1},{2,10},{10... | collective-permute-start | bytes 1572872 | tf_op jit(solution)/shard_map/ppermute | solution.py:28
  87.2 13.6 %collective-permute-start.4 = (bf16[8,256,128]{2,1,0:T(8,128)(2,1)}, bf16[8,256,128]{2,1,0:T(8,128)(2,1)}, u32[]{:S(2)}, u32[]{:S(2)}) collective-permute-start(bf16[8,256,128]{2,1,0:T(8,128)(2,1)} %assemble.1.p0), channel_id=1, source_target_pairs={{0,24},{8,0},{16,8},{24,16},{1,25},{9,1},{17,9},{25,17},{2,26},{10... | collective-permute-start | bytes 1572872 | tf_op jit(solution)/shard_map/ppermute | solution.py:28
  100.7 8.6 %copy-start.7 = (bf16[8,256,128]{2,1,0:T(8,128)(2,1)}, bf16[8,256,128]{2,1,0:T(8,128)(2,1)S(1)}, u32[]{:S(2)}) copy-start(bf16[8,256,128]{2,1,0:T(8,128)(2,1)S(1)} %collective-permute-done.5.p2) | copy-start | bytes 1572868
  100.8 8.2 %collective-permute-start.6 = (bf16[4,256,128]{2,1,0:T(8,128)(2,1)S(1)}, bf16[4,256,128]{2,1,0:T(8,128)(2,1)S(1)}, u32[]{:S(2)}, u32[]{:S(2)}) collective-permute-start(bf16[4,256,128]{2,1,0:T(8,128)(2,1)S(1)} %slice.33), channel_id=1, source_target_pairs={{0,8},{8,16},{16,24},{24,0},{1,9},{9,17},{17,25},{25,1},{2,10},{10... | collective-permute-start | bytes 786440 | tf_op jit(solution)/shard_map/ppermute | solution.py:28
  101.9 7.4 %collective-permute-start.7 = (bf16[4,256,128]{2,1,0:T(8,128)(2,1)S(1)}, bf16[4,256,128]{2,1,0:T(8,128)(2,1)}, u32[]{:S(2)}, u32[]{:S(2)}) collective-permute-start(bf16[4,256,128]{2,1,0:T(8,128)(2,1)S(1)} %slice.34), channel_id=1, source_target_pairs={{0,24},{8,0},{16,8},{24,16},{1,25},{9,1},{17,9},{25,17},{2,26},{10... | collective-permute-start | bytes 786440 | tf_op jit(solution)/shard_map/ppermute | solution.py:28
  109.7 1.4 copy-start.1
  129.7 3.9 %collective-permute-start.8 = (f32[8,128]{1,0:T(8,128)}, f32[8,128]{1,0:T(8,128)S(1)}, u32[]{:S(2)}, u32[]{:S(2)}) collective-permute-start(f32[8,128]{1,0:T(8,128)} %rates.1), channel_id=1, source_target_pairs={{0,64},{64,0},{128,192},{192,128},{1,65},{65,1},{129,193},{193,129... | collective-permute-start | bytes 12296 | tf_op jit(solution)/shard_map/ppermute | solution.py:33
  134.3 5.1 %collective-permute-start.9 = (f32[8,128]{1,0:T(8,128)S(1)}, f32[8,128]{1,0:T(8,128)S(1)}, u32[]{:S(2)}, u32[]{:S(2)}) collective-permute-start(f32[8,128]{1,0:T(8,128)S(1)} %add.18), channel_id=1, source_target_pairs={{0,128},{64,192},{128,0},{192,64},{1,129},{65,193},{129,1},{193,65... | collective-permute-start | bytes 12296 | tf_op jit(solution)/shard_map/ppermute | solution.py:33
  139.4 1.2 collective-permute-start.10
  155.3 32.9 %all-to-all-start.1 = ((bf16[32,128,128]{2,1,0:T(8,128)(2,1)}), bf16[32,128,128]{2,1,0:T(8,128)(2,1)S(1)}, u32[]{:S(2)}, u32[]{:S(2)}) async-start(bf16[32,128,128]{2,1,0:T(8,128)(2,1)} %series.1.sum_ref), calls=%async_computation.1 | async-start | bytes 2097152 | tf_op jit(solution)/shard_map/all_to_all | solution.py:389
  188.2 1.0 copy-start
  (2 other events, 1.4 us)
